TPU v7x, 64 devices: a 2x2x8 block of a 4x4x8 slice. The times are simulated.
64 devices in a mesh: rep: 4 (over x, y), kv: 16 (over z, core).
Axes of the slice: x: 2, y: 2, z: 8, core: 2. Of those that a mesh axis runs over, the one named last changes fastest.
The devices are a block of a 4x4x8 slice.
Arguments:
- embeds: bfloat16 [2, 2048, 2048], P(None, ('rep', 'kv')), parts along dimension 1
- w_query: bfloat16 [2, 2048, 2048], replicated
- w_key: bfloat16 [2, 2048, 256], replicated
- w_value: bfloat16 [2, 2048, 256], replicated
- w_out: bfloat16 [2, 2048, 2048], replicated
- w_up: bfloat16 [2, 2048, 5632], replicated
- w_down: bfloat16 [2, 5632, 2048], replicated
- k_pool: bfloat16 [5120, 2, 64, 4, 64], P(('rep', 'kv')), parts along dimension 0
- v_pool: bfloat16 [5120, 2, 64, 4, 64], P(('rep', 'kv')), parts along dimension 0
- new_table: int32 [2048, 2], P('rep'), parts along dimension 0
- seq_lens: int32 [2048], P('rep'), parts along dimension 0
- mig_src: int32 [64], P('rep'), parts along dimension 0
- mig_dst: int32 [64], P('rep'), parts along dimension 0
Outputs:
- output 1: bfloat16 [2, 2048, 2048], P(None, ('rep', 'kv')), parts along dimension 1
- output 2: bfloat16 [5120, 2, 64, 4, 64], P(('rep', 'kv')), parts along dimension 0
- output 3: bfloat16 [5120, 2, 64, 4, 64], P(('rep', 'kv')), parts along dimension 0
There are 4 independent parts. A program takes and returns all parts, laid end to end along the dimension named above; an argument that names none is the same for every part.
All inputs are finite; a program needn't handle non-finite values.
Results may differ from a plain program's by a relative error of at most 0.0153616.
Values are sent between devices in bfloat16 or wider.
A program may use at most 768 MiB of HBM per device.

v0:
```python
import jax
import jax.numpy as jnp
from jax import lax
from jax.sharding import PartitionSpec as P


def local_index(slot_ids, dev_idx, slots):
    local_ids = slot_ids - dev_idx * slots
    return jnp.where((local_ids >= 0) & (local_ids < slots), local_ids, slots)


def slot_owners(page_table, dev_idx, slots):
    seq_count, page_count = page_table.shape
    seg_ids = local_index(page_table, dev_idx, slots).reshape(-1)
    seq_plus = jnp.broadcast_to(jnp.arange(1, seq_count + 1)[:, None], page_table.shape).reshape(-1)
    page_plus = jnp.broadcast_to(jnp.arange(1, page_count + 1)[None, :], page_table.shape).reshape(-1)
    owner_seq = jax.ops.segment_sum(seq_plus, seg_ids, num_segments=slots + 1)[:slots] - 1
    owner_page = jax.ops.segment_sum(page_plus, seg_ids, num_segments=slots + 1)[:slots] - 1
    return owner_seq, owner_page


def local_partials(queries_all, k_layer, v_layer, owner_seq, owner_page, seq_lens, step_idx):
    seq_count = queries_all.shape[0]
    page_len = k_layer.shape[1]
    head_dim = k_layer.shape[3]
    is_owned = owner_seq >= 0
    safe_seq = jnp.maximum(owner_seq, 0)
    q_slots = jnp.take(queries_all, safe_seq, axis=0)
    scores = jnp.einsum('skgd,sikd->skgi', q_slots, k_layer, preferred_element_type=jnp.float32) * head_dim ** -0.5
    positions = owner_page[:, None] * page_len + jnp.arange(page_len)[None, :]
    limits = jnp.take(seq_lens, safe_seq) + step_idx
    valid_mask = (is_owned[:, None] & (positions <= limits[:, None]))[:, None, None, :]
    scores = jnp.where(valid_mask, scores, -1e30)
    slot_max = jnp.max(scores, axis=-1)
    prob_vals = jnp.where(valid_mask, jnp.exp(scores - slot_max[..., None]), 0.0)
    slot_sum = jnp.sum(prob_vals, axis=-1)
    slot_out = jnp.einsum('skgi,sikd->skgd', prob_vals.astype(jnp.bfloat16), v_layer, preferred_element_type=jnp.float32)
    seg_ids = jnp.where(is_owned, owner_seq, seq_count)
    seq_max = jax.ops.segment_max(slot_max, seg_ids, num_segments=seq_count + 1)[:seq_count]
    seq_max = jnp.maximum(seq_max, -1e30)
    rescale = jnp.exp(slot_max - jnp.take(seq_max, safe_seq, axis=0))
    seq_sum = jax.ops.segment_sum(slot_sum * rescale, seg_ids, num_segments=seq_count + 1)[:seq_count]
    seq_out = jax.ops.segment_sum(slot_out * rescale[..., None], seg_ids, num_segments=seq_count + 1)[:seq_count]
    return jnp.concatenate([seq_out, seq_max[..., None], seq_sum[..., None]], axis=-1)


def merge_partials(packed, group_size):
    head_dim = packed.shape[-1] - 2
    received = lax.all_to_all(packed, 'kv', 0, 0, tiled=True)
    received = received.reshape((group_size, -1) + packed.shape[1:])
    part_out = received[..., :head_dim]
    part_max = received[..., head_dim]
    part_sum = received[..., head_dim + 1]
    glob_max = jnp.max(part_max, axis=0)
    scale_w = jnp.exp(part_max - glob_max)
    total_sum = jnp.sum(scale_w * part_sum, axis=0)
    merged = jnp.sum(scale_w[..., None] * part_out, axis=0) / total_sum[..., None]
    return merged.reshape(merged.shape[0], -1).astype(jnp.bfloat16)


def decode_layer(hidden, layer_idx, step_idx, pools, owners, page_table, seq_lens, weights, dev_idx, group_size):
    w_query, w_key, w_value, w_out, w_up, w_down = weights
    k_pool, v_pool = pools
    owner_seq, owner_page = owners
    slots = k_pool.shape[0]
    page_len = k_pool.shape[2]
    kv_heads = k_pool.shape[3]
    head_dim = k_pool.shape[4]
    num_heads = w_query.shape[2] // head_dim
    queries = jnp.dot(hidden, w_query[layer_idx], preferred_element_type=jnp.float32).astype(jnp.bfloat16)
    new_keys = jnp.dot(hidden, w_key[layer_idx], preferred_element_type=jnp.float32).astype(jnp.bfloat16)
    new_vals = jnp.dot(hidden, w_value[layer_idx], preferred_element_type=jnp.float32).astype(jnp.bfloat16)
    queries_all = lax.all_gather(queries, 'kv', axis=0, tiled=True)
    kv_all = lax.all_gather(jnp.stack([new_keys, new_vals]), 'kv', axis=1, tiled=True)
    seq_count = queries_all.shape[0]
    positions = seq_lens + step_idx
    slot_ids = jnp.take_along_axis(page_table, (positions // page_len)[:, None], axis=1)[:, 0]
    local_ids = local_index(slot_ids, dev_idx, slots)
    offsets = positions % page_len
    kv_rows = kv_all.reshape(2, seq_count, kv_heads, head_dim)
    k_pool = k_pool.at[local_ids, layer_idx, offsets].set(kv_rows[0], mode='drop')
    v_pool = v_pool.at[local_ids, layer_idx, offsets].set(kv_rows[1], mode='drop')
    packed = local_partials(queries_all.reshape(seq_count, kv_heads, num_heads // kv_heads, head_dim), k_pool[:, layer_idx], v_pool[:, layer_idx], owner_seq, owner_page, seq_lens, step_idx)
    attn_out = merge_partials(packed, group_size)
    hidden = (hidden.astype(jnp.float32) + jnp.dot(attn_out, w_out[layer_idx], preferred_element_type=jnp.float32)).astype(jnp.bfloat16)
    up_proj = jnp.dot(hidden, w_up[layer_idx], preferred_element_type=jnp.float32).astype(jnp.bfloat16)
    act_vals = jax.nn.gelu(up_proj.astype(jnp.float32), approximate=True).astype(jnp.bfloat16)
    hidden = (hidden.astype(jnp.float32) + jnp.dot(act_vals, w_down[layer_idx], preferred_element_type=jnp.float32)).astype(jnp.bfloat16)
    return hidden, (k_pool, v_pool)


def decode_step(hidden, step_idx, pools, page_table, seq_lens, weights, dev_idx, group_size):
    owners = slot_owners(page_table, dev_idx, pools[0].shape[0])
    for layer_idx in range(pools[0].shape[1]):
        hidden, pools = decode_layer(hidden, layer_idx, step_idx, pools, owners, page_table, seq_lens, weights, dev_idx, group_size)
    return hidden, pools


def migrate(pools, mig_src, mig_dst, dev_idx):
    k_pool, v_pool = pools
    slots = k_pool.shape[0]
    src_local = local_index(mig_src, dev_idx, slots)
    dst_local = local_index(mig_dst, dev_idx, slots)
    k_pages = jnp.take(k_pool, src_local, axis=0, mode='fill', fill_value=0)
    v_pages = jnp.take(v_pool, src_local, axis=0, mode='fill', fill_value=0)
    k_pages, v_pages = lax.psum((k_pages, v_pages), 'kv')
    k_pool = k_pool.at[dst_local].set(k_pages, mode='drop').at[src_local].set(0, mode='drop')
    v_pool = v_pool.at[dst_local].set(v_pages, mode='drop').at[src_local].set(0, mode='drop')
    return k_pool, v_pool


def solution(mesh):
    group_size = mesh.shape['kv']
    pool_spec = P(('rep', 'kv'))
    tok_spec = P(None, ('rep', 'kv'), None)

    def device_fn(embeds, w_query, w_key, w_value, w_out, w_up, w_down, k_pool, v_pool, new_table, seq_lens, mig_src, mig_dst):
        dev_idx = lax.axis_index('kv')
        slots = k_pool.shape[0]
        weights = (w_query, w_key, w_value, w_out, w_up, w_down)
        slot_remap = jnp.arange(slots * group_size, dtype=jnp.int32).at[mig_dst].set(mig_src)
        old_table = jnp.take(slot_remap, new_table, axis=0)
        pools = (k_pool, v_pool)
        first_out, pools = decode_step(embeds[0], 0, pools, old_table, seq_lens, weights, dev_idx, group_size)
        pools = migrate(pools, mig_src, mig_dst, dev_idx)
        second_out, pools = decode_step(embeds[1], 1, pools, new_table, seq_lens, weights, dev_idx, group_size)
        return jnp.stack([first_out, second_out]), pools[0], pools[1]

    return jax.shard_map(device_fn, mesh=mesh, in_specs=(tok_spec, P(), P(), P(), P(), P(), P(), pool_spec, pool_spec, P('rep', None), P('rep'), P('rep'), P('rep')), out_specs=(tok_spec, pool_spec, pool_spec), check_vma=False)
```

profile of v0, /device:TPU:21, one launch (start us, length us, event | category | flops | bytes accessed | tf_op | source)
XLA Modules:
  0.0 2032.3 jit_solution(2025051164059223663)
XLA Ops:
  22.0 7.6 scatter_custom_fusion.1
  45.4 24.2 %all_gather.25 = bf16[2,512,256]{2,1,0:T(8,128)(2,1)S(1)} all-gather(bf16[2,32,256]{2,1,0:T(8,128)(2,1)S(1)} %pad_maximum_fusion.5), channel_id=1, replica_groups=mesh['rep'=4,'kv'=16] {'kv'}, dimensions={1}, use_global_device_ids=true | all-gather | bytes 557056 | tf_op jit(solution)/shard_map/all_gather | solution.py:74
  70.0 17.8 copy.326
  93.3 57.7 %scatter_fusion.1 = bf16[80,2,64,4,64]{4,3,2,1,0:T(4,128)(2,1)} fusion(bf16[80,2,64,4,64]{4,3,2,1,0:T(4,128)(2,1)} %copy.326, s32[512]{0:T(512)S(1)} %bitcast.361, bf16[512,4,64]{2,1,0:T(4,128)(2,1)S(1)} %copy.327), kind=kCustom, calls=%fused_computation.18 | custom fusion | bytes 792576 | tf_op jit(solution)/shard_map/scatter | solution.py:81
  151.1 9.0 slice.313
  160.6 17.4 copy.330
  178.0 56.9 %scatter_fusion.2 = bf16[80,2,64,4,64]{4,3,2,1,0:T(4,128)(2,1)} fusion(bf16[80,2,64,4,64]{4,3,2,1,0:T(4,128)(2,1)} %copy.330, s32[512]{0:T(512)S(1)} %bitcast.362, bf16[512,4,64]{2,1,0:T(4,128)(2,1)S(1)} %copy.331), kind=kCustom, calls=%fused_computation.19 | custom fusion | bytes 792576 | tf_op jit(solution)/shard_map/scatter | solution.py:82
  234.9 9.0 slice.315
  278.2 9.9 scatter_fusion.4
  288.0 7.7 slice.317
  299.3 13.5 copy.334
  312.9 13.5 copy.333
  326.4 13.2 pad_maximum_fusion
  360.3 189.9 %all_gather.29 = bf16[2,512,256]{2,1,0:T(8,128)(2,1)S(1)} all-gather(bf16[2,32,256]{2,1,0:T(8,128)(2,1)S(1)} %pad_maximum_fusion.7), channel_id=1, replica_groups=mesh['rep'=4,'kv'=16] {'kv'}, dimensions={1}, use_global_device_ids=true | all-gather | bytes 557056 | tf_op jit(solution)/shard_map/all_gather | solution.py:74
  550.3 12.0 fusion.339
  586.4 9.9 fusion.203
  596.3 9.8 fusion.117
  606.8 16.1 all_gather.27
  623.9 57.8 %scatter_fusion.6 = bf16[80,2,64,4,64]{4,3,2,1,0:T(4,128)(2,1)} fusion(bf16[80,2,64,4,64]{4,3,2,1,0:T(4,128)(2,1)} %scatter_fusion.1, s32[512]{0:T(512)S(1)} %bitcast.357, bf16[512,4,64]{2,1,0:T(4,128)(2,1)S(1)} %copy.342), kind=kCustom, calls=%fused_computation.23 | custom fusion | bytes 792576 | tf_op jit(solution)/shard_map/scatter | solution.py:81
  681.7 57.1 %scatter_fusion.7 = bf16[80,2,64,4,64]{4,3,2,1,0:T(4,128)(2,1)} fusion(bf16[80,2,64,4,64]{4,3,2,1,0:T(4,128)(2,1)} %scatter_fusion.2, s32[512]{0:T(512)S(1)} %bitcast.358, bf16[512,4,64]{2,1,0:T(4,128)(2,1)S(1)} %copy.345), kind=kCustom, calls=%fused_computation.24 | custom fusion | bytes 792576 | tf_op jit(solution)/shard_map/scatter | solution.py:82
  781.6 11.1 copy.362
  792.7 11.2 copy.356
  803.9 69.9 %all-reduce.3.cloned.1.call-done = (bf16[16,2,64,4,64]{4,3,2,1,0:T(4,128)(2,1)}, bf16[16,2,64,4,64]{4,3,2,1,0:T(4,128)(2,1)}) async-done(((bf16[16,2,64,4,64]{4,3,2,1,0:T(4,128)(2,1)}, bf16[16,2,64,4,64]{4,3,2,1,0:T(4,128)(2,1)}), (bf16[16,2,64,4,64]{4,3,2,1,0:T(4,128)(2,1)}, bf16[16,2,64,4,64]{4,3,2,1,0:T(4,128)(2,1)})) %all-reduce.3.cloned.1.call-update) | async-done | bytes 2097168 | tf_op jit(solution)/shard_map/psum | solution.py:106
  885.5 13.3 copy.365
  898.8 53.9 %scatter_fusion.16 = bf16[80,2,64,4,64]{4,3,2,1,0:T(4,128)(2,1)} fusion(bf16[80,2,64,4,64]{4,3,2,1,0:T(4,128)(2,1)} %copy.365, s32[512]{0:T(512)S(1)} %bitcast.359, bf16[512,4,64]{2,1,0:T(4,128)(2,1)S(1)} %copy.366), kind=kCustom, calls=%fused_computation.35 | custom fusion | bytes 792576 | tf_op jit(solution)/shard_map/scatter | solution.py:82
  952.8 9.2 slice.337
  973.5 13.3 copy.359
  986.8 53.7 %scatter_fusion.13 = bf16[80,2,64,4,64]{4,3,2,1,0:T(4,128)(2,1)} fusion(bf16[80,2,64,4,64]{4,3,2,1,0:T(4,128)(2,1)} %copy.359, s32[512]{0:T(512)S(1)} %bitcast.360, bf16[512,4,64]{2,1,0:T(4,128)(2,1)S(1)} %copy.360), kind=kCustom, calls=%fused_computation.32 | custom fusion | bytes 792576 | tf_op jit(solution)/shard_map/scatter | solution.py:81
  1067.2 10.0 scatter_fusion.18
  1077.2 7.6 slice.339
  1088.4 13.5 copy.369
  1101.9 13.5 copy.368
  1115.5 13.2 pad_maximum_fusion.2
  1140.3 9.0 slice.323
  1149.4 9.0 slice.325
  1158.4 44.2 %all-gather.7.cloned.1.call-done = bf16[512,2048]{1,0:T(8,128)(2,1)} async-done(((bf16[32,2048]{1,0:T(8,128)(2,1)}), bf16[512,2048]{1,0:T(8,128)(2,1)}) %all-gather.7.cloned.1.call-update) | async-done | bytes 2097168 | tf_op jit(solution)/shard_map/all_gather | solution.py:73
  1239.2 9.9 scatter_fusion.9
  1249.1 7.6 slice.327
  1260.3 13.5 copy.348
  1273.8 13.5 copy.347
  1287.4 13.6 pad_maximum_fusion.1
  1301.0 26.2 %all-to-all-done.2 = f32[512,4,8,66]{3,2,1,0:T(8,128)} async-done(((f32[512,4,8,66]{3,2,1,0:T(8,128)}), f32[512,4,8,66]{3,2,1,0:T(8,128)}, u32[]{:S(2)}, u32[]{:S(2)}) %all-to-all-start.2) | async-done | bytes 4325408 | tf_op jit(solution)/shard_map/all_to_all | solution.py:49
  1327.2 8.5 all-to-all-start.1
  1335.7 11.7 fusion.338
  1371.6 10.0 fusion.227
  1381.7 9.9 fusion.114
  1395.8 154.2 %all_gather.31 = bf16[2,512,256]{2,1,0:T(8,128)(2,1)S(1)} all-gather(bf16[2,32,256]{2,1,0:T(8,128)(2,1)S(1)} %pad_maximum_fusion.8), channel_id=1, replica_groups=mesh['rep'=4,'kv'=16] {'kv'}, dimensions={1}, use_global_device_ids=true | all-gather | bytes 557056 | tf_op jit(solution)/shard_map/all_gather | solution.py:74
  1550.5 53.7 %scatter_fusion.21 = bf16[80,2,64,4,64]{4,3,2,1,0:T(4,128)(2,1)} fusion(bf16[80,2,64,4,64]{4,3,2,1,0:T(4,128)(2,1)} %scatter_fusion.16, s32[512]{0:T(512)S(1)} %bitcast.355, bf16[512,4,64]{2,1,0:T(4,128)(2,1)S(1)} %copy.380), kind=kCustom, calls=%fused_computation.40 | custom fusion | bytes 792576 | tf_op jit(solution)/shard_map/scatter | solution.py:82
  1604.2 9.0 slice.347
  1613.7 53.7 %scatter_fusion.20 = bf16[80,2,64,4,64]{4,3,2,1,0:T(4,128)(2,1)} fusion(bf16[80,2,64,4,64]{4,3,2,1,0:T(4,128)(2,1)} %scatter_fusion.13, s32[512]{0:T(512)S(1)} %bitcast.356, bf16[512,4,64]{2,1,0:T(4,128)(2,1)S(1)} %copy.377), kind=kCustom, calls=%fused_computation.39 | custom fusion | bytes 792576 | tf_op jit(solution)/shard_map/scatter | solution.py:81
  1667.5 9.0 slice.345
  1712.9 10.0 scatter_fusion.23
  1734.0 13.5 copy.385
  1747.6 13.5 copy.384
  1761.1 13.2 pad_maximum_fusion.3
  1780.7 17.5 copy.391
  1798.3 17.5 copy.390
  1815.8 11.6 fusion.336
  1851.5 9.9 fusion.215
  1861.3 9.8 fusion.144
  1871.1 98.2 %all-to-all-done.3 = f32[512,4,8,66]{3,2,1,0:T(8,128)} async-done(((f32[512,4,8,66]{3,2,1,0:T(8,128)}), f32[512,4,8,66]{3,2,1,0:T(8,128)}, u32[]{:S(2)}, u32[]{:S(2)}) %all-to-all-start.3) | async-done | bytes 4325408 | tf_op jit(solution)/shard_map/all_to_all | solution.py:49
  1969.4 11.8 fusion.337
  2005.2 9.9 fusion.239
  2015.1 9.8 fusion.147
  (305 shorter events, 400.2 us)
Async XLA Ops:
  7.2 5.8 copy-start
  7.2 6.2 copy-start.23
  7.2 6.8 copy-start.20
  7.2 236.9 %all-gather.5.cloned.1.call-start = ((), (), s32[]{:S(2)}) async-start(), calls=%async_computation.4 | async-start | bytes 2228224 | tf_op jit(solution)/shard_map/all_gather | solution.py:73
  14.6 22.7 %copy-start.1 = (s32[512]{0:T(512)S(1)}, s32[512]{0:T(512)}, u32[]{:S(2)}) copy-start(s32[512]{0:T(512)} %param.33) | copy-start | bytes 6148
  14.7 28.9 %copy-start.24 = (bf16[2,2048,256]{2,1,0:T(8,128)(2,1)S(1)}, bf16[2,2048,256]{2,1,0:T(8,128)(2,1)}, u32[]{:S(2)}) copy-start(bf16[2,2048,256]{2,1,0:T(8,128)(2,1)} %param.25) | copy-start | bytes 6291460
  14.7 28.9 %copy-start.29 = (bf16[2,32,2048]{2,1,0:T(8,128)(2,1)S(1)}, bf16[2,32,2048]{2,1,0:T(8,128)(2,1)}, u32[]{:S(2)}) copy-start(bf16[2,32,2048]{2,1,0:T(8,128)(2,1)} %param.23) | copy-start | bytes 786436
  37.3 229.4 %copy-start.18 = (s32[1024]{0:T(1024)}, s32[1024]{0:T(1024)S(1)}, u32[]{:S(2)}) copy-start(s32[1024]{0:T(1024)S(1)} %pad_clamp_fusion.2) | copy-start | bytes 12292
  244.0 23.4 %copy-start.21 = (pred[80]{0:T(512)(128)(4,1)}, pred[80]{0:T(512)(128)(4,1)S(1)}, u32[]{:S(2)}) copy-start(pred[80]{0:T(512)(128)(4,1)S(1)} %get-tuple-element.88) | copy-start | bytes 244
  244.0 51.9 %copy-start.16 = (s32[80]{0:T(128)}, s32[80]{0:T(128)S(1)}, u32[]{:S(2)}) copy-start(s32[80]{0:T(128)S(1)} %get-tuple-element.90) | copy-start | bytes 964
  244.1 24.1 %copy-start.14 = (pred[80,64]{1,0:T(8,128)(4,1)}, pred[80,64]{1,0:T(8,128)(4,1)S(1)}, u32[]{:S(2)}) copy-start(pred[80,64]{1,0:T(8,128)(4,1)S(1)} %fusion.294) | copy-start | bytes 15364
  261.6 1.1 copy-start.4
  273.8 4.3 copy-start.7
  288.0 7.9 copy-start.12
  339.6 5.1 copy-start.30
  339.6 210.7 %all-to-all-start = ((f32[512,4,8,66]{3,2,1,0:T(8,128)}), f32[512,4,8,66]{3,2,1,0:T(8,128)}, u32[]{:S(2)}, u32[]{:S(2)}) async-start(f32[512,4,8,66]{3,2,1,0:T(8,128)} %pad_maximum_fusion), calls=%async_computation | async-start | bytes 16777216 | tf_op jit(solution)/shard_map/all_to_all | solution.py:49
  344.6 13.9 copy-start.25
  344.6 423.8 %all-gather.9.cloned.1.call-start = ((), (), s32[]{:S(2)}) async-start(), calls=%async_computation.6 | async-start | bytes 2228224 | tf_op jit(solution)/shard_map/all_gather | solution.py:73
  350.5 523.3 %all-reduce.3.cloned.1.call-start = ((), (), s32[]{:S(2)}) async-start(), calls=%async_computation.8 | async-start | bytes 8388608 | tf_op jit(solution)/shard_map/psum | solution.py:106
  596.3 9.9 copy-start.26
  596.3 10.2 copy-start.28
  606.2 139.0 %copy-start.32 = (bf16[32,2048]{1,0:T(8,128)(2,1)}, bf16[32,2048]{1,0:T(8,128)(2,1)S(1)}, u32[]{:S(2)}) copy-start(bf16[32,2048]{1,0:T(8,128)(2,1)S(1)} %fusion.117) | copy-start | bytes 393220
  792.7 83.3 %copy-start.19 = (s32[16]{0:T(128)S(1)}, s32[16]{0:T(128)}, u32[]{:S(2)}) copy-start(s32[16]{0:T(128)} %get-tuple-element.85) | copy-start | bytes 196
  952.8 9.2 copy-start.3
  1040.5 4.9 copy-start.9
  1062.9 4.3 copy-start.8
  1077.2 7.8 copy-start.13
  1128.7 6.0 copy-start.33
  1128.7 198.5 %all-to-all-start.2 = ((f32[512,4,8,66]{3,2,1,0:T(8,128)}), f32[512,4,8,66]{3,2,1,0:T(8,128)}, u32[]{:S(2)}, u32[]{:S(2)}) async-start(f32[512,4,8,66]{3,2,1,0:T(8,128)} %pad_maximum_fusion.2), calls=%async_computation.2 | async-start | bytes 16777216 | tf_op jit(solution)/shard_map/all_to_all | solution.py:49
  1134.6 68.0 %all-gather.7.cloned.1.call-start = ((), (), s32[]{:S(2)}) async-start(), calls=%async_computation.5 | async-start | bytes 2228224 | tf_op jit(solution)/shard_map/all_gather | solution.py:73
  1158.4 56.9 %copy-start.15 = (pred[80,64]{1,0:T(8,128)(4,1)S(1)}, pred[80,64]{1,0:T(8,128)(4,1)}, u32[]{:S(2)}) copy-start(pred[80,64]{1,0:T(8,128)(4,1)} %copy-done.14) | copy-start | bytes 15364
  1158.4 56.9 %copy-start.22 = (pred[80]{0:T(512)(128)(4,1)S(1)}, pred[80]{0:T(512)(128)(4,1)}, u32[]{:S(2)}) copy-start(pred[80]{0:T(512)(128)(4,1)} %copy-done.21) | copy-start | bytes 244
  1212.3 9.7 copy-start.17
  1234.9 4.3 copy-start.5
  1249.1 7.8 copy-start.11
  1327.2 447.1 %all-to-all-start.1 = ((f32[512,4,8,66]{3,2,1,0:T(8,128)}), f32[512,4,8,66]{3,2,1,0:T(8,128)}, u32[]{:S(2)}, u32[]{:S(2)}) async-start(f32[512,4,8,66]{3,2,1,0:T(8,128)} %pad_maximum_fusion.1), calls=%async_computation.1 | async-start | bytes 16777216 | tf_op jit(solution)/shard_map/all_to_all | solution.py:49
  1335.7 340.9 %all-gather.11.cloned.1.call-start = ((), (), s32[]{:S(2)}) async-start(), calls=%async_computation.7 | async-start | bytes 2228224 | tf_op jit(solution)/shard_map/all_gather | solution.py:73
  1360.9 5.8 copy-start.31
  1371.6 20.0 slice-start
  1371.6 20.0 slice-start.1
  1381.7 10.0 slice-start.2
  1381.7 10.0 slice-start.3
  1391.7 4.1 copy-start.35
  1391.7 2.3 copy-start.27
  1391.7 158.8 %copy-start.2 = (s32[512,1]{0,1:T(1,128)S(1)}, s32[512,1]{0,1:T(1,128)}, u32[]{:S(2)}) copy-start(s32[512,1]{0,1:T(1,128)} %get-tuple-element.34) | copy-start | bytes 6148
  1708.6 4.3 copy-start.6
  1722.8 7.8 copy-start.10
  1774.3 195.1 %all-to-all-start.3 = ((f32[512,4,8,66]{3,2,1,0:T(8,128)}), f32[512,4,8,66]{3,2,1,0:T(8,128)}, u32[]{:S(2)}, u32[]{:S(2)}) async-start(f32[512,4,8,66]{3,2,1,0:T(8,128)} %pad_maximum_fusion.3), calls=%async_computation.3 | async-start | bytes 16777216 | tf_op jit(solution)/shard_map/all_to_all | solution.py:49
  1840.7 5.8 copy-start.34
  1994.5 5.8 copy-start.36
Sparse Core Ops, SparseCore 0:
  13.1 41.2 all-gather.4
  350.6 59.5 all-gather.8
  758.3 115.4 all-reduce.2
  1140.5 62.1 all-gather.6
  1394.1 90.4 all-gather.10
where the time goes:
time: 2050 us; the launch traced here: 2030 us
  local copies, waits for them, and re-layouts  959 us (47%)
  blocking collectives  384 us (19%)
  other arithmetic  240 us (12%)
  waiting for transfers between devices  239 us (12%)
  matrix products  168 us (8%)
  starting transfers between devices  26.1 us (1%)
    all_gather x4, blocking collectives, decode_layer(): lax.all_gather(jnp.stack([new_keys, new_vals]), 'kv', axis=1, tiled=True)  384 us
    scatter x5, local copies, waits for them, and re-layouts, decode_layer(): k_pool.at[local_ids, layer_idx, offsets].set(kv_rows[0], mode='drop')  234 us
    scatter x5, local copies, waits for them, and re-layouts, decode_layer(): v_pool.at[local_ids, layer_idx, offsets].set(kv_rows[1], mode='drop')  233 us
    all_to_all x4, waiting for transfers between devices, merge_partials(): received = lax.all_to_all(packed, 'kv', 0, 0, tiled=True)  124 us
    unnamed x94, local copies, waits for them, and re-layouts  96.2 us
    psum x1, waiting for transfers between devices, migrate(): k_pages, v_pages = lax.psum((k_pages, v_pages), 'kv')  69.9 us
    broadcast_in_dim x8, local copies, waits for them, and re-layouts, local_partials(): seq_sum[..., None]  54.5 us
    broadcast_in_dim x4, local copies, waits for them, and re-layouts, local_partials(): seq_max[..., None]  54.2 us
  transfers between devices with their start and end apart: 9, of which 4 were waited for; matrix products, arithmetic and copies ran while one was open for 47% of the time, Pallas kernels for 0%

commit v1 on v0

v1 whole, which is shorter than its diff:
```python
import functools

import jax
import jax.numpy as jnp
from jax import lax
from jax.experimental import pallas as pl
from jax.experimental.pallas import tpu as pltpu
from jax.sharding import PartitionSpec as P

MESH = pl.DeviceIdType.MESH
F32 = jnp.float32
BF16 = jnp.bfloat16
NEG = -1e30
HOPS = 4


def dot(a, b):
    return jnp.dot(a, b, preferred_element_type=F32)


def split3(x):
    hi = x.astype(BF16)
    rest = x - hi.astype(F32)
    mid = rest.astype(BF16)
    low = (rest - mid.astype(F32)).astype(BF16)
    return jnp.concatenate([hi, mid, low], axis=0)


def exact_dot(x, onehot):
    rows = x.shape[0]
    out = dot(split3(x), onehot)
    return out[:rows] + out[rows : 2 * rows] + out[2 * rows :]


def takes(way, hop, half):
    return hop < HOPS or way == half


def main_kernel(
    dims,
    x_ref, wq, wk, wv, wo, wu, wd, kp, vp, oh_ref, e0_ref, e1_ref, et_ref, pres_ref, lane_ref,
    y_ref, knew_ref,
    h_all, hsel, wbig, wk_v, wv_v, wo_v, wu_v, kv_v, q_ref, kn_ref, s_ref, oa, ob, a_ref, ms_ref, pd, rd,
    olhs, pf, rf, hm, act,
    ag_send, ag_recv, dd_send, dd_recv, own_send, own_recv, rs_send, rs_recv, x_send, x_recv, f_send, f_recv, m_send, m_recv,
    w_sem,
):
    layers, d_model, ff, chips, seqs, slots, kv_heads, head, page, rep_heads = dims
    lanes = 128
    me = lax.axis_index("kv")
    z = me // 2
    c = lax.rem(me, 2)
    peer = {"kv": z * 2 + 1 - c}
    pair = 2 * seqs
    half_d = d_model // 2
    own_rows = rep_heads * head
    sub = own_rows // 2
    d_cols = 256

    def chip(step):
        return lax.rem(z + step + 2 * chips, chips)

    def ring_to(way):
        return {"kv": 2 * chip(1 if way == 0 else -1) + c}

    barrier = pltpu.get_barrier_semaphore()
    for target in (peer, ring_to(0), ring_to(1)):
        pl.semaphore_signal(barrier, inc=1, device_id=target, device_id_type=MESH)
    pl.semaphore_wait(barrier, 3)

    heads_cols = 2 * rep_heads * head
    ff_half = ff // 2

    def load(name, l):
        src, dst, i = {
            "q": (lambda: wq.at[l], lambda: wbig.at[pl.ds(0, d_model), :], 0),
            "k": (lambda: wk.at[l], lambda: wk_v, 1),
            "v": (lambda: wv.at[l], lambda: wv_v, 2),
            "o": (lambda: wo.at[l, pl.ds(pl.multiple_of(c * heads_cols, heads_cols), heads_cols), :], lambda: wo_v, 3),
            "u": (lambda: wu.at[l, :, pl.ds(pl.multiple_of(c * ff_half, ff_half), ff_half)], lambda: wu_v, 4),
            "d": (lambda: wd.at[l, pl.ds(pl.multiple_of(c * ff_half, ff_half), ff_half), :], lambda: wbig.at[pl.ds(0, ff_half), :], 5),
            "K": (lambda: kp.at[l], lambda: kv_v.at[0], 6),
            "V": (lambda: vp.at[l], lambda: kv_v.at[1], 7),
        }[name]
        return pltpu.make_async_copy(src(), dst(), w_sem.at[i])

    def block(t, zz, cc, half):
        return h_all.at[t, pl.ds(pl.multiple_of(zz * pair + cc * seqs, seqs), seqs), pl.ds(half * half_d, half_d)]

    def ag_copy(t, way, hop, half):
        sgn = 1 if way == 0 else -1
        ref = block(t, chip(-sgn * (hop - 1)), c, half)
        return pltpu.make_async_remote_copy(
            src_ref=ref, dst_ref=ref, send_sem=ag_send.at[t, way, hop - 1, half], recv_sem=ag_recv.at[t, way, hop - 1, half],
            device_id=ring_to(way), device_id_type=MESH)

    def dd_copy(t, way, hop, half):
        sgn = 1 if way == 0 else -1
        ref = block(t, chip(-sgn * hop), c, half)
        return pltpu.make_async_remote_copy(
            src_ref=ref, dst_ref=ref, send_sem=dd_send.at[t, way, hop - 1, half], recv_sem=dd_recv.at[t, way, hop - 1, half],
            device_id=peer, device_id_type=MESH)

    def own_copy(t, half):
        ref = block(t, z, c, half)
        return pltpu.make_async_remote_copy(
            src_ref=ref, dst_ref=ref, send_sem=own_send.at[t, half], recv_sem=own_recv.at[t, half],
            device_id=peer, device_id_type=MESH)

    def ag_start(t):
        for half in range(2):
            for way in range(2):
                ag_copy(t, way, 1, half).start()
        for half in range(2):
            own_copy(t, half).start()

    def ag_hop(t, hop):
        for half in range(2):
            for way in range(2):
                if takes(way, hop, half):
                    ag_copy(t, way, hop, half).wait_recv()
                    if hop < HOPS and takes(way, hop + 1, half):
                        ag_copy(t, way, hop + 1, half).start()
                    dd_copy(t, way, hop, half).start()

    def ag_finish(t):
        for half in range(2):
            own_copy(t, half).wait_recv()
            own_copy(t, half).wait_send()
            for way in range(2):
                for hop in range(1, HOPS + 1):
                    if takes(way, hop, half):
                        dd_copy(t, way, hop, half).wait_recv()
                        dd_copy(t, way, hop, half).wait_send()
                        ag_copy(t, way, hop, half).wait_send()

    def rs_copy(t, way, k, half):
        sgn = 1 if way == 0 else -1
        return pltpu.make_async_remote_copy(
            src_ref=pd.at[t, chip(sgn * k), half], dst_ref=rd.at[t, way, k - 1, half],
            send_sem=rs_send.at[t, way, k - 1, half], recv_sem=rs_recv.at[t, way, k - 1, half],
            device_id=ring_to(way), device_id_type=MESH)

    def merge(t, way, k, half):
        sgn = 1 if way == 0 else -1
        zz = chip(sgn * (k - 1))
        got = rd.at[t, way, k - 1, half]
        mine = pd.at[t, zz, half]
        m1, l1 = got[pl.ds(sub, 8), :], got[pl.ds(sub + 8, 8), :]
        m2, l2 = mine[pl.ds(sub, 8), :], mine[pl.ds(sub + 8, 8), :]
        m = jnp.maximum(m1, m2)
        a1, a2 = jnp.exp(m1 - m), jnp.exp(m2 - m)
        mine[pl.ds(sub, 8), :] = m
        mine[pl.ds(sub + 8, 8), :] = a1 * l1 + a2 * l2
        for i in range(rep_heads // 2):
            r = half * (rep_heads // 2) + i
            at = pl.ds(i * head, head)
            mine[at, :] = a1[r : r + 1] * got[at, :] + a2[r : r + 1] * mine[at, :]

    def rs_start(t):
        for half in range(2):
            for way in range(2):
                rs_copy(t, way, HOPS if takes(way, HOPS, half) else HOPS - 1, half).start()

    def rs_step(t, k):
        for half in range(2):
            for way in range(2):
                if takes(way, k, half):
                    rs_copy(t, way, k, half).wait_recv()
                    merge(t, way, k, half)
                    if k > 1:
                        rs_copy(t, way, k - 1, half).start()

    def rs_finish(t):
        for half in range(2):
            for way in range(2):
                for k in range(1, HOPS + 1):
                    if takes(way, k, half):
                        rs_copy(t, way, k, half).wait_send()

    def select(t):
        def body(nb, _):
            cols = pl.ds(pl.multiple_of(nb * d_cols, d_cols), d_cols)
            hsel[:, cols] = dot(oh_ref[...], h_all[t, :, cols]).astype(BF16)
            return 0

        lax.fori_loop(0, d_model // d_cols, body, 0)

    def turned(w):
        return dot(hsel[...], w).astype(BF16).astype(F32).T

    def project(t):
        per = d_cols // head

        def body(nb, _):
            cols = pl.ds(pl.multiple_of(nb * d_cols, d_cols), d_cols)
            q_ref[pl.ds(nb * per, per)] = turned(wbig[pl.ds(0, d_model), cols]).reshape(per, head, lanes)
            return 0

        lax.fori_loop(0, kv_heads * rep_heads // per, body, 0)
        for i, w in enumerate((wk_v, wv_v)):
            kn_ref[t, i] = turned(w[...])

    def attend(t, kvh):
        rows = pl.ds(pl.multiple_of(kvh * head, head), head)
        live = pl.ds(0, slots)
        scale = head ** -0.5
        owner, which = kvh // 2, lax.rem(kvh, 2)
        out = oa.at[t, owner, which]

        def scores(keys):
            parts = [
                jnp.concatenate(
                    [jnp.sum(q_ref[kvh * rep_heads + h, :, live] * key, axis=0, keepdims=True) for h in range(rep_heads)], axis=0)
                for key in keys
            ]
            return parts

        def qk(pb, _):
            keys = [kv_v[0, pb * 4 + i, rows, :].astype(F32) for i in range(4)]
            for i, part in enumerate(scores(keys)):
                s_ref[pb * 4 + i, :, live] = part
            return 0

        lax.fori_loop(0, page // 4, qk, 0)
        fresh = list(range(t + 1))
        news = scores([kn_ref[i, 0, rows, live] for i in fresh])
        lim = lane_ref[0:1, live]
        has_new = lane_ref[1:2, live] > 0
        news = [jnp.where(has_new, s * scale, NEG) for s in news]
        pos = lax.broadcasted_iota(jnp.int32, (page, rep_heads, slots), 0)
        valid = pos < lim[None]
        old = jnp.where(valid, s_ref[:, :, live] * scale, NEG)
        m = jnp.max(old, axis=0)
        for s in news:
            m = jnp.maximum(m, s)
        probs = jnp.where(valid, jnp.exp(old - m[None]), 0.0)
        s_ref[:, :, live] = probs
        news = [jnp.where(has_new, jnp.exp(s - m), 0.0) for s in news]
        total = jnp.sum(probs, axis=0)
        for p in news:
            total = total + p
        out[pl.ds(own_rows, rep_heads), live] = m
        out[pl.ds(own_rows + 8, rep_heads), live] = total
        vals = [kn_ref[i, 1, rows, live] for i in fresh]
        for h in range(rep_heads):
            acc = news[0][h : h + 1] * vals[0]
            for p, v in zip(news[1:], vals[1:], strict=True):
                acc = acc + p[h : h + 1] * v
            out[pl.ds(h * head, head), live] = acc

        def pv(pb, _):
            vals = [kv_v[1, pb * 4 + i, rows, :].astype(F32) for i in range(4)]
            ps = [s_ref[pb * 4 + i, :, live] for i in range(4)]
            for h in range(rep_heads):
                at = pl.ds(h * head, head)
                acc = out[at, live]
                for p, v in zip(ps, vals, strict=True):
                    acc = acc + p[h : h + 1] * v
                out[at, live] = acc
            return 0

        lax.fori_loop(0, page // 4, pv, 0)

    def exchange(t):
        return pltpu.make_async_remote_copy(
            src_ref=oa.at[t, 1 - c], dst_ref=ob.at[t], send_sem=x_send.at[t], recv_sem=x_recv.at[t],
            device_id=peer, device_id_type=MESH)

    lane = lax.broadcasted_iota(jnp.int32, (1, lanes), 1)
    low_lanes = lane < pair

    def by_chip(parts, put):
        for zp in range(chips // 2):
            a, b = (p[:, zp * lanes : (zp + 1) * lanes] for p in parts)
            put(2 * zp, jnp.where(low_lanes, a, pltpu.roll(b, pair, 1)))
            put(2 * zp + 1, jnp.where(low_lanes, pltpu.roll(a, pair, 1), b))

    def scatter(t):
        both = [e0_ref[...], e1_ref[...]]
        tops, sums = [], []
        for hh in range(2):
            stat = [
                jnp.concatenate([oa[t, c, hh, pl.ds(own_rows + o, 8), :], ob[t, hh, pl.ds(own_rows + o, 8), :]], axis=1)
                for o in (0, 8)
            ]
            tops.append(stat[0])
            sums.append(stat[1])
        dense_m, dense_l = [], []
        for hh in range(2):
            m_page = [jnp.where(pres_ref[i : i + 1, :] > 0, exact_dot(tops[hh], both[i]), NEG) for i in range(2)]
            m_seq = jnp.maximum(m_page[0], m_page[1])
            back = exact_dot(m_seq, et_ref[...])
            a = jnp.exp(jnp.minimum(tops[hh] - back, 0.0))
            a_ref[hh] = a
            dense_m.append(m_seq)
            dense_l.append(exact_dot(sums[hh] * a, e0_ref[...] + e1_ref[...]))
        for dense, at in ((dense_m, sub), (dense_l, sub + 8)):
            def put(zz, v, at=at):
                for half in range(2):
                    pd[t, zz, half, pl.ds(at, 8), :] = v

            by_chip(dense, put)

        def body(i, _):
            half, r = i // (rep_heads // 2), lax.rem(i, rep_heads // 2)
            at = pl.ds(pl.multiple_of(i * head, head), head)
            parts = []
            for hh in range(2):
                o = jnp.concatenate([oa[t, c, hh, at, :], ob[t, hh, at, :]], axis=1)
                parts.append(exact_dot(o * a_ref[hh, pl.ds(i, 1), :], e0_ref[...] + e1_ref[...]))

            def put(zz, v):
                pd[t, zz, half, pl.ds(pl.multiple_of(r * head, head), head), :] = v

            by_chip(parts, put)
            return 0

        lax.fori_loop(0, rep_heads, body, 0)

    def finalize(t):
        for half in range(2):
            mine = pd.at[t, z, half]
            inv = 1.0 / mine[pl.ds(sub + 8, 8), :]
            rows = []
            for i in range(rep_heads // 2):
                r = half * (rep_heads // 2) + i
                rows.append(mine[pl.ds(i * head, head), :] * inv[r : r + 1])
            turned_o = jnp.concatenate(rows, axis=0).T.astype(BF16)
            for hh in range(2):
                olhs[:, pl.ds(hh * own_rows + half * sub, sub)] = turned_o[hh * pair : (hh + 1) * pair]

    def f_copy(t, stage):
        return pltpu.make_async_remote_copy(
            src_ref=pf.at[stage, 1 - c], dst_ref=rf.at[t, stage], send_sem=f_send.at[t, stage], recv_sem=f_recv.at[t, stage],
            device_id=peer, device_id_type=MESH)

    def m_copy(t):
        return pltpu.make_async_remote_copy(
            src_ref=hm.at[t, c], dst_ref=hm.at[t, c], send_sem=m_send.at[t], recv_sem=m_recv.at[t],
            device_id=peer, device_id_type=MESH)

    def own_block(t):
        return pl.ds(pl.multiple_of(z * pair + c * seqs, seqs), seqs)

    def spread(stage, cols, val):
        pf[stage, 0, :, cols] = val[:seqs]
        pf[stage, 1, :, cols] = val[seqs:]

    def out_proj(t):
        def body(nb, _):
            cols = pl.ds(pl.multiple_of(nb * d_cols, d_cols), d_cols)
            spread(0, cols, dot(olhs[...], wo_v[:, cols]))
            return 0

        lax.fori_loop(0, d_model // d_cols, body, 0)
        f_copy(t, 0).start()
        f_copy(t, 0).wait()
        hm[t, c] = (h_all[t, own_block(t), :].astype(F32) + (pf[0, c] + rf[t, 0])).astype(BF16)
        m_copy(t).start()
        m_copy(t).wait()

    def up(t):
        def body(nb, _):
            cols = pl.ds(pl.multiple_of(nb * d_cols, d_cols), d_cols)
            lhs = hm[t].reshape(pair, d_model)
            u = dot(lhs, wu_v[:, cols]).astype(BF16).astype(F32)
            act[:, cols] = jax.nn.gelu(u, approximate=True).astype(BF16)
            return 0

        lax.fori_loop(0, ff_half // d_cols, body, 0)

    def down(t):
        def body(nb, _):
            cols = pl.ds(pl.multiple_of(nb * d_cols, d_cols), d_cols)
            spread(1, cols, dot(act[...], wbig[pl.ds(0, ff_half), cols]))
            return 0

        lax.fori_loop(0, d_model // d_cols, body, 0)
        f_copy(t, 1).start()
        f_copy(t, 1).wait()
        new = (hm[t, c].astype(F32) + (pf[1, c] + rf[t, 1])).astype(BF16)
        h_all[t, own_block(t), :] = new
        y_ref[t] = new

    for name in ("q", "k", "v", "K", "V", "o", "u"):
        load(name, 0).start()
    oa[...] = jnp.zeros_like(oa)
    for t in range(2):
        h_all[t, own_block(t), :] = x_ref[t]
        ag_start(t)

    def layer(l, _):
        more = l + 1 < layers

        def refill(*names):
            @pl.when(more)
            def _():
                for name in names:
                    load(name, l + 1).start()

        for t in range(2):
            for hop in range(1, HOPS + 1):
                ag_hop(t, hop)
            ag_finish(t)
        for name in ("q", "k", "v", "K", "V"):
            load(name, l).wait()
        for t in range(2):
            select(t)
            project(t)
            for i in range(2):
                knew_ref[l, t, i] = kn_ref[t, i].astype(BF16)
            if t == 1:
                load("d", l).start()
                refill("k", "v")

            def heads(kvh, _, t=t):
                attend(t, kvh)
                return 0

            lax.fori_loop(0, kv_heads, heads, 0)
            if t == 1:
                refill("K", "V")
            exchange(t).start()
            exchange(t).wait()
            scatter(t)
            rs_start(t)
        load("o", l).wait()
        load("u", l).wait()
        load("d", l).wait()
        for t in range(2):
            for k in range(HOPS, 0, -1):
                rs_step(t, k)
            rs_finish(t)
            finalize(t)
            out_proj(t)
            if t == 1:
                refill("o")
            up(t)
            if t == 1:
                refill("u")
            down(t)
            if t == 1:
                refill("q")

            @pl.when(more)
            def _(t=t):
                ag_start(t)

        return 0

    lax.fori_loop(0, layers, layer, 0)


def pool_kernel(vec_ref, move_ref, mig_ref, new_ref, pool_ref, out_ref):
    rows, slots = pool_ref.shape[2], pool_ref.shape[3]
    live = slice(0, slots)
    at0, at1, keep = vec_ref[0:1, live], vec_ref[1:2, live], vec_ref[2:3, live] > 0
    base = pl.program_id(1) * pool_ref.shape[1]
    new0, new1 = new_ref[0, 0, 0, :, live].astype(F32), new_ref[0, 1, 0, :, live].astype(F32)
    for i in range(pool_ref.shape[1]):
        moved = lax.dot_general(
            mig_ref[0, :, i * rows : (i + 1) * rows], move_ref[...], (((0,), (0,)), ((), ())), preferred_element_type=F32)
        val = jnp.where(keep, pool_ref[0, i].astype(F32), moved)
        val = jnp.where(at0 == base + i, new0, val)
        val = jnp.where(at1 == base + i, new1, val)
        out_ref[0, i] = val.astype(BF16)


def new_pool(pool, mig, knew, which, vec, move):
    layers, page, rows, slots = pool.shape
    step = 8
    entries = mig.shape[1]
    return pl.pallas_call(
        pool_kernel,
        out_shape=jax.ShapeDtypeStruct(pool.shape, BF16),
        grid=(layers, page // step),
        in_specs=[
            pl.BlockSpec(vec.shape, lambda l, i: (0, 0)),
            pl.BlockSpec(move.shape, lambda l, i: (0, 0)),
            pl.BlockSpec((1, entries, step * rows), lambda l, i: (which, 0, l * (page // step) + i)),
            pl.BlockSpec((1, 2, 1, rows, 128), lambda l, i: (l, 0, which, 0, 0)),
            pl.BlockSpec((1, step, rows, slots), lambda l, i: (l, i, 0, 0)),
        ],
        out_specs=pl.BlockSpec((1, step, rows, slots), lambda l, i: (l, i, 0, 0)),
        compiler_params=pltpu.CompilerParams(dimension_semantics=("arbitrary", "arbitrary"), vmem_limit_bytes=32 << 20),
        name="new_pool",
    )(vec, move, mig, knew, pool)


def slot_tables(table, lens, src, dst, dev, slots, page):
    ids = dev * slots + jnp.arange(slots, dtype=jnp.int32)
    from_src = ids[:, None] == src[None, :]
    is_src = jnp.any(from_src, axis=1)
    is_dst = jnp.any(ids[:, None] == dst[None, :], axis=1)
    target = jnp.where(is_src, jnp.sum(jnp.where(from_src, dst[None, :], 0), axis=1), ids)
    hit = [table[None, :, p] == target[:, None] for p in range(2)]
    live = [h & ~is_dst[:, None] for h in hit]
    return ids, is_src, is_dst, hit, live


def pad_rows(a, rows):
    return jnp.pad(a, ((0, rows - a.shape[0]), (0, 0)))


def solution(mesh):
    devs = mesh.shape["kv"]
    chips = devs // 2
    pool_spec = P(("rep", "kv"))
    tok_spec = P(None, ("rep", "kv"), None)

    def device_fn(embeds, w_query, w_key, w_value, w_out, w_up, w_down, k_pool, v_pool, new_table, seq_lens, mig_src, mig_dst):
        slots, layers, page, kv_heads, head = k_pool.shape
        seqs, d_model = embeds.shape[1:]
        ff = w_up.shape[2]
        rep_heads = w_query.shape[2] // head // kv_heads
        total = seqs * devs
        dev = lax.axis_index("kv")
        peer = dev + 1 - 2 * lax.rem(dev, 2)
        pools = [jnp.transpose(p, (1, 2, 3, 4, 0)).reshape(layers, page, kv_heads * head, slots) for p in (k_pool, v_pool)]

        ids, is_src, is_dst, hit, live = slot_tables(new_table, seq_lens, mig_src, mig_dst, dev, slots, page)
        peer_live = slot_tables(new_table, seq_lens, mig_src, mig_dst, peer, slots, page)[4]
        onehot = pad_rows((hit[0] | hit[1]).astype(BF16), 128)
        e_page = [jnp.concatenate([pad_rows(live[p].astype(BF16), 128), pad_rows(peer_live[p].astype(BF16), 128)]) for p in range(2)]
        e_back = (e_page[0] + e_page[1]).T
        pres = pad_rows(jnp.stack([jnp.sum(e.astype(F32), axis=0) for e in e_page]), 8)
        length = jnp.sum(jnp.where(hit[0] | hit[1], seq_lens[None, :], 0), axis=1)
        first, last = jnp.any(live[0], axis=1), jnp.any(live[1], axis=1)
        limit = jnp.where(first, jnp.minimum(length, page), jnp.where(last, length - page, 0))
        lane_tab = jnp.pad(jnp.stack([limit, last.astype(jnp.int32)]).astype(jnp.int32), ((0, 6), (0, 128 - slots)))
        on_last = jnp.any(hit[1], axis=1) & ~is_src
        at = [jnp.where(on_last, length - page + t, -1) for t in range(2)]
        keep = ~(is_src | is_dst)
        vec = jnp.pad(jnp.stack(at + [keep.astype(jnp.int32)]).astype(jnp.int32), ((0, 5), (0, 128 - slots)))
        move = (mig_dst[:, None] == ids[None, :]).astype(BF16)
        pick = (mig_src[:, None] == ids[None, :]).astype(BF16)

        mig = jnp.stack([
            lax.dot_general(pick, p.reshape(-1, slots), (((1,), (1,)), ((), ())), preferred_element_type=F32).astype(BF16)
            for p in pools
        ])
        mig = lax.psum(mig, "kv")

        dims = (layers, d_model, ff, chips, seqs, slots, kv_heads, head, page, rep_heads)
        own_rows = rep_heads * head
        sub = own_rows // 2
        kv_cols = kv_heads * head
        big = max(d_model, ff // 2)
        vm, dma = pltpu.VMEM, pltpu.SemaphoreType.DMA
        any_spec, vmem_spec = pl.BlockSpec(memory_space=pl.ANY), pl.BlockSpec(memory_space=pltpu.VMEM)
        flops = 2 * layers * 2 * (128 * d_model * (total + heads_all(w_query, kv_cols)) + 64 * d_model * (d_model + ff) * 2)
        y, knew = pl.pallas_call(
            functools.partial(main_kernel, dims),
            out_shape=[
                jax.ShapeDtypeStruct((2, seqs, d_model), BF16),
                jax.ShapeDtypeStruct((layers, 2, 2, kv_cols, 128), BF16),
            ],
            in_specs=[vmem_spec] + [any_spec] * 8 + [vmem_spec] * 6,
            out_specs=[vmem_spec] * 2,
            scratch_shapes=[
                vm((2, total, d_model), BF16),
                vm((128, d_model), BF16),
                vm((big, d_model), BF16),
                vm((d_model, kv_cols), BF16),
                vm((d_model, kv_cols), BF16),
                vm((2 * own_rows, d_model), BF16),
                vm((d_model, ff // 2), BF16),
                vm((2, page, kv_cols, slots), BF16),
                vm((kv_heads * rep_heads, head, 128), F32),
                vm((2, 2, kv_cols, 128), F32),
                vm((page, rep_heads, 128), F32),
                vm((2, 2, 2, own_rows + 16, 128), F32),
                vm((2, 2, own_rows + 16, 128), F32),
                vm((2, rep_heads, 256), F32),
                vm((2, rep_heads, 256), F32),
                vm((2, chips, 2, sub + 16, 128), F32),
                vm((2, 2, HOPS, 2, sub + 16, 128), F32),
                vm((2 * seqs, 2 * own_rows), BF16),
                vm((2, 2, seqs, d_model), F32),
                vm((2, 2, seqs, d_model), F32),
                vm((2, 2, seqs, d_model), BF16),
                vm((2 * seqs, ff // 2), BF16),
                dma((2, 2, HOPS, 2)), dma((2, 2, HOPS, 2)),
                dma((2, 2, HOPS, 2)), dma((2, 2, HOPS, 2)),
                dma((2, 2)), dma((2, 2)),
                dma((2, 2, HOPS, 2)), dma((2, 2, HOPS, 2)),
                dma((2,)), dma((2,)),
                dma((2, 2)), dma((2, 2)),
                dma((2,)), dma((2,)),
                dma((8,)),
            ],
            compiler_params=pltpu.CompilerParams(collective_id=0, has_side_effects=True, vmem_limit_bytes=67043328),
            cost_estimate=pl.CostEstimate(flops=int(flops), bytes_accessed=int(90e6), transcendentals=0),
            name="decode",
        )(embeds, w_query, w_key, w_value, w_out, w_up, w_down, *pools, onehot, *e_page, e_back, pres, lane_tab)

        outs = [
            jnp.transpose(new_pool(p, mig, knew, i, vec, move).reshape(layers, page, kv_heads, head, slots), (4, 0, 1, 2, 3))
            for i, p in enumerate(pools)
        ]
        return y, outs[0], outs[1]

    def heads_all(w_query, kv_cols):
        return w_query.shape[2] + 2 * kv_cols

    return jax.shard_map(
        device_fn, mesh=mesh,
        in_specs=(tok_spec, P(), P(), P(), P(), P(), P(), pool_spec, pool_spec, P("rep", None), P("rep"), P("rep"), P("rep")),
        out_specs=(tok_spec, pool_spec, pool_spec), check_vma=False)
```

time: 2050 us -> 394 us (0.19)
  local copies, waits for them, and re-layouts: 959 us -> 13.2 us
  blocking collectives: 384 us -> 0 us
  Pallas kernels: 0 us -> 351 us
  waiting for transfers between devices: 239 us -> 0.06 us
  other arithmetic: 240 us -> 6.79 us
  matrix products: 168 us -> 8.2 us
  starting transfers between devices: 26.1 us -> 0.06 us
    scatter x17 -> x0, local copies, waits for them, and re-layouts: 513 us -> none  [the longest x5 234 us: decode_layer(): k_pool.at[local_ids, layer_idx, offsets].set(kv_rows[0], mode='drop')]
    all_gather x4 -> x0, blocking collectives: 384 us -> none  [decode_layer(): lax.all_gather(jnp.stack([new_keys, new_vals]), 'kv', axis=1, tiled=True)]
    pallas_call x0 -> x3, Pallas kernels: none -> 351 us  [the longest x1 332 us: device_fn(): pl.pallas_call(functools.partial(main_kernel, dims), out_shape=[jax.Shape...]
    dot_general x32 -> x2, matrix products: 168 us -> 8.2 us  [device_fn(): lax.dot_general(pick, p.reshape(-1, slots), (((1,), (1,)), ((), ())), pre...]
    slice x28 -> x1, local copies, waits for them, and re-layouts: 126 us -> 0.01 us  [slot_tables(): hit = [table[None, :, p] == target[:, None] for p in range(2)]]
    all_to_all x4 -> x0, waiting for transfers between devices: 124 us -> none  [merge_partials(): received = lax.all_to_all(packed, 'kv', 0, 0, tiled=True)]
    broadcast_in_dim x15 -> x0, local copies, waits for them, and re-layouts: 109 us -> none  [the longest x8 54.5 us: local_partials(): seq_sum[..., None]]
    unnamed x94 -> x25, local copies, waits for them, and re-layouts: 96.2 us -> 10.2 us
  transfers between devices with their start and end apart: 9 -> 1, of which waited for: 4 -> 0; matrix products, arithmetic and copies ran while one was open for 47% -> 2% of each run, Pallas kernels for 0% -> 84%
where the time goes in v1:
time: 394 us
  Pallas kernels  351 us (89%)
  between operations  14.3 us (4%)
  local copies, waits for them, and re-layouts  13.2 us (3%)
  matrix products  8.2 us (2%)
  other arithmetic  6.79 us (2%)
    pallas_call x1, Pallas kernels, device_fn(): pl.pallas_call(functools.partial(main_kernel, dims), out_shape=[jax.Shape...  332 us
    pallas_call x2, Pallas kernels, new_pool(): pl.pallas_call(pool_kernel, out_shape=jax.ShapeDtypeStruct(pool.shape, BF...  19.9 us
    unnamed x25, local copies, waits for them, and re-layouts  10.2 us
    dot_general x2, matrix products, device_fn(): lax.dot_general(pick, p.reshape(-1, slots), (((1,), (1,)), ((), ())), pre...  8.2 us
  transfers between devices with their start and end apart: 1, of which 0 were waited for; matrix products, arithmetic and copies ran while one was open for 2% of the time, Pallas kernels for 84%

profile of v1, /device:TPU:21, one launch (start us, length us, event | category | flops | bytes accessed | tf_op | source)
XLA Modules:
  0.0 394.0 jit_solution(8947697604716056855)
XLA Ops:
  7.2 0.0 copy-start.6
  7.2 0.1 all-reduce.10.cloned.1.call-start
  7.3 0.0 slice-start
  7.3 0.0 copy-start.5
  7.3 0.0 slice-start.1
  7.3 5.9 %fusion = bf16[1,16,32768]{2,1,0:T(8,128)(2,1)S(1)} fusion(bf16[32768,80]{1,0:T(8,128)(2,1)} %bitcast.43, s32[80]{0:T(128)S(1)} %iota_add_fusion.1, s32[16]{0:T(128)} %param.24), kind=kOutput, calls=%fused_computation.2 | convolution fusion | flops 84411648 | bytes 6291840 | tf_op jit(solution)/shard_map/dot_general | solution.py:540
  13.2 0.0 copy-done.6
  13.2 0.0 slice-done
  13.2 0.0 slice-done.1
  13.2 0.0 copy-start.7
  13.2 0.0 copy-start.8
  13.3 0.0 copy-start.9
  13.3 2.3 fusion.1
  15.6 1.5 pad_maximum_fusion
  17.1 0.1 all-reduce.10.cloned.1.call-update
  17.2 0.0 copy-done.7
  17.2 0.1 fusion.7
  17.3 0.0 copy-done.5
  17.3 0.1 compare_reduce_fusion.4
  17.4 0.0 copy-done.8
  17.4 0.5 fusion.12
  18.0 0.3 compare_reduce_fusion
  18.3 0.2 convert_reduce_fusion
  18.4 0.2 convert_reduce_fusion.1
  18.6 0.9 add_bitcast_fusion.et_ref
  19.4 0.1 fusion.2
  19.5 0.1 fusion.3
  19.6 0.0 copy-done.9
  19.6 0.3 select_reduce_fusion
  19.9 0.6 select_bitcast_fusion.1
  20.5 0.6 pad.41.lane_ref
  21.1 0.8 copy.19.oh_ref
  21.9 0.8 copy.21.e1_ref
  22.7 0.8 copy.20.e0_ref
  23.6 0.6 select_maximum_fusion.pres_ref
  24.2 331.5 %decode.1 = (bf16[2,32,2048]{2,1,0:T(8,128)(2,1)}, bf16[2,2,2,256,128]{4,3,2,1,0:T(8,128)(2,1)}) custom-call(bf16[2,32,2048]{2,1,0:T(8,128)(2,1)} %x_ref.1, bf16[2,2048,2048]{2,1,0:T(8,128)(2,1)} %wq.1, bf16[2,2048,256]{2,1,0:T(8,128)(2,1)} %wk.1, bf16[2,2048,256]{2,1,0:T(8,128)(2,1)} %wv.1, bf16[2,2048,2048]{2,1,0:T(8,128)(2,1)} %wo.1, ...), custom_call_target="tpu_custom_call" | custom-call | flops 22548578304 | bytes 90000000 | tf_op jit(solution)/shard_map/decode/pallas_call | solution.py:553
  355.7 0.7 pad_add_fusion.2
  356.4 0.7 compare_convert_fusion.move_ref
  357.1 0.0 all-reduce.10.cloned.1.call-done.mig_ref
  357.1 0.0 copy-start
  357.1 3.4 copy-done
  360.5 0.0 copy-start.2
  360.5 1.6 copy-done.2
  362.1 0.0 copy-start.3
  362.1 1.0 copy-done.3
  363.1 9.9 %new_pool.3 = bf16[2,64,256,80]{3,2,1,0:T(8,128)(2,1)} custom-call(s32[8,128]{1,0:T(8,128)S(1)} %pad.42.vec_ref, bf16[16,80]{1,0:T(8,128)(2,1)S(1)} %compare_convert_fusion.move_ref, bf16[2,16,32768]{2,1,0:T(8,128)(2,1)S(1)} %copy-done.2, bf16[2,2,2,256,128]{4,3,2,1,0:T(8,128)(2,1)S(1)} %copy-done.3, bf16[2,64,256,80]{3,2,1,0:T(8,128)(2,1)S(1)} %bitcast.42), custom_call_target="tpu_custom_call" | custom-call | tf_op jit(solution)/shard_map/new_pool/pallas_call | solution.py:474
  373.1 0.0 copy-start.1
  373.1 3.4 copy-done.1
  376.4 0.0 copy-start.4
  376.4 9.9 %new_pool.2 = bf16[2,64,256,80]{3,2,1,0:T(8,128)(2,1)} custom-call(s32[8,128]{1,0:T(8,128)S(1)} %pad.42.vec_ref, bf16[16,80]{1,0:T(8,128)(2,1)S(1)} %compare_convert_fusion.move_ref, bf16[2,16,32768]{2,1,0:T(8,128)(2,1)S(1)} %copy-done.2, bf16[2,2,2,256,128]{4,3,2,1,0:T(8,128)(2,1)S(1)} %copy-done.3, bf16[2,64,256,80]{3,2,1,0:T(8,128)(2,1)S(1)} %bitcast.45), custom_call_target="tpu_custom_call" | custom-call | tf_op jit(solution)/shard_map/new_pool/pallas_call | solution.py:474
  386.4 0.0 copy-done.4
  386.4 0.7 copy.24
  (10 shorter events, 0.1 us)
Async XLA Ops:
  7.2 6.0 %copy-start.6 = (s32[16]{0:T(128)S(1)}, s32[16]{0:T(128)}, u32[]{:S(2)}) copy-start(s32[16]{0:T(128)} %param.24) | copy-start | bytes 196
  7.2 349.9 %all-reduce.10.cloned.1.call-start = ((), (), s32[]{:S(2)}) async-start(), calls=%async_computation | async-start | bytes 4194304 | tf_op jit(solution)/shard_map/psum | solution.py:543
  7.3 5.9 %slice-start = ((s8[8388608]{0:T(1024)(128)(4,1)}), s8[4194304]{0:T(1024)(128)(4,1)S(1)}, s32[]{:S(2)}) async-start(s8[8388608]{0:T(1024)(128)(4,1)} %bitcast.39), calls=%async_computation.1 | async-start | bytes 8388608
  7.3 10.0 %copy-start.5 = (s32[80]{0:T(128)}, s32[80]{0:T(128)S(1)}, u32[]{:S(2)}) copy-start(s32[80]{0:T(128)S(1)} %iota_add_fusion.1) | copy-start | bytes 964
  7.3 5.9 %slice-start.1 = ((s8[8388608]{0:T(1024)(128)(4,1)}), s8[4194304]{0:T(1024)(128)(4,1)S(1)}, s32[]{:S(2)}) async-start(s8[8388608]{0:T(1024)(128)(4,1)} %bitcast.39), calls=%async_computation.2 | async-start | bytes 8388608
  13.2 4.0 %copy-start.7 = (s32[16]{0:T(128)S(1)}, s32[16]{0:T(128)}, u32[]{:S(2)}) copy-start(s32[16]{0:T(128)} %param.25) | copy-start | bytes 196
  13.2 4.2 %copy-start.8 = (s32[512,2]{0,1:T(2,128)S(1)}, s32[512,2]{0,1:T(2,128)}, u32[]{:S(2)}) copy-start(s32[512,2]{0,1:T(2,128)} %param.22) | copy-start | bytes 12292
  13.3 6.3 %copy-start.9 = (s32[512]{0:T(512)S(1)}, s32[512]{0:T(512)}, u32[]{:S(2)}) copy-start(s32[512]{0:T(512)} %param.23) | copy-start | bytes 6148
  357.1 3.4 copy-start
  360.5 1.6 copy-start.2
  362.1 1.0 copy-start.3
  373.1 3.4 copy-start.1
  376.4 9.9 %copy-start.4 = (bf16[2,32,2048]{2,1,0:T(8,128)(2,1)S(1)}, bf16[2,32,2048]{2,1,0:T(8,128)(2,1)}, u32[]{:S(2)}) copy-start(bf16[2,32,2048]{2,1,0:T(8,128)(2,1)} %get-tuple-element.33) | copy-start | bytes 786436
Sparse Core Ops, SparseCore 0:
  17.3 119.6 all-reduce.9

commit v2 on v1

--- a/solution.py
+++ b/solution.py
@@ -26,10 +26,23 @@
     return jnp.concatenate([hi, mid, low], axis=0)
 
 
-def exact_dot(x, onehot):
+def exact_dot(x, onehot, across=False):
     rows = x.shape[0]
-    out = dot(split3(x), onehot)
+    dims = (((1,), (1 if across else 0,)), ((), ()))
+    out = lax.dot_general(split3(x), onehot, dims, preferred_element_type=F32)
     return out[:rows] + out[rows : 2 * rows] + out[2 * rows :]
+
+
+def sums_to_rows(parts):
+    sub = lax.broadcasted_iota(jnp.int32, parts[0].shape, 0)
+    for shift in (4, 2, 1):
+        half = len(parts) // 2
+        high = (sub & shift) != 0
+        parts = [
+            jnp.where(high, a + pltpu.roll(a, shift, 0), b + pltpu.roll(b, 8 - shift, 0))
+            for a, b in zip(parts[half:], parts[:half], strict=True)
+        ]
+    return parts[0]
 
 
 def takes(way, hop, half):
@@ -38,7 +51,7 @@
 
 def main_kernel(
     dims,
-    x_ref, wq, wk, wv, wo, wu, wd, kp, vp, oh_ref, e0_ref, e1_ref, et_ref, pres_ref, lane_ref,
+    x_ref, wq, wk, wv, wo, wu, wd, kp, vp, oh_ref, e0_ref, e1_ref, es_ref, pres_ref, lane_ref,
     y_ref, knew_ref,
     h_all, hsel, wbig, wk_v, wv_v, wo_v, wu_v, kv_v, q_ref, kn_ref, s_ref, oa, ob, a_ref, ms_ref, pd, rd,
     olhs, pf, rf, hm, act,
@@ -162,14 +175,13 @@
             for way in range(2):
                 rs_copy(t, way, HOPS if takes(way, HOPS, half) else HOPS - 1, half).start()
 
-    def rs_step(t, k):
-        for half in range(2):
-            for way in range(2):
-                if takes(way, k, half):
-                    rs_copy(t, way, k, half).wait_recv()
-                    merge(t, way, k, half)
-                    if k > 1:
-                        rs_copy(t, way, k - 1, half).start()
+    def rs_step(t, k, late):
+        for way in range(2):
+            half = way if late else 1 - way
+            rs_copy(t, way, k, half).wait_recv()
+            merge(t, way, k, half)
+            if k > 1:
+                rs_copy(t, way, k - 1, half).start()
 
     def rs_finish(t):
         for half in range(2):
@@ -209,12 +221,11 @@
         out = oa.at[t, owner, which]
 
         def scores(keys):
-            parts = [
-                jnp.concatenate(
-                    [jnp.sum(q_ref[kvh * rep_heads + h, :, live] * key, axis=0, keepdims=True) for h in range(rep_heads)], axis=0)
-                for key in keys
-            ]
-            return parts
+            sums = []
+            for h in range(rep_heads):
+                q = q_ref[kvh * rep_heads + h, :, live]
+                sums.append([jnp.sum((q * key).reshape(head // 8, 8, slots), axis=0) for key in keys])
+            return [sums_to_rows([part[i] for part in sums]) for i in range(len(keys))]
 
         def qk(pb, _):
             keys = [kv_v[0, pb * 4 + i, rows, :].astype(F32) for i in range(4)]
@@ -290,11 +301,11 @@
         for hh in range(2):
             m_page = [jnp.where(pres_ref[i : i + 1, :] > 0, exact_dot(tops[hh], both[i]), NEG) for i in range(2)]
             m_seq = jnp.maximum(m_page[0], m_page[1])
-            back = exact_dot(m_seq, et_ref[...])
+            back = exact_dot(m_seq, es_ref[...], across=True)
             a = jnp.exp(jnp.minimum(tops[hh] - back, 0.0))
             a_ref[hh] = a
             dense_m.append(m_seq)
-            dense_l.append(exact_dot(sums[hh] * a, e0_ref[...] + e1_ref[...]))
+            dense_l.append(exact_dot(sums[hh] * a, es_ref[...]))
         for dense, at in ((dense_m, sub), (dense_l, sub + 8)):
             def put(zz, v, at=at):
                 for half in range(2):
@@ -308,7 +319,7 @@
             parts = []
             for hh in range(2):
                 o = jnp.concatenate([oa[t, c, hh, at, :], ob[t, hh, at, :]], axis=1)
-                parts.append(exact_dot(o * a_ref[hh, pl.ds(i, 1), :], e0_ref[...] + e1_ref[...]))
+                parts.append(exact_dot(o * a_ref[hh, pl.ds(i, 1), :], es_ref[...]))
 
             def put(zz, v):
                 pd[t, zz, half, pl.ds(pl.multiple_of(r * head, head), head), :] = v
@@ -355,19 +366,26 @@
 
         lax.fori_loop(0, d_model // d_cols, body, 0)
         f_copy(t, 0).start()
+
+    def mid(t):
         f_copy(t, 0).wait()
         hm[t, c] = (h_all[t, own_block(t), :].astype(F32) + (pf[0, c] + rf[t, 0])).astype(BF16)
         m_copy(t).start()
-        m_copy(t).wait()
-
-    def up(t):
+
+    def up(t, halfway):
         def body(nb, _):
             cols = pl.ds(pl.multiple_of(nb * d_cols, d_cols), d_cols)
             lhs = hm[t].reshape(pair, d_model)
             u = dot(lhs, wu_v[:, cols]).astype(BF16).astype(F32)
             act[:, cols] = jax.nn.gelu(u, approximate=True).astype(BF16)
-            return 0
-
+
+            @pl.when(nb == ff_half // d_cols // 2)
+            def _():
+                halfway()
+
+            return 0
+
+        m_copy(t).wait()
         lax.fori_loop(0, ff_half // d_cols, body, 0)
 
     def down(t):
@@ -378,20 +396,49 @@
 
         lax.fori_loop(0, d_model // d_cols, body, 0)
         f_copy(t, 1).start()
+
+    def new_h(t):
         f_copy(t, 1).wait()
         new = (hm[t, c].astype(F32) + (pf[1, c] + rf[t, 1])).astype(BF16)
         h_all[t, own_block(t), :] = new
         y_ref[t] = new
 
+    def attend_all(t, between):
+        mine = kv_heads // 2
+
+        def body(i, _):
+            attend(t, jnp.where(i < mine, (1 - c) * mine + i, c * mine + i - mine))
+
+            @pl.when(i == mine - 1)
+            def _():
+                exchange(t).start()
+
+            for at, work in between.items():
+                pl.when(i == at)(work)
+            return 0
+
+        lax.fori_loop(0, kv_heads, body, 0)
+
     for name in ("q", "k", "v", "K", "V", "o", "u"):
         load(name, 0).start()
+    h_all[0, own_block(0), :] = x_ref[0]
+    ag_start(0)
+    h_all[1, own_block(1), :] = x_ref[1]
     oa[...] = jnp.zeros_like(oa)
-    for t in range(2):
-        h_all[t, own_block(t), :] = x_ref[t]
-        ag_start(t)
+    ag_hop(0, 1)
+    ag_hop(0, 2)
+    ag_start(1)
+    ag_hop(0, 3)
+    ag_hop(0, 4)
+    ag_finish(0)
 
     def layer(l, _):
         more = l + 1 < layers
+
+        def if_more(work, *args):
+            @pl.when(more)
+            def _():
+                work(*args)
 
         def refill(*names):
             @pl.when(more)
@@ -399,54 +446,70 @@
                 for name in names:
                     load(name, l + 1).start()
 
-        for t in range(2):
-            for hop in range(1, HOPS + 1):
-                ag_hop(t, hop)
-            ag_finish(t)
-        for name in ("q", "k", "v", "K", "V"):
-            load(name, l).wait()
-        for t in range(2):
-            select(t)
-            project(t)
+        def keep_new(t):
             for i in range(2):
                 knew_ref[l, t, i] = kn_ref[t, i].astype(BF16)
-            if t == 1:
-                load("d", l).start()
-                refill("k", "v")
-
-            def heads(kvh, _, t=t):
-                attend(t, kvh)
-                return 0
-
-            lax.fori_loop(0, kv_heads, heads, 0)
-            if t == 1:
-                refill("K", "V")
-            exchange(t).start()
-            exchange(t).wait()
-            scatter(t)
-            rs_start(t)
+
+        for name in ("q", "k", "v"):
+            load(name, l).wait()
+        select(0)
+        project(0)
+        keep_new(0)
+        ag_hop(1, 1)
+        for name in ("K", "V"):
+            load(name, l).wait()
+        attend_all(0, {0: lambda: ag_hop(1, 2), 1: lambda: ag_hop(1, 3), 2: lambda: ag_hop(1, 4)})
+        exchange(0).wait()
+        scatter(0)
+        rs_start(0)
+        ag_finish(1)
+        select(1)
+        project(1)
+        keep_new(1)
+        load("d", l).start()
+        refill("k", "v")
+        rs_step(0, 4, True)
+        attend_all(1, {
+            0: lambda: rs_step(0, 3, False), 1: lambda: rs_step(0, 3, True),
+            2: lambda: rs_step(0, 2, False), 3: lambda: rs_step(0, 2, True)})
+        refill("K", "V")
+        exchange(1).wait()
+        scatter(1)
+        rs_start(1)
+        rs_step(0, 1, False)
+        rs_step(0, 1, True)
+        rs_finish(0)
         load("o", l).wait()
         load("u", l).wait()
         load("d", l).wait()
-        for t in range(2):
-            for k in range(HOPS, 0, -1):
-                rs_step(t, k)
-            rs_finish(t)
-            finalize(t)
-            out_proj(t)
-            if t == 1:
-                refill("o")
-            up(t)
-            if t == 1:
-                refill("u")
-            down(t)
-            if t == 1:
-                refill("q")
-
-            @pl.when(more)
-            def _(t=t):
-                ag_start(t)
-
+        finalize(0)
+        out_proj(0)
+        rs_step(1, 4, True)
+        mid(0)
+        rs_step(1, 3, False)
+        up(0, lambda: rs_step(1, 3, True))
+        down(0)
+        rs_step(1, 2, False)
+        new_h(0)
+        if_more(ag_start, 0)
+        rs_step(1, 2, True)
+        rs_step(1, 1, False)
+        if_more(ag_hop, 0, 1)
+        rs_step(1, 1, True)
+        rs_finish(1)
+        finalize(1)
+        out_proj(1)
+        if_more(ag_hop, 0, 2)
+        mid(1)
+        refill("o")
+        if_more(ag_hop, 0, 3)
+        up(1, lambda: if_more(ag_hop, 0, 4))
+        refill("u")
+        down(1)
+        refill("q")
+        if_more(ag_finish, 0)
+        new_h(1)
+        if_more(ag_start, 1)
         return 0
 
     lax.fori_loop(0, layers, layer, 0)
@@ -483,7 +546,7 @@
             pl.BlockSpec((1, step, rows, slots), lambda l, i: (l, i, 0, 0)),
         ],
         out_specs=pl.BlockSpec((1, step, rows, slots), lambda l, i: (l, i, 0, 0)),
-        compiler_params=pltpu.CompilerParams(dimension_semantics=("arbitrary", "arbitrary"), vmem_limit_bytes=32 << 20),
+        compiler_params=pltpu.CompilerParams(dimension_semantics=("arbitrary", "arbitrary"), vmem_limit_bytes=67043328),
         name="new_pool",
     )(vec, move, mig, knew, pool)
 
@@ -523,7 +586,7 @@
         peer_live = slot_tables(new_table, seq_lens, mig_src, mig_dst, peer, slots, page)[4]
         onehot = pad_rows((hit[0] | hit[1]).astype(BF16), 128)
         e_page = [jnp.concatenate([pad_rows(live[p].astype(BF16), 128), pad_rows(peer_live[p].astype(BF16), 128)]) for p in range(2)]
-        e_back = (e_page[0] + e_page[1]).T
+        e_sum = e_page[0] + e_page[1]
         pres = pad_rows(jnp.stack([jnp.sum(e.astype(F32), axis=0) for e in e_page]), 8)
         length = jnp.sum(jnp.where(hit[0] | hit[1], seq_lens[None, :], 0), axis=1)
         first, last = jnp.any(live[0], axis=1), jnp.any(live[1], axis=1)
@@ -593,7 +656,7 @@
             compiler_params=pltpu.CompilerParams(collective_id=0, has_side_effects=True, vmem_limit_bytes=67043328),
             cost_estimate=pl.CostEstimate(flops=int(flops), bytes_accessed=int(90e6), transcendentals=0),
             name="decode",
-        )(embeds, w_query, w_key, w_value, w_out, w_up, w_down, *pools, onehot, *e_page, e_back, pres, lane_tab)
+        )(embeds, w_query, w_key, w_value, w_out, w_up, w_down, *pools, onehot, *e_page, e_sum, pres, lane_tab)
 
         outs = [
             jnp.transpose(new_pool(p, mig, knew, i, vec, move).reshape(layers, page, kv_heads, head, slots), (4, 0, 1, 2, 3))

time: 394 us -> 295 us (0.75)
  Pallas kernels: 351 us -> 259 us
  local copies, waits for them, and re-layouts: 13.2 us -> 2.92 us
    pallas_call x1, Pallas kernels: 332 us -> 230 us  [device_fn(): pl.pallas_call(functools.partial(main_kernel, dims), out_shape=[jax.Shape...]
    pallas_call x2, Pallas kernels: 19.9 us -> 29.5 us  [new_pool(): pl.pallas_call(pool_kernel, out_shape=jax.ShapeDtypeStruct(pool.shape, BF...]
    unnamed x25 -> x15, local copies, waits for them, and re-layouts: 10.2 us -> 1.73 us
  transfers between devices with their start and end apart: 1 -> 1, of which waited for: 0 -> 0; matrix products, arithmetic and copies ran while one was open for 2% -> 3% of each run, Pallas kernels for 84% -> 78%
where the time goes in v2:
time: 295 us; the launch traced here: 294 us
  Pallas kernels  259 us (88%)
  between operations  14.2 us (5%)
  other arithmetic  8.91 us (3%)
  matrix products  8.2 us (3%)
    pallas_call x1, Pallas kernels, device_fn(): pl.pallas_call(functools.partial(main_kernel, dims), out_shape=[jax.Shape...  230 us
    pallas_call x2, Pallas kernels, new_pool(): pl.pallas_call(pool_kernel, out_shape=jax.ShapeDtypeStruct(pool.shape, BF...  29.5 us
    dot_general x2, matrix products, device_fn(): lax.dot_general(pick, p.reshape(-1, slots), (((1,), (1,)), ((), ())), pre...  8.2 us
  transfers between devices with their start and end apart: 1, of which 0 were waited for; matrix products, arithmetic and copies ran while one was open for 3% of the time, Pallas kernels for 78%

profile of v2, /device:TPU:21, one launch (start us, length us, event | category | flops | bytes accessed | tf_op | source)
XLA Modules:
  0.0 293.7 jit_solution(6286115422522907743)
XLA Ops:
  7.2 0.0 copy-start.1
  7.2 0.1 all-reduce.10.cloned.1.call-start
  7.3 0.0 slice-start
  7.3 0.0 copy-start
  7.3 0.0 slice-start.1
  7.3 5.9 %fusion = bf16[1,16,32768]{2,1,0:T(8,128)(2,1)S(1)} fusion(bf16[32768,80]{1,0:T(8,128)(2,1)} %bitcast.41, s32[80]{0:T(128)S(1)} %iota_add_fusion.1, s32[16]{0:T(128)} %param.24), kind=kOutput, calls=%fused_computation.2 | convolution fusion | flops 84411648 | bytes 6291840 | tf_op jit(solution)/shard_map/dot_general | solution.py:603
  13.2 0.0 copy-done.1
  13.2 0.0 slice-done
  13.2 0.0 slice-done.1
  13.2 0.0 copy-start.2
  13.2 0.0 copy-start.3
  13.3 0.0 copy-start.4
  13.3 2.3 fusion.1
  15.6 1.5 pad_maximum_fusion
  17.1 0.1 all-reduce.10.cloned.1.call-update
  17.2 0.0 copy-done.2
  17.2 0.1 fusion.7
  17.3 0.0 copy-done
  17.3 0.1 compare_reduce_fusion.4
  17.4 0.0 copy-done.3
  17.4 0.5 fusion.12
  18.0 0.3 compare_reduce_fusion
  18.3 0.1 convert_reduce_fusion.1
  18.3 0.1 convert_reduce_fusion
  18.4 0.8 fusion.15.es_ref
  19.2 0.7 fusion.2.e1_ref
  19.9 0.7 fusion.3.e0_ref
  20.6 0.0 copy-done.4
  20.6 0.2 select_reduce_fusion
  20.8 0.6 select_bitcast_fusion.1
  21.4 0.6 pad.41.lane_ref
  22.0 0.7 pad_convert_fusion.oh_ref
  22.6 0.6 select_maximum_fusion.pres_ref
  23.2 229.8 %decode.1 = (bf16[2,32,2048]{2,1,0:T(8,128)(2,1)}, bf16[2,2,2,256,128]{4,3,2,1,0:T(8,128)(2,1)}) custom-call(bf16[2,32,2048]{2,1,0:T(8,128)(2,1)} %x_ref.1, bf16[2,2048,2048]{2,1,0:T(8,128)(2,1)} %wq.1, bf16[2,2048,256]{2,1,0:T(8,128)(2,1)} %wk.1, bf16[2,2048,256]{2,1,0:T(8,128)(2,1)} %wv.1, bf16[2,2048,2048]{2,1,0:T(8,128)(2,1)} %wo.1, ...), custom_call_target="tpu_custom_call" | custom-call | flops 22548578304 | bytes 90000000 | tf_op jit(solution)/shard_map/decode/pallas_call | solution.py:616
  253.1 0.7 pad_add_fusion.2
  253.7 0.6 pad.42.vec_ref
  254.3 1.3 compare_convert_fusion.move_ref
  255.7 0.0 all-reduce.10.cloned.1.call-done.mig_ref
  255.7 14.8 %new_pool.3 = bf16[2,64,256,80]{3,2,1,0:T(8,128)(2,1)} custom-call(s32[8,128]{1,0:T(8,128)} %pad.42.vec_ref, bf16[16,80]{1,0:T(8,128)(2,1)} %compare_convert_fusion.move_ref, bf16[2,16,32768]{2,1,0:T(8,128)(2,1)} %all-reduce.10.cloned.1.call-done.mig_ref, bf16[2,2,2,256,128]{4,3,2,1,0:T(8,128)(2,1)} %get-tuple-element.6.new_ref, ...), custom_call_target="tpu_custom_call" | custom-call | tf_op jit(solution)/shard_map/new_pool/pallas_call | solution.py:537
  270.4 14.8 %new_pool.2 = bf16[2,64,256,80]{3,2,1,0:T(8,128)(2,1)} custom-call(s32[8,128]{1,0:T(8,128)} %pad.42.vec_ref, bf16[16,80]{1,0:T(8,128)(2,1)} %compare_convert_fusion.move_ref, bf16[2,16,32768]{2,1,0:T(8,128)(2,1)} %all-reduce.10.cloned.1.call-done.mig_ref, bf16[2,2,2,256,128]{4,3,2,1,0:T(8,128)(2,1)} %get-tuple-element.6.new_ref, ...), custom_call_target="tpu_custom_call" | custom-call | tf_op jit(solution)/shard_map/new_pool/pallas_call | solution.py:537
  285.2 1.7 copy.18
  (8 shorter events, 0.0 us)
Async XLA Ops:
  7.2 6.0 %copy-start.1 = (s32[16]{0:T(128)S(1)}, s32[16]{0:T(128)}, u32[]{:S(2)}) copy-start(s32[16]{0:T(128)} %param.24) | copy-start | bytes 196
  7.2 248.5 %all-reduce.10.cloned.1.call-start = ((), (), s32[]{:S(2)}) async-start(), calls=%async_computation | async-start | bytes 4194304 | tf_op jit(solution)/shard_map/psum | solution.py:606
  7.3 5.9 %slice-start = ((s8[8388608]{0:T(1024)(128)(4,1)}), s8[4194304]{0:T(1024)(128)(4,1)S(1)}, s32[]{:S(2)}) async-start(s8[8388608]{0:T(1024)(128)(4,1)} %bitcast.38), calls=%async_computation.1 | async-start | bytes 8388608
  7.3 10.0 %copy-start = (s32[80]{0:T(128)}, s32[80]{0:T(128)S(1)}, u32[]{:S(2)}) copy-start(s32[80]{0:T(128)S(1)} %iota_add_fusion.1) | copy-start | bytes 964
  7.3 5.9 %slice-start.1 = ((s8[8388608]{0:T(1024)(128)(4,1)}), s8[4194304]{0:T(1024)(128)(4,1)S(1)}, s32[]{:S(2)}) async-start(s8[8388608]{0:T(1024)(128)(4,1)} %bitcast.38), calls=%async_computation.2 | async-start | bytes 8388608
  13.2 4.0 %copy-start.2 = (s32[16]{0:T(128)S(1)}, s32[16]{0:T(128)}, u32[]{:S(2)}) copy-start(s32[16]{0:T(128)} %param.25) | copy-start | bytes 196
  13.2 4.2 %copy-start.3 = (s32[512,2]{0,1:T(2,128)S(1)}, s32[512,2]{0,1:T(2,128)}, u32[]{:S(2)}) copy-start(s32[512,2]{0,1:T(2,128)} %param.22) | copy-start | bytes 12292
  13.3 7.3 %copy-start.4 = (s32[512]{0:T(512)S(1)}, s32[512]{0:T(512)}, u32[]{:S(2)}) copy-start(s32[512]{0:T(512)} %param.23) | copy-start | bytes 6148
Sparse Core Ops, SparseCore 0:
  17.3 121.5 all-reduce.9

commit v3 on v2

--- a/solution.py
+++ b/solution.py
@@ -68,7 +68,10 @@
     half_d = d_model // 2
     own_rows = rep_heads * head
     sub = own_rows // 2
-    d_cols = 256
+    d_cols = 512
+    s_cols = 1024
+    o_cols = 512
+    u_cols = ff // 2 // 2
 
     def chip(step):
         return lax.rem(z + step + 2 * chips, chips)
@@ -192,14 +195,15 @@
 
     def select(t):
         def body(nb, _):
-            cols = pl.ds(pl.multiple_of(nb * d_cols, d_cols), d_cols)
-            hsel[:, cols] = dot(oh_ref[...], h_all[t, :, cols]).astype(BF16)
-            return 0
-
-        lax.fori_loop(0, d_model // d_cols, body, 0)
+            cols = pl.ds(pl.multiple_of(nb * s_cols, s_cols), s_cols)
+            hsel[:, cols] = dot(oh_ref[pl.ds(0, slots), :], h_all[t, :, cols]).astype(BF16)
+            return 0
+
+        lax.fori_loop(0, d_model // s_cols, body, 0)
 
     def turned(w):
-        return dot(hsel[...], w).astype(BF16).astype(F32).T
+        rows = dot(hsel[...], w).astype(BF16).astype(F32)
+        return jnp.concatenate([rows, jnp.zeros((lanes - slots, rows.shape[1]), F32)], axis=0).T
 
     def project(t):
         per = d_cols // head
@@ -223,8 +227,14 @@
         def scores(keys):
             sums = []
             for h in range(rep_heads):
-                q = q_ref[kvh * rep_heads + h, :, live]
-                sums.append([jnp.sum((q * key).reshape(head // 8, 8, slots), axis=0) for key in keys])
+                q = [q_ref[kvh * rep_heads + h, pl.ds(d, 8), live] for d in range(0, head, 8)]
+                parts = []
+                for key in keys:
+                    acc = q[0] * key[:8]
+                    for i in range(1, head // 8):
+                        acc = acc + q[i] * key[8 * i : 8 * i + 8]
+                    parts.append(acc)
+                sums.append(parts)
             return [sums_to_rows([part[i] for part in sums]) for i in range(len(keys))]
 
         def qk(pb, _):
@@ -288,46 +298,41 @@
             put(2 * zp + 1, jnp.where(low_lanes, pltpu.roll(a, pair, 1), b))
 
     def scatter(t):
-        both = [e0_ref[...], e1_ref[...]]
-        tops, sums = [], []
-        for hh in range(2):
-            stat = [
+        def stat(o):
+            return jnp.concatenate([
                 jnp.concatenate([oa[t, c, hh, pl.ds(own_rows + o, 8), :], ob[t, hh, pl.ds(own_rows + o, 8), :]], axis=1)
-                for o in (0, 8)
-            ]
-            tops.append(stat[0])
-            sums.append(stat[1])
-        dense_m, dense_l = [], []
-        for hh in range(2):
-            m_page = [jnp.where(pres_ref[i : i + 1, :] > 0, exact_dot(tops[hh], both[i]), NEG) for i in range(2)]
-            m_seq = jnp.maximum(m_page[0], m_page[1])
-            back = exact_dot(m_seq, es_ref[...], across=True)
-            a = jnp.exp(jnp.minimum(tops[hh] - back, 0.0))
-            a_ref[hh] = a
-            dense_m.append(m_seq)
-            dense_l.append(exact_dot(sums[hh] * a, es_ref[...]))
-        for dense, at in ((dense_m, sub), (dense_l, sub + 8)):
+                for hh in range(2)
+            ], axis=0)
+
+        top = stat(0)
+        m_page = [jnp.where(pres_ref[i : i + 1, :] > 0, exact_dot(top, e[...]), NEG) for i, e in enumerate((e0_ref, e1_ref))]
+        m_seq = jnp.maximum(m_page[0], m_page[1])
+        a = jnp.exp(jnp.minimum(top - exact_dot(m_seq, es_ref[...], across=True), 0.0))
+        a_ref[0], a_ref[1] = a[:8], a[8:]
+        l_seq = exact_dot(stat(8) * a, es_ref[...])
+        for dense, at in ((m_seq, sub), (l_seq, sub + 8)):
             def put(zz, v, at=at):
                 for half in range(2):
                     pd[t, zz, half, pl.ds(at, 8), :] = v
 
-            by_chip(dense, put)
-
-        def body(i, _):
-            half, r = i // (rep_heads // 2), lax.rem(i, rep_heads // 2)
-            at = pl.ds(pl.multiple_of(i * head, head), head)
-            parts = []
-            for hh in range(2):
-                o = jnp.concatenate([oa[t, c, hh, at, :], ob[t, hh, at, :]], axis=1)
-                parts.append(exact_dot(o * a_ref[hh, pl.ds(i, 1), :], es_ref[...]))
-
-            def put(zz, v):
-                pd[t, zz, half, pl.ds(pl.multiple_of(r * head, head), head), :] = v
-
-            by_chip(parts, put)
-            return 0
-
-        lax.fori_loop(0, rep_heads, body, 0)
+            by_chip([dense[:8], dense[8:]], put)
+
+        def body(n, _):
+            for half in range(2):
+                i = half * (rep_heads // 2) + n
+                at = pl.ds(pl.multiple_of(i * head, head), head)
+                parts = []
+                for hh in range(2):
+                    o = jnp.concatenate([oa[t, c, hh, at, :], ob[t, hh, at, :]], axis=1)
+                    parts.append(exact_dot(o * a_ref[hh, pl.ds(i, 1), :], es_ref[...]))
+
+                def put(zz, v, half=half):
+                    pd[t, zz, half, pl.ds(pl.multiple_of(n * head, head), head), :] = v
+
+                by_chip(parts, put)
+            return 0
+
+        lax.fori_loop(0, rep_heads // 2, body, 0)
 
     def finalize(t):
         for half in range(2):
@@ -360,11 +365,11 @@
 
     def out_proj(t):
         def body(nb, _):
-            cols = pl.ds(pl.multiple_of(nb * d_cols, d_cols), d_cols)
+            cols = pl.ds(pl.multiple_of(nb * o_cols, o_cols), o_cols)
             spread(0, cols, dot(olhs[...], wo_v[:, cols]))
             return 0
 
-        lax.fori_loop(0, d_model // d_cols, body, 0)
+        lax.fori_loop(0, d_model // o_cols, body, 0)
         f_copy(t, 0).start()
 
     def mid(t):
@@ -374,27 +379,26 @@
 
     def up(t, halfway):
         def body(nb, _):
-            cols = pl.ds(pl.multiple_of(nb * d_cols, d_cols), d_cols)
-            lhs = hm[t].reshape(pair, d_model)
-            u = dot(lhs, wu_v[:, cols]).astype(BF16).astype(F32)
+            cols = pl.ds(pl.multiple_of(nb * u_cols, 128), u_cols)
+            u = dot(hm[t].reshape(pair, d_model), wu_v[:, cols]).astype(BF16).astype(F32)
             act[:, cols] = jax.nn.gelu(u, approximate=True).astype(BF16)
 
-            @pl.when(nb == ff_half // d_cols // 2)
+            @pl.when(nb == ff_half // u_cols // 2 - 1)
             def _():
                 halfway()
 
             return 0
 
         m_copy(t).wait()
-        lax.fori_loop(0, ff_half // d_cols, body, 0)
+        lax.fori_loop(0, ff_half // u_cols, body, 0)
 
     def down(t):
         def body(nb, _):
-            cols = pl.ds(pl.multiple_of(nb * d_cols, d_cols), d_cols)
+            cols = pl.ds(pl.multiple_of(nb * o_cols, o_cols), o_cols)
             spread(1, cols, dot(act[...], wbig[pl.ds(0, ff_half), cols]))
             return 0
 
-        lax.fori_loop(0, d_model // d_cols, body, 0)
+        lax.fori_loop(0, d_model // o_cols, body, 0)
         f_copy(t, 1).start()
 
     def new_h(t):
@@ -515,40 +519,57 @@
     lax.fori_loop(0, layers, layer, 0)
 
 
-def pool_kernel(vec_ref, move_ref, mig_ref, new_ref, pool_ref, out_ref):
-    rows, slots = pool_ref.shape[2], pool_ref.shape[3]
+def pool_kernel(vec_ref, move_ref, mig_ref, new_ref, k_ref, v_ref, ko_ref, vo_ref, moved):
+    step, rows, slots = k_ref.shape[1:]
     live = slice(0, slots)
-    at0, at1, keep = vec_ref[0:1, live], vec_ref[1:2, live], vec_ref[2:3, live] > 0
-    base = pl.program_id(1) * pool_ref.shape[1]
-    new0, new1 = new_ref[0, 0, 0, :, live].astype(F32), new_ref[0, 1, 0, :, live].astype(F32)
-    for i in range(pool_ref.shape[1]):
-        moved = lax.dot_general(
-            mig_ref[0, :, i * rows : (i + 1) * rows], move_ref[...], (((0,), (0,)), ((), ())), preferred_element_type=F32)
-        val = jnp.where(keep, pool_ref[0, i].astype(F32), moved)
-        val = jnp.where(at0 == base + i, new0, val)
-        val = jnp.where(at1 == base + i, new1, val)
-        out_ref[0, i] = val.astype(BF16)
-
-
-def new_pool(pool, mig, knew, which, vec, move):
-    layers, page, rows, slots = pool.shape
-    step = 8
+    group = moved.shape[1] // rows
+    tab = vec_ref[...].astype(F32)
+    at0, at1, keep = (tab[i : i + 1, live].astype(BF16) for i in range(3))
+    keep = keep > 0
+    base = pl.program_id(1) * step
+    turns = [(which, g) for which in range(2) for g in range(step // group)]
+
+    def move(which, g, slot):
+        moved[slot] = lax.dot_general(
+            mig_ref[which, :, g * group * rows : (g + 1) * group * rows], move_ref[...], (((0,), (0,)), ((), ())),
+            preferred_element_type=F32).astype(BF16)
+
+    move(0, 0, 0)
+    for n, (which, g) in enumerate(turns):
+        if n + 1 < len(turns):
+            move(*turns[n + 1], (n + 1) % 2)
+        pool_ref, out_ref = ((k_ref, ko_ref), (v_ref, vo_ref))[which]
+        for j in range(group):
+            i = g * group + j
+            pos = jnp.full((1, slots), (base + i).astype(F32), F32).astype(BF16)
+            for r in range(0, rows, 64):
+                cut = slice(r, r + 64)
+                val = jnp.where(keep, pool_ref[0, i, cut], moved[n % 2, j * rows + r : j * rows + r + 64, :])
+                val = jnp.where(at0 == pos, new_ref[0, 0, which, cut, live], val)
+                out_ref[0, i, cut] = jnp.where(at1 == pos, new_ref[0, 1, which, cut, live], val)
+
+
+def new_pools(pools, mig, knew, vec, move):
+    layers, page, rows, slots = pools[0].shape
+    step = 16
     entries = mig.shape[1]
+    block = pl.BlockSpec((1, step, rows, slots), lambda l, i: (l, i, 0, 0))
     return pl.pallas_call(
         pool_kernel,
-        out_shape=jax.ShapeDtypeStruct(pool.shape, BF16),
+        out_shape=[jax.ShapeDtypeStruct(pools[0].shape, BF16)] * 2,
         grid=(layers, page // step),
         in_specs=[
             pl.BlockSpec(vec.shape, lambda l, i: (0, 0)),
             pl.BlockSpec(move.shape, lambda l, i: (0, 0)),
-            pl.BlockSpec((1, entries, step * rows), lambda l, i: (which, 0, l * (page // step) + i)),
-            pl.BlockSpec((1, 2, 1, rows, 128), lambda l, i: (l, 0, which, 0, 0)),
-            pl.BlockSpec((1, step, rows, slots), lambda l, i: (l, i, 0, 0)),
+            pl.BlockSpec((2, entries, step * rows), lambda l, i: (0, 0, l * (page // step) + i)),
+            pl.BlockSpec((1, 2, 2, rows, 128), lambda l, i: (l, 0, 0, 0, 0)),
+            block, block,
         ],
-        out_specs=pl.BlockSpec((1, step, rows, slots), lambda l, i: (l, i, 0, 0)),
+        out_specs=[block, block],
+        scratch_shapes=[pltpu.VMEM((2, 4 * rows, slots), BF16)],
         compiler_params=pltpu.CompilerParams(dimension_semantics=("arbitrary", "arbitrary"), vmem_limit_bytes=67043328),
-        name="new_pool",
-    )(vec, move, mig, knew, pool)
+        name="new_pools",
+    )(vec, move, mig, knew, *pools)
 
 
 def slot_tables(table, lens, src, dst, dev, slots, page):
@@ -623,7 +644,7 @@
             out_specs=[vmem_spec] * 2,
             scratch_shapes=[
                 vm((2, total, d_model), BF16),
-                vm((128, d_model), BF16),
+                vm((slots, d_model), BF16),
                 vm((big, d_model), BF16),
                 vm((d_model, kv_cols), BF16),
                 vm((d_model, kv_cols), BF16),
@@ -659,8 +680,8 @@
         )(embeds, w_query, w_key, w_value, w_out, w_up, w_down, *pools, onehot, *e_page, e_sum, pres, lane_tab)
 
         outs = [
-            jnp.transpose(new_pool(p, mig, knew, i, vec, move).reshape(layers, page, kv_heads, head, slots), (4, 0, 1, 2, 3))
-            for i, p in enumerate(pools)
+            jnp.transpose(p.reshape(layers, page, kv_heads, head, slots), (4, 0, 1, 2, 3))
+            for p in new_pools(pools, mig, knew, vec, move)
         ]
         return y, outs[0], outs[1]
 

time: 295 us -> 266 us (0.902)
  Pallas kernels: 259 us -> 232 us
    pallas_call x1, Pallas kernels: 230 us -> 214 us  [device_fn(): pl.pallas_call(functools.partial(main_kernel, dims), out_shape=[jax.Shape...]
    pallas_call x2 -> x1, Pallas kernels: 29.5 us -> 17.4 us  [new_pools(): pl.pallas_call(pool_kernel, out_shape=[jax.ShapeDtypeStruct(pools[0].shap...]
  transfers between devices with their start and end apart: 1 -> 1, of which waited for: 0 -> 0; matrix products, arithmetic and copies ran while one was open for 3% -> 3% of each run, Pallas kernels for 78% -> 81%
where the time goes in v3:
time: 266 us
  Pallas kernels  232 us (87%)
  between operations  14.2 us (5%)
  other arithmetic  8.91 us (3%)
  matrix products  8.2 us (3%)
  local copies, waits for them, and re-layouts  2.92 us (1%)
    pallas_call x1, Pallas kernels, device_fn(): pl.pallas_call(functools.partial(main_kernel, dims), out_shape=[jax.Shape...  214 us
    pallas_call x1, Pallas kernels, new_pools(): pl.pallas_call(pool_kernel, out_shape=[jax.ShapeDtypeStruct(pools[0].shap...  17.4 us
    dot_general x2, matrix products, device_fn(): lax.dot_general(pick, p.reshape(-1, slots), (((1,), (1,)), ((), ())), pre...  8.2 us
  transfers between devices with their start and end apart: 1, of which 0 were waited for; matrix products, arithmetic and copies ran while one was open for 3% of the time, Pallas kernels for 81%

profile of v3, /device:TPU:21, one launch (start us, length us, event | category | flops | bytes accessed | tf_op | source)
XLA Modules:
  0.0 266.0 jit_solution(17084198062217116294)
XLA Ops:
  7.2 0.0 copy-start.1
  7.2 0.1 all-reduce.10.cloned.1.call-start
  7.3 0.0 slice-start
  7.3 0.0 copy-start
  7.3 0.0 slice-start.1
  7.3 5.9 %fusion = bf16[1,16,32768]{2,1,0:T(8,128)(2,1)S(1)} fusion(bf16[32768,80]{1,0:T(8,128)(2,1)} %bitcast.36, s32[80]{0:T(128)S(1)} %iota_add_fusion.1, s32[16]{0:T(128)} %param.24), kind=kOutput, calls=%fused_computation.2 | convolution fusion | flops 84411648 | bytes 6291840 | tf_op jit(solution)/shard_map/dot_general | solution.py:624
  13.2 0.0 copy-done.1
  13.2 0.0 slice-done
  13.2 0.0 slice-done.1
  13.2 0.0 copy-start.2
  13.2 0.0 copy-start.3
  13.3 0.0 copy-start.4
  13.3 2.3 fusion.1
  15.6 1.5 pad_maximum_fusion
  17.1 0.1 all-reduce.10.cloned.1.call-update
  17.2 0.0 copy-done.2
  17.2 0.1 fusion.7
  17.3 0.0 copy-done
  17.3 0.1 compare_reduce_fusion.4
  17.4 0.0 copy-done.3
  17.4 0.5 fusion.12
  18.0 0.3 compare_reduce_fusion
  18.3 0.1 convert_reduce_fusion.1
  18.3 0.1 convert_reduce_fusion
  18.4 0.8 fusion.15.es_ref
  19.2 0.7 fusion.2.e1_ref
  19.9 0.7 fusion.3.e0_ref
  20.6 0.0 copy-done.4
  20.6 0.2 select_reduce_fusion
  20.8 0.6 select_bitcast_fusion.1
  21.4 0.6 pad.41.lane_ref
  22.0 0.7 pad_convert_fusion.oh_ref
  22.6 0.6 select_maximum_fusion.pres_ref
  23.2 214.2 %decode.1 = (bf16[2,32,2048]{2,1,0:T(8,128)(2,1)}, bf16[2,2,2,256,128]{4,3,2,1,0:T(8,128)(2,1)}) custom-call(bf16[2,32,2048]{2,1,0:T(8,128)(2,1)} %x_ref.1, bf16[2,2048,2048]{2,1,0:T(8,128)(2,1)} %wq.1, bf16[2,2048,256]{2,1,0:T(8,128)(2,1)} %wk.1, bf16[2,2048,256]{2,1,0:T(8,128)(2,1)} %wv.1, bf16[2,2048,2048]{2,1,0:T(8,128)(2,1)} %wo.1, ...), custom_call_target="tpu_custom_call" | custom-call | flops 22548578304 | bytes 90000000 | tf_op jit(solution)/shard_map/decode/pallas_call | solution.py:637
  237.5 0.7 pad_add_fusion.2
  238.2 0.6 pad.42.vec_ref
  238.8 1.3 compare_convert_fusion.move_ref
  240.1 0.0 all-reduce.10.cloned.1.call-done.mig_ref
  240.1 17.4 %new_pools.1 = (bf16[2,64,256,80]{3,2,1,0:T(8,128)(2,1)}, bf16[2,64,256,80]{3,2,1,0:T(8,128)(2,1)}) custom-call(s32[8,128]{1,0:T(8,128)} %pad.42.vec_ref, bf16[16,80]{1,0:T(8,128)(2,1)} %compare_convert_fusion.move_ref, bf16[2,16,32768]{2,1,0:T(8,128)(2,1)} %all-reduce.10.cloned.1.call-done.mig_ref, bf16[2,2,2,256,128]{4,3,2,1,0:T(8,128)(2,1)} %get-tuple-element.8.new_ref, ...), custom_call_target="tpu_custom_call" | custom-call | tf_op jit(solution)/shard_map/new_pools/pallas_call | solution.py:557
  257.4 1.7 copy.18
  (8 shorter events, 0.0 us)
Async XLA Ops:
  7.2 6.0 %copy-start.1 = (s32[16]{0:T(128)S(1)}, s32[16]{0:T(128)}, u32[]{:S(2)}) copy-start(s32[16]{0:T(128)} %param.24) | copy-start | bytes 196
  7.2 232.9 %all-reduce.10.cloned.1.call-start = ((), (), s32[]{:S(2)}) async-start(), calls=%async_computation | async-start | bytes 4194304 | tf_op jit(solution)/shard_map/psum | solution.py:627
  7.3 5.9 %slice-start = ((s8[8388608]{0:T(1024)(128)(4,1)}), s8[4194304]{0:T(1024)(128)(4,1)S(1)}, s32[]{:S(2)}) async-start(s8[8388608]{0:T(1024)(128)(4,1)} %bitcast.41), calls=%async_computation.1 | async-start | bytes 8388608
  7.3 10.0 %copy-start = (s32[80]{0:T(128)}, s32[80]{0:T(128)S(1)}, u32[]{:S(2)}) copy-start(s32[80]{0:T(128)S(1)} %iota_add_fusion.1) | copy-start | bytes 964
  7.3 5.9 %slice-start.1 = ((s8[8388608]{0:T(1024)(128)(4,1)}), s8[4194304]{0:T(1024)(128)(4,1)S(1)}, s32[]{:S(2)}) async-start(s8[8388608]{0:T(1024)(128)(4,1)} %bitcast.41), calls=%async_computation.2 | async-start | bytes 8388608
  13.2 4.0 %copy-start.2 = (s32[16]{0:T(128)S(1)}, s32[16]{0:T(128)}, u32[]{:S(2)}) copy-start(s32[16]{0:T(128)} %param.25) | copy-start | bytes 196
  13.2 4.2 %copy-start.3 = (s32[512,2]{0,1:T(2,128)S(1)}, s32[512,2]{0,1:T(2,128)}, u32[]{:S(2)}) copy-start(s32[512,2]{0,1:T(2,128)} %param.22) | copy-start | bytes 12292
  13.3 7.3 %copy-start.4 = (s32[512]{0:T(512)S(1)}, s32[512]{0:T(512)}, u32[]{:S(2)}) copy-start(s32[512]{0:T(512)} %param.23) | copy-start | bytes 6148
Sparse Core Ops, SparseCore 0:
  17.3 123.2 all-reduce.9

commit v4 on v3

--- a/solution.py
+++ b/solution.py
@@ -51,12 +51,13 @@
 
 def main_kernel(
     dims,
-    x_ref, wq, wk, wv, wo, wu, wd, kp, vp, oh_ref, e0_ref, e1_ref, es_ref, pres_ref, lane_ref,
-    y_ref, knew_ref,
+    src_ref, dst_ref, tab_ref, len_ref, x_ref, wq, wk, wv, wo, wu, wd, kp, vp,
+    y_ref, knew_ref, vec_ref, mig_out,
+    oh_ref, e0_ref, e1_ref, es_ref, pres_ref, lane_ref, pick_ref, mg, mx, mr, mf,
     h_all, hsel, wbig, wk_v, wv_v, wo_v, wu_v, kv_v, q_ref, kn_ref, s_ref, oa, ob, a_ref, ms_ref, pd, rd,
     olhs, pf, rf, hm, act,
     ag_send, ag_recv, dd_send, dd_recv, own_send, own_recv, rs_send, rs_recv, x_send, x_recv, f_send, f_recv, m_send, m_recv,
-    w_sem,
+    gs_send, gs_recv, gg_send, gg_recv, gp_send, gp_recv, go_send, go_recv, go_sem, w_sem,
 ):
     layers, d_model, ff, chips, seqs, slots, kv_heads, head, page, rep_heads = dims
     lanes = 128
@@ -85,6 +86,7 @@
     pl.semaphore_wait(barrier, 3)
 
     heads_cols = 2 * rep_heads * head
+    kv_cols = kv_heads * head
     ff_half = ff // 2
 
     def load(name, l):
@@ -423,15 +425,159 @@
 
         lax.fori_loop(0, kv_heads, body, 0)
 
+    entries = src_ref.shape[0]
+
+    def ids_of(dev, axis):
+        shape = (lanes, 1) if axis == 0 else (1, lanes)
+        at = lax.broadcasted_iota(jnp.int32, shape, axis)
+        return jnp.where(at < slots, dev * slots + at, -1)
+
+    def tables():
+        page_of = [tab_ref[p : p + 1, :] for p in range(2)]
+        for g, dev in enumerate((me, z * 2 + 1 - c)):
+            ids = ids_of(dev, 0)
+            target, stale = ids, jnp.zeros_like(ids)
+            for e in range(entries):
+                target = jnp.where(ids == src_ref[e], dst_ref[e], target)
+                stale = jnp.where(ids == dst_ref[e], 1, stale)
+            hit = [jnp.where(p == target, 1.0, 0.0) for p in page_of]
+            live = [jnp.where(stale == 0, h, 0.0) for h in hit]
+            at = pl.ds(g * lanes, lanes)
+            e0_ref[at, :] = live[0].astype(BF16)
+            e1_ref[at, :] = live[1].astype(BF16)
+            es_ref[at, :] = (live[0] + live[1]).astype(BF16)
+            if g == 0:
+                oh_ref[...] = (hit[0] + hit[1]).astype(BF16)
+                held = [h.astype(BF16) for h in (live[0], live[1], hit[1])]
+        for p, e in enumerate((e0_ref, e1_ref)):
+            pres_ref[p : p + 1, :] = jnp.sum(e[...].astype(F32), axis=0, keepdims=True)
+        lens = len_ref[...].astype(F32)
+        rows = jnp.concatenate([lens, jnp.ones_like(lens), jnp.zeros((6, lens.shape[1]), F32)], axis=0).astype(BF16)
+        first, last, fresh = (
+            lax.dot_general(rows, h, (((1,), (1,)), ((), ())), preferred_element_type=F32) for h in held)
+        limit = jnp.where(
+            first[1:2] > 0, jnp.minimum(first[0:1], page), jnp.where(last[1:2] > 0, last[0:1] - page, 0.0))
+        lane_ref[0:1, :] = limit.astype(jnp.int32)
+        lane_ref[1:2, :] = last[1:2].astype(jnp.int32)
+        ids = ids_of(me, 1)
+        is_src, is_dst = jnp.zeros_like(ids), jnp.zeros_like(ids)
+        row = lax.broadcasted_iota(jnp.int32, (entries, lanes), 0)
+        pick = jnp.zeros((entries, lanes), F32)
+        for e in range(entries):
+            is_src = jnp.where(ids == src_ref[e], 1, is_src)
+            is_dst = jnp.where(ids == dst_ref[e], 1, is_dst)
+            pick = jnp.where(row == e, jnp.where(ids == src_ref[e], 1.0, 0.0), pick)
+        pick_ref[...] = pick[:, :slots].astype(BF16)
+        on_last = jnp.where(is_src == 0, fresh[1:2], 0.0) > 0
+        start = fresh[0:1] - page
+        vec_ref[0:1, :] = jnp.where(on_last, start, -1.0)
+        vec_ref[1:2, :] = jnp.where(on_last, start + 1, -1.0)
+        vec_ref[2:3, :] = jnp.where(is_src + is_dst == 0, 1.0, 0.0)
+        vec_ref[3:8, :] = jnp.zeros((5, lanes), F32)
+
+    m_cols = mf.shape[1] // chips // 2
+
+    def extract():
+        def body(i, _):
+            for w in range(2):
+                for j in range(4):
+                    n = i * 4 + j
+                    mg[w, :, pl.ds(pl.multiple_of(n * kv_cols, kv_cols), kv_cols)] = lax.dot_general(
+                        pick_ref[...], kv_v[w, n], (((1,), (1,)), ((), ())), preferred_element_type=F32).astype(BF16)
+            return 0
+
+        lax.fori_loop(0, page // 4, body, 0)
+        mig_pair().start()
+
+    def mig_pair():
+        return pltpu.make_async_remote_copy(
+            src_ref=mg.at[1 - c], dst_ref=mx, send_sem=gp_send, recv_sem=gp_recv, device_id=peer, device_id_type=MESH)
+
+    def m_at(zz, half):
+        return pl.ds(pl.multiple_of((zz * 2 + half) * m_cols, m_cols), m_cols)
+
+    def ms_copy(way, k, half):
+        sgn = 1 if way == 0 else -1
+        return pltpu.make_async_remote_copy(
+            src_ref=mg.at[c, :, m_at(chip(sgn * k), half)], dst_ref=mr.at[way, k - 1, half],
+            send_sem=gs_send.at[way, k - 1, half], recv_sem=gs_recv.at[way, k - 1, half],
+            device_id=ring_to(way), device_id_type=MESH)
+
+    def mig_start():
+        mig_pair().wait()
+        mg[c] = mg[c] + mx[...]
+        for half in range(2):
+            for way in range(2):
+                ms_copy(way, HOPS if takes(way, HOPS, half) else HOPS - 1, half).start()
+
+    def mig_step(k):
+        for half in range(2):
+            for way in range(2):
+                if takes(way, k, half):
+                    sgn = 1 if way == 0 else -1
+                    ms_copy(way, k, half).wait_recv()
+                    at = m_at(chip(sgn * (k - 1)), half)
+                    mg[c, :, at] = mg[c, :, at] + mr[way, k - 1, half]
+                    if k > 1:
+                        ms_copy(way, k - 1, half).start()
+        if k == 1:
+            for half in range(2):
+                mf[:, m_at(z, half)] = mg[c, :, m_at(z, half)]
+                for way in range(2):
+                    for k2 in range(1, HOPS + 1):
+                        if takes(way, k2, half):
+                            ms_copy(way, k2, half).wait_send()
+
+    def mgat_copy(way, hop, half):
+        sgn = 1 if way == 0 else -1
+        ref = mf.at[:, m_at(chip(-sgn * (hop - 1)), half)]
+        return pltpu.make_async_remote_copy(
+            src_ref=ref, dst_ref=ref, send_sem=gg_send.at[way, hop - 1, half], recv_sem=gg_recv.at[way, hop - 1, half],
+            device_id=ring_to(way), device_id_type=MESH)
+
+    def mgat_hop(hop):
+        for half in range(2):
+            for way in range(2):
+                if hop == 0:
+                    mgat_copy(way, 1, half).start()
+                elif takes(way, hop, half):
+                    mgat_copy(way, hop, half).wait_recv()
+                    if hop < HOPS and takes(way, hop + 1, half):
+                        mgat_copy(way, hop + 1, half).start()
+
+    def mig_out_copies(l):
+        return (
+            pltpu.make_async_remote_copy(
+                src_ref=mf, dst_ref=mig_out.at[l, c], send_sem=go_send, recv_sem=go_recv, device_id=peer, device_id_type=MESH),
+            pltpu.make_async_copy(mf, mig_out.at[l, c], go_sem),
+        )
+
+    def mig_put(l):
+        for way in range(2):
+            for half in range(2):
+                for hop in range(1, HOPS + 1):
+                    if takes(way, hop, half):
+                        mgat_copy(way, hop, half).wait_send()
+        for copy in mig_out_copies(l):
+            copy.start()
+
+    def mig_done(l):
+        for copy in mig_out_copies(l):
+            copy.wait()
+
     for name in ("q", "k", "v", "K", "V", "o", "u"):
         load(name, 0).start()
     h_all[0, own_block(0), :] = x_ref[0]
     ag_start(0)
     h_all[1, own_block(1), :] = x_ref[1]
+    tables()
+    ag_hop(0, 1)
     oa[...] = jnp.zeros_like(oa)
-    ag_hop(0, 1)
     ag_hop(0, 2)
     ag_start(1)
+    load("K", 0).wait()
+    load("V", 0).wait()
+    extract()
     ag_hop(0, 3)
     ag_hop(0, 4)
     ag_finish(0)
@@ -457,12 +603,20 @@
         for name in ("q", "k", "v"):
             load(name, l).wait()
         select(0)
+        mig_start()
         project(0)
         keep_new(0)
         ag_hop(1, 1)
-        for name in ("K", "V"):
-            load(name, l).wait()
-        attend_all(0, {0: lambda: ag_hop(1, 2), 1: lambda: ag_hop(1, 3), 2: lambda: ag_hop(1, 4)})
+        mig_step(4)
+
+        def also(hop, k):
+            def work():
+                ag_hop(1, hop)
+                mig_step(k)
+
+            return work
+
+        attend_all(0, {0: also(2, 3), 1: also(3, 2), 2: also(4, 1)})
         exchange(0).wait()
         scatter(0)
         rs_start(0)
@@ -496,42 +650,66 @@
         rs_step(1, 2, False)
         new_h(0)
         if_more(ag_start, 0)
+
+        @pl.when(more)
+        def _():
+            load("K", l + 1).wait()
+            load("V", l + 1).wait()
+            extract()
+
         rs_step(1, 2, True)
         rs_step(1, 1, False)
         if_more(ag_hop, 0, 1)
         rs_step(1, 1, True)
+        mgat_hop(0)
         rs_finish(1)
         finalize(1)
         out_proj(1)
         if_more(ag_hop, 0, 2)
+        mgat_hop(1)
         mid(1)
         refill("o")
         if_more(ag_hop, 0, 3)
-        up(1, lambda: if_more(ag_hop, 0, 4))
+        mgat_hop(2)
+        up(1, lambda: (if_more(ag_hop, 0, 4), mgat_hop(3)))
         refill("u")
+        mgat_hop(4)
+        mig_put(l)
         down(1)
         refill("q")
         if_more(ag_finish, 0)
         new_h(1)
         if_more(ag_start, 1)
+        mig_done(l)
         return 0
 
     lax.fori_loop(0, layers, layer, 0)
 
 
-def pool_kernel(vec_ref, move_ref, mig_ref, new_ref, k_ref, v_ref, ko_ref, vo_ref, moved):
+def pool_kernel(dst_ref, vec_ref, mig_ref, new_ref, y_ref, k_ref, v_ref, ko_ref, vo_ref, yo_ref, moved, move_ref):
     step, rows, slots = k_ref.shape[1:]
+    entries = dst_ref.shape[0]
     live = slice(0, slots)
     group = moved.shape[1] // rows
-    tab = vec_ref[...].astype(F32)
+    tab = vec_ref[...]
     at0, at1, keep = (tab[i : i + 1, live].astype(BF16) for i in range(3))
     keep = keep > 0
     base = pl.program_id(1) * step
     turns = [(which, g) for which in range(2) for g in range(step // group)]
 
+    @pl.when((pl.program_id(0) == 0) & (pl.program_id(1) == 0))
+    def _():
+        yo_ref[...] = y_ref[...]
+        ids = lax.axis_index("kv") * slots + lax.broadcasted_iota(jnp.int32, (entries, slots), 1)
+        row = lax.broadcasted_iota(jnp.int32, (entries, slots), 0)
+        put = jnp.zeros((entries, slots), F32)
+        for e in range(entries):
+            put = jnp.where(row == e, jnp.where(ids == dst_ref[e], 1.0, 0.0), put)
+        move_ref[...] = put.astype(BF16)
+
     def move(which, g, slot):
         moved[slot] = lax.dot_general(
-            mig_ref[which, :, g * group * rows : (g + 1) * group * rows], move_ref[...], (((0,), (0,)), ((), ())),
+            mig_ref[0, which, :, g * group * rows : (g + 1) * group * rows], move_ref[...], (((0,), (0,)), ((), ())),
             preferred_element_type=F32).astype(BF16)
 
     move(0, 0, 0)
@@ -542,49 +720,33 @@
         for j in range(group):
             i = g * group + j
             pos = jnp.full((1, slots), (base + i).astype(F32), F32).astype(BF16)
-            for r in range(0, rows, 64):
-                cut = slice(r, r + 64)
-                val = jnp.where(keep, pool_ref[0, i, cut], moved[n % 2, j * rows + r : j * rows + r + 64, :])
-                val = jnp.where(at0 == pos, new_ref[0, 0, which, cut, live], val)
-                out_ref[0, i, cut] = jnp.where(at1 == pos, new_ref[0, 1, which, cut, live], val)
-
-
-def new_pools(pools, mig, knew, vec, move):
+            val = jnp.where(keep, pool_ref[0, i], moved[n % 2, j * rows : (j + 1) * rows, :])
+            val = jnp.where(at0 == pos, new_ref[0, 0, which, :, live], val)
+            out_ref[0, i] = jnp.where(at1 == pos, new_ref[0, 1, which, :, live], val)
+
+
+def new_pools(pools, mig, knew, vec, dst, y):
     layers, page, rows, slots = pools[0].shape
-    step = 16
-    entries = mig.shape[1]
+    step = 32
+    entries = mig.shape[2]
     block = pl.BlockSpec((1, step, rows, slots), lambda l, i: (l, i, 0, 0))
+    whole = pl.BlockSpec(y.shape, lambda l, i: (0, 0, 0))
     return pl.pallas_call(
         pool_kernel,
-        out_shape=[jax.ShapeDtypeStruct(pools[0].shape, BF16)] * 2,
+        out_shape=[jax.ShapeDtypeStruct(pools[0].shape, BF16)] * 2 + [jax.ShapeDtypeStruct(y.shape, BF16)],
         grid=(layers, page // step),
         in_specs=[
+            pl.BlockSpec(memory_space=pltpu.SMEM),
             pl.BlockSpec(vec.shape, lambda l, i: (0, 0)),
-            pl.BlockSpec(move.shape, lambda l, i: (0, 0)),
-            pl.BlockSpec((2, entries, step * rows), lambda l, i: (0, 0, l * (page // step) + i)),
+            pl.BlockSpec((1, 2, entries, step * rows), lambda l, i: (l, 0, 0, i)),
             pl.BlockSpec((1, 2, 2, rows, 128), lambda l, i: (l, 0, 0, 0, 0)),
-            block, block,
+            whole, block, block,
         ],
-        out_specs=[block, block],
-        scratch_shapes=[pltpu.VMEM((2, 4 * rows, slots), BF16)],
+        out_specs=[block, block, whole],
+        scratch_shapes=[pltpu.VMEM((2, 4 * rows, slots), BF16), pltpu.VMEM((entries, slots), BF16)],
         compiler_params=pltpu.CompilerParams(dimension_semantics=("arbitrary", "arbitrary"), vmem_limit_bytes=67043328),
         name="new_pools",
-    )(vec, move, mig, knew, *pools)
-
-
-def slot_tables(table, lens, src, dst, dev, slots, page):
-    ids = dev * slots + jnp.arange(slots, dtype=jnp.int32)
-    from_src = ids[:, None] == src[None, :]
-    is_src = jnp.any(from_src, axis=1)
-    is_dst = jnp.any(ids[:, None] == dst[None, :], axis=1)
-    target = jnp.where(is_src, jnp.sum(jnp.where(from_src, dst[None, :], 0), axis=1), ids)
-    hit = [table[None, :, p] == target[:, None] for p in range(2)]
-    live = [h & ~is_dst[:, None] for h in hit]
-    return ids, is_src, is_dst, hit, live
-
-
-def pad_rows(a, rows):
-    return jnp.pad(a, ((0, rows - a.shape[0]), (0, 0)))
+    )(dst, vec, mig, knew, y, *pools)
 
 
 def solution(mesh):
@@ -599,32 +761,8 @@
         ff = w_up.shape[2]
         rep_heads = w_query.shape[2] // head // kv_heads
         total = seqs * devs
-        dev = lax.axis_index("kv")
-        peer = dev + 1 - 2 * lax.rem(dev, 2)
+        entries = mig_src.shape[0]
         pools = [jnp.transpose(p, (1, 2, 3, 4, 0)).reshape(layers, page, kv_heads * head, slots) for p in (k_pool, v_pool)]
-
-        ids, is_src, is_dst, hit, live = slot_tables(new_table, seq_lens, mig_src, mig_dst, dev, slots, page)
-        peer_live = slot_tables(new_table, seq_lens, mig_src, mig_dst, peer, slots, page)[4]
-        onehot = pad_rows((hit[0] | hit[1]).astype(BF16), 128)
-        e_page = [jnp.concatenate([pad_rows(live[p].astype(BF16), 128), pad_rows(peer_live[p].astype(BF16), 128)]) for p in range(2)]
-        e_sum = e_page[0] + e_page[1]
-        pres = pad_rows(jnp.stack([jnp.sum(e.astype(F32), axis=0) for e in e_page]), 8)
-        length = jnp.sum(jnp.where(hit[0] | hit[1], seq_lens[None, :], 0), axis=1)
-        first, last = jnp.any(live[0], axis=1), jnp.any(live[1], axis=1)
-        limit = jnp.where(first, jnp.minimum(length, page), jnp.where(last, length - page, 0))
-        lane_tab = jnp.pad(jnp.stack([limit, last.astype(jnp.int32)]).astype(jnp.int32), ((0, 6), (0, 128 - slots)))
-        on_last = jnp.any(hit[1], axis=1) & ~is_src
-        at = [jnp.where(on_last, length - page + t, -1) for t in range(2)]
-        keep = ~(is_src | is_dst)
-        vec = jnp.pad(jnp.stack(at + [keep.astype(jnp.int32)]).astype(jnp.int32), ((0, 5), (0, 128 - slots)))
-        move = (mig_dst[:, None] == ids[None, :]).astype(BF16)
-        pick = (mig_src[:, None] == ids[None, :]).astype(BF16)
-
-        mig = jnp.stack([
-            lax.dot_general(pick, p.reshape(-1, slots), (((1,), (1,)), ((), ())), preferred_element_type=F32).astype(BF16)
-            for p in pools
-        ])
-        mig = lax.psum(mig, "kv")
 
         dims = (layers, d_model, ff, chips, seqs, slots, kv_heads, head, page, rep_heads)
         own_rows = rep_heads * head
@@ -632,17 +770,30 @@
         kv_cols = kv_heads * head
         big = max(d_model, ff // 2)
         vm, dma = pltpu.VMEM, pltpu.SemaphoreType.DMA
-        any_spec, vmem_spec = pl.BlockSpec(memory_space=pl.ANY), pl.BlockSpec(memory_space=pltpu.VMEM)
+        any_spec, vmem_spec, smem_spec = (pl.BlockSpec(memory_space=m) for m in (pl.ANY, pltpu.VMEM, pltpu.SMEM))
         flops = 2 * layers * 2 * (128 * d_model * (total + heads_all(w_query, kv_cols)) + 64 * d_model * (d_model + ff) * 2)
-        y, knew = pl.pallas_call(
+        y, knew, vec, mig = pl.pallas_call(
             functools.partial(main_kernel, dims),
             out_shape=[
                 jax.ShapeDtypeStruct((2, seqs, d_model), BF16),
                 jax.ShapeDtypeStruct((layers, 2, 2, kv_cols, 128), BF16),
+                jax.ShapeDtypeStruct((8, 128), F32),
+                jax.ShapeDtypeStruct((layers, 2, entries, page * kv_cols), BF16),
             ],
-            in_specs=[vmem_spec] + [any_spec] * 8 + [vmem_spec] * 6,
-            out_specs=[vmem_spec] * 2,
+            in_specs=[smem_spec] * 2 + [vmem_spec] * 3 + [any_spec] * 8,
+            out_specs=[vmem_spec] * 3 + [any_spec],
             scratch_shapes=[
+                vm((128, total), BF16),
+                vm((256, total), BF16),
+                vm((256, total), BF16),
+                vm((256, total), BF16),
+                vm((8, total), F32),
+                vm((8, 128), jnp.int32),
+                vm((entries, slots), BF16),
+                vm((2, entries, page * kv_cols), BF16),
+                vm((entries, page * kv_cols), BF16),
+                vm((2, HOPS, 2, entries, page * kv_cols // chips // 2), BF16),
+                vm((entries, page * kv_cols), BF16),
                 vm((2, total, d_model), BF16),
                 vm((slots, d_model), BF16),
                 vm((big, d_model), BF16),
@@ -672,17 +823,17 @@
                 dma((2,)), dma((2,)),
                 dma((2, 2)), dma((2, 2)),
                 dma((2,)), dma((2,)),
+                dma((2, HOPS, 2)), dma((2, HOPS, 2)), dma((2, HOPS, 2)), dma((2, HOPS, 2)),
+                dma, dma, dma, dma, dma,
                 dma((8,)),
             ],
             compiler_params=pltpu.CompilerParams(collective_id=0, has_side_effects=True, vmem_limit_bytes=67043328),
             cost_estimate=pl.CostEstimate(flops=int(flops), bytes_accessed=int(90e6), transcendentals=0),
             name="decode",
-        )(embeds, w_query, w_key, w_value, w_out, w_up, w_down, *pools, onehot, *e_page, e_sum, pres, lane_tab)
-
-        outs = [
-            jnp.transpose(p.reshape(layers, page, kv_heads, head, slots), (4, 0, 1, 2, 3))
-            for p in new_pools(pools, mig, knew, vec, move)
-        ]
+        )(mig_src, mig_dst, new_table.T, seq_lens[None], embeds, w_query, w_key, w_value, w_out, w_up, w_down, *pools)
+
+        *outs, y = new_pools(pools, mig, knew, vec, mig_dst, y)
+        outs = [jnp.transpose(p.reshape(layers, page, kv_heads, head, slots), (4, 0, 1, 2, 3)) for p in outs]
         return y, outs[0], outs[1]
 
     def heads_all(w_query, kv_cols):

time: 266 us -> 234 us (0.88)
  between operations: 14.2 us -> 0.64 us
  other arithmetic: 8.91 us -> 0 us
  matrix products: 8.2 us -> 0 us
  local copies, waits for them, and re-layouts: 2.92 us -> 0 us
    dot_general x2 -> x0, matrix products: 8.2 us -> none  [device_fn(): lax.dot_general(pick, p.reshape(-1, slots), (((1,), (1,)), ((), ())), pre...]
    another operation x4 -> x0, other arithmetic: 2.82 us -> none  [the longest x1 1.53 us: device_fn(): jnp.stack([lax.dot_general(pick, p.reshape(-1, slots), (((1,), (1,)), (()...]
  transfers between devices with their start and end apart: 1 -> 0, of which waited for: 0 -> 0; matrix products, arithmetic and copies ran while one was open for 3% -> 0% of each run, Pallas kernels for 81% -> 0%
where the time goes in v4:
time: 234 us
  Pallas kernels  233 us (100%)
    pallas_call x1, Pallas kernels, device_fn(): pl.pallas_call(functools.partial(main_kernel, dims), out_shape=[jax.Shape...  217 us
    pallas_call x1, Pallas kernels, new_pools(): pl.pallas_call(pool_kernel, out_shape=[jax.ShapeDtypeStruct(pools[0].shap...  16.3 us

profile of v4, /device:TPU:21, one launch (start us, length us, event | category | flops | bytes accessed | tf_op | source)
XLA Modules:
  0.0 233.7 jit_solution(10098487334550832399)
XLA Ops:
  0.6 216.7 %decode.1 = (bf16[2,32,2048]{2,1,0:T(8,128)(2,1)}, bf16[2,2,2,256,128]{4,3,2,1,0:T(8,128)(2,1)}, f32[8,128]{1,0:T(8,128)}, bf16[2,2,16,16384]{3,2,1,0:T(8,128)(2,1)}) custom-call(s32[16]{0:T(128)} %src_ref.1, s32[16]{0:T(128)} %dst_ref.3, s32[2,512]{1,0:T(2,128)} %bitcast.18, s32[1,512]{1,0:T(1,128)} %bitcast.19, bf16[2,32,2048]{2,1,0:T(8,128)(2,1)} %x_ref.1, ...), custom_call_target="tpu_custom_call" | custom-call | flops 22548578304 | bytes 90000000 | tf_op jit(solution)/shard_map/decode/pallas_call | solution.py:775
  217.4 16.3 %new_pools.1 = (bf16[2,64,256,80]{3,2,1,0:T(8,128)(2,1)}, bf16[2,64,256,80]{3,2,1,0:T(8,128)(2,1)}, bf16[2,32,2048]{2,1,0:T(8,128)(2,1)}) custom-call(s32[16]{0:T(128)} %dst_ref.3, f32[8,128]{1,0:T(8,128)} %get-tuple-element.10.vec_ref, bf16[2,2,16,16384]{3,2,1,0:T(8,128)(2,1)} %get-tuple-element.11.mig_ref, ...), custom_call_target="tpu_custom_call" | custom-call | tf_op jit(solution)/shard_map/new_pools/pallas_call | solution.py:734

commit v5 on v0

v5 whole, which is shorter than its diff:
```python
import functools
from types import SimpleNamespace

import jax
import jax.numpy as jnp
from jax import lax
from jax.experimental import pallas as pl
from jax.experimental.pallas import tpu as pltpu
from jax.sharding import PartitionSpec as P

MESH = pl.DeviceIdType.MESH
F32, BF16, I32 = jnp.float32, jnp.bfloat16, jnp.int32
NEG = -1e30
LANES = 128
SUB = 8
A, B = BOTH = range(2)
PAIR = len(BOTH)
VMEM_BYTES = 67043328
FAR = 4
HOPS = range(1, FAR + 1)


class Names:
    def __getattr__(self, name):
        return name


W = Names()
ORDER = (
    W.AG00s, W.AG01s, W.TAB, W.EXT0, W.AG00h10, W.AG00h11, W.AG01h10, W.AG01h11, W.MS0s, W.AG00h20, W.AG00h21,
    W.AG01h20, W.AG01h21, W.MS0k400, W.MS0k310, W.MS0k301, W.MS0k411, W.AG00h30, W.AG00h31, W.AG01h30, W.AG01h31,
    W.MS0k300, W.MS0k210, W.MS0k201, W.MS0k311, W.AG00h40, W.AG00h41, W.AG01h40, W.SEL00, W.PROJ00, W.AG01h41,
    W.MS0k200, W.MS0k211, W.MS0k110, W.MS0k101, W.ATT000, W.ATT001, W.MS0k100, W.MS0k111, W.MG0s, W.ATT002, W.ATT003,
    W.MG0h10, W.MG0h11, W.SCAT00, W.RS00s, W.SEL01, W.PROJ01, W.MG0h20, W.MG0h21, W.ATT010, W.RS00k400, W.RS00k310,
    W.ATT011, W.RS00k411, W.RS00k301, W.MG0h30, W.MG0h31, W.ATT012, W.RS00k300, W.RS00k210, W.ATT013, W.RS00k311,
    W.RS00k201, W.MG0h41, W.SCAT01, W.RS01s, W.MG0h40, W.RS00k200, W.RS00k110, W.EXT1, W.RS00k211, W.RS00k101,
    W.RS01k400, W.RS01k310, W.MS1s, W.RS01k301, W.RS01k411, W.RS00k100, W.RS00k111, W.FO00, W.RS01k300, W.MS1k400,
    W.RS01k210, W.MS1k301, W.MS1k310, W.MS1k411, W.MID00, W.RS01k201, W.RS01k311, W.UP000, W.UP001, W.DOWN00,
    W.RS01k200, W.RS01k110, W.MS1k300, W.MS1k210, W.MS1k311, W.MS1k201, W.NEWH00, W.AG10s, W.RS01k101, W.RS01k211,
    W.MS1k110, W.MS1k211, W.RS01k100, W.MS1k200, W.MS1k101, W.AG10h10, W.AG10h11, W.RS01k111, W.FO01, W.MS1k111,
    W.MS1k100, W.MG1s, W.MID01, W.AG10h20, W.AG10h21, W.UP010, W.UP011, W.DOWN01, W.MG1h10, W.MG1h11, W.AG10h30,
    W.AG10h31, W.NEWH01, W.AG11s, W.MG1h20, W.MG1h21, W.AG10h40, W.AG10h41, W.AG11h10, W.SEL10, W.AG11h11, W.PROJ10,
    W.MG1h30, W.MG1h31, W.ATT100, W.AG11h20, W.AG11h21, W.ATT101, W.MG1h40, W.MG1h41, W.ATT102, W.AG11h30, W.AG11h31,
    W.ATT103, W.SCAT10, W.RS10s, W.AG11h40, W.AG11h41, W.SEL11, W.PROJ11, W.ATT110, W.RS10k400, W.RS10k310, W.ATT111,
    W.RS10k411, W.RS10k301, W.ATT112, W.RS10k300, W.RS10k210, W.ATT113, W.RS10k311, W.RS10k201, W.SCAT11, W.RS11s,
    W.RS10k200, W.RS10k110, W.RS10k211, W.RS10k101, W.RS11k400, W.RS11k310, W.RS11k301, W.RS11k411, W.RS10k100,
    W.RS10k111, W.FO10, W.RS11k300, W.RS11k210, W.MID10, W.RS11k201, W.RS11k311, W.UP100, W.UP101, W.DOWN10,
    W.RS11k200, W.RS11k110, W.NEWH10, W.RS11k101, W.RS11k211, W.RS11k100, W.RS11k111, W.FO11, W.MID11, W.UP110,
    W.UP111, W.DOWN11, W.NEWH11,
)


def dot(a, b):
    return jnp.dot(a, b, preferred_element_type=F32)


def dot_by(a, b, left, right):
    return lax.dot_general(a, b, (((left,), (right,)), ((), ())), preferred_element_type=F32)


def exact_dot(x, onehot, right=A):
    high = x.astype(BF16)
    rest = x - high.astype(F32)
    mid = rest.astype(BF16)
    low = (rest - mid.astype(F32)).astype(BF16)
    out = dot_by(jnp.concatenate([high, mid, low], axis=A), onehot, B, right).reshape(FAR - 1, x.shape[A], -1)
    return out[A] + out[B] + out[PAIR]


def sums_to_rows(parts):
    axis = parts[A].ndim - PAIR
    sub = lax.broadcasted_iota(I32, parts[A].shape, axis)
    while len(parts) > 1:
        half = len(parts) // PAIR
        high = (sub & half) != 0
        parts = [
            jnp.where(high, a + pltpu.roll(a, half, axis), b + pltpu.roll(b, SUB - half, axis))
            for a, b in zip(parts[half:], parts[:half], strict=True)
        ]
    return parts[A]


def at_block(i, size):
    return pl.ds(pl.multiple_of(i * size, size), size)


def loop(count, body):
    def step(i, carry):
        body(i)
        return carry

    lax.fori_loop(A, count, step, A)


def takes(way, hop, half):
    return hop < FAR or way == half


def taken(hops=HOPS):
    return [(way, hop, half) for half in BOTH for way in BOTH for hop in hops if takes(way, hop, half)]


def mask_rows(ids, values, shape=None):
    out = jnp.zeros(shape or ids.shape, I32)
    for e in range(values.shape[A]):
        out = jnp.where(ids == values[e], 1, out)
    return out


def placed(ids, values, slots):
    entries = values.shape[A]
    row = lax.broadcasted_iota(I32, (entries, slots), A)
    out = jnp.zeros((entries, slots), F32)
    for e in range(entries):
        out = jnp.where(row == e, jnp.where(ids == values[e], 1.0, 0.0), out)
    return out.astype(BF16)


def main_kernel(
    n,
    src_ref, dst_ref, tab_ref, len_ref, x_ref, wq, wk, wv, wo, wu, wd, kp, vp,
    y_ref, knew_ref, vec_ref, mig_out,
    oh_ref, e_ref, es_ref, pres_ref, lane_ref, pick_ref, mg, mx, mr, mf,
    h_all, hsel, wbig, wk_v, wv_v, wo_v, wu_v, kv_v, q_ref, kn_ref, s_ref, oa, ob, a_ref, pd, rd,
    olhs, pf, rf, hm, act, ag_sent, ag_got, dd_sem, rs_sent, rs_got, x_sem, f_sem, m_sem, gs_sent, gs_got, gg_sent, gg_got,
    gp_sem, go_sem, w_sem,
):
    me = lax.axis_index("kv")
    z, c = me // PAIR, lax.rem(me, PAIR)
    group = lax.axis_index("rep")
    peer = (group, z * PAIR + 1 - c)
    live = pl.ds(A, n.slots)
    half_d = n.d_model // PAIR
    heads_half = n.rep_heads // PAIR

    chips = {step: lax.rem(z + step + n.chips, n.chips) for step in range(-FAR, FAR + 1)}
    rings = {step: (group, PAIR * chips[step] + c) for step in (-1, 1)}
    h_rows = {step: (chips[step] * PAIR + c) * n.seqs for step in chips}

    def along(way, steps):
        return steps if way == A else -steps

    def on_ring(way, steps):
        return rings[along(way, steps)]

    def remote_by(src, dst, send, recv, target):
        return pltpu.make_async_remote_copy(
            src_ref=src, dst_ref=dst, send_sem=send, recv_sem=recv, device_id=target, device_id_type=MESH)

    def remote(src, dst, sems, at, target):
        return remote_by(src, dst, sems.at[(A, *at)], sems.at[(B, *at)], target)

    barrier = pltpu.get_barrier_semaphore()
    others = (peer, *rings.values())
    for target in others:
        pl.semaphore_signal(barrier, inc=1, device_id=target, device_id_type=MESH)
    pl.semaphore_wait(barrier, len(others))

    mine_o, mine_f = at_block(c, n.wide), at_block(c, n.ff_half)
    sources = {
        "q": lambda l: (wq.at[l], wbig.at[pl.ds(A, n.d_model), :]), "k": lambda l: (wk.at[l], wk_v), "v": lambda l: (wv.at[l], wv_v),
        "o": lambda l: (wo.at[l, mine_o, :], wo_v), "u": lambda l: (wu.at[l, :, mine_f], wu_v),
        "d": lambda l: (wd.at[l, mine_f, :], wbig.at[pl.ds(A, n.ff_half), :]),
        "K": lambda l: (kp.at[l], kv_v.at[A]), "V": lambda l: (vp.at[l], kv_v.at[B]),
    }
    follows = {"q": ("d", A), "d": ("q", B)} | {name: (name, B) for name in "kvouKV"}
    users = {name: PAIR for name in "qkvoud"} | {name: PAIR + 1 for name in "KV"}
    ready, used = set(), {}

    def load(name, l):
        src, dst = sources[name](l)
        return pltpu.make_async_copy(src, dst, w_sem.at[list(sources).index(name)])

    def need(names, l):
        for name in names:
            if (name, l) not in ready:
                ready.add((name, l))
                load(name, l).wait()

    def release(names, l):
        for name in names:
            used[name, l] = used.get((name, l), A) + 1
            after, more = follows[name]
            if used[name, l] == users[name] and l + more < n.layers:
                load(after, l + more).start()

    def gather(ref_of, sent, got, key):
        def copy(way, hop, half):
            ref = ref_of(along(way, 1 - hop), half)
            return remote_by(ref, ref, sent.at[key], got.at[key, way, hop - 1, half], on_ring(way, 1))

        return copy

    def gather_start(copy):
        for half in BOTH:
            for way in BOTH:
                copy(way, 1, half).start()

    def gather_hop(copy, hop, half, passed_on=None):
        for way in BOTH:
            if takes(way, hop, half):
                copy(way, hop, half).wait_recv()
                if hop < FAR and takes(way, hop + 1, half):
                    copy(way, hop + 1, half).start()
                if passed_on:
                    passed_on(way, hop, half).start()

    def total(src_of, got_of, sent, got, key):
        def copy(way, dist, half):
            return remote_by(
                src_of(along(way, dist), half), got_of(way, dist, half), sent.at[key], got.at[key, way, dist - 1, half],
                on_ring(way, 1))

        return copy

    def total_start(copy):
        for way in BOTH:
            copy(way, FAR, way).start()
        for way in BOTH:
            copy(way, FAR - 1, 1 - way).start()

    def total_hop(copy, add, dist, way, half):
        copy(way, dist, half).wait_recv()
        add(along(way, dist - 1), way, dist, half)
        if dist > 1:
            copy(way, dist - 1, half).start()

    ring_copies = len(taken())

    def all_sent(ref, sem):
        remote_by(ref, ref, sem, sem, peer).wait_send()

    def block(t, step, half):
        return h_all.at[t, pl.ds(pl.multiple_of(h_rows[step], n.seqs), n.seqs), pl.ds(half * half_d, half_d)]

    ag_copies = [gather(lambda step, half, t=t: block(t, step, half), ag_sent, ag_got, t) for t in BOTH]

    def to_peer(t):
        def copy(way, hop, half):
            ref = block(t, along(way, -hop), half)
            return remote(ref, ref, dd_sem, (t,), peer)

        return copy

    def ag_start(l, t):
        gather_start(ag_copies[t])
        for half in BOTH:
            to_peer(t)(A, A, half).start()

    def ag_hop(t, hop, half):
        gather_hop(ag_copies[t], hop, half, to_peer(t))

    def ag_finish(t):
        blocks = ring_copies // PAIR
        from_peer = h_all.at[t, pl.ds(A, (blocks + 1) * n.seqs), :]
        remote(from_peer, from_peer, dd_sem, (t,), peer).wait()
        all_sent(h_all.at[t, pl.ds(A, blocks * n.seqs), :], ag_sent.at[t])

    tops, sums = pl.ds(n.sub, SUB), pl.ds(n.sub + SUB, SUB)
    rs_copies = [
        total(lambda step, half, t=t: pd.at[t, chips[step], half], lambda way, d, half, t=t: rd.at[t, way, d - 1, half], rs_sent, rs_got, t)
        for t in BOTH
    ]

    def merge(t):
        def add(step, way, d, half):
            got, mine = rd.at[t, way, d - 1, half], pd.at[t, chips[step], half]
            m1, m2 = got[tops, :], mine[tops, :]
            m = jnp.maximum(m1, m2)
            a1, a2 = jnp.exp(m1 - m), jnp.exp(m2 - m)
            mine[tops, :] = m
            mine[sums, :] = a1 * got[sums, :] + a2 * mine[sums, :]
            at = pl.ds(A, n.sub)
            by_head = (heads_half, n.head, LANES)
            a1, a2 = (a[half * heads_half : (half + 1) * heads_half][:, None] for a in (a1, a2))
            mine[at, :] = (a1 * got[at, :].reshape(by_head) + a2 * mine[at, :].reshape(by_head)).reshape(n.sub, LANES)

        return add

    def select(l, t):
        ag_finish(t)

        def body(i):
            cols = at_block(i, n.s_cols)
            hsel[:, cols] = dot(oh_ref[live, :], h_all[t, :, cols]).astype(BF16)

        loop(n.d_model // n.s_cols, body)

    def turned(w):
        rows = dot(hsel[...], w).astype(BF16).astype(F32)
        return jnp.concatenate([rows, jnp.zeros((LANES - n.slots, rows.shape[B]), F32)], axis=A).T

    def project(l, t):
        need("qkv", l)
        per = n.d_cols // n.head

        def body(i):
            q_ref[pl.ds(i * per, per)] = turned(wbig[pl.ds(A, n.d_model), at_block(i, n.d_cols)]).reshape(per, n.head, LANES)

        loop(n.kv_heads * n.rep_heads // per, body)
        for i, w in enumerate((wk_v, wv_v)):
            kn_ref[t, i] = turned(w[...])
            knew_ref[l, t, i] = kn_ref[t, i].astype(BF16)
        release("qkv", l)

    def attend(t, kvh):
        rows = at_block(kvh, n.head)
        scale = n.head ** -0.5
        out = oa.at[t, kvh // PAIR, lax.rem(kvh, PAIR)]
        heads = range(n.rep_heads)

        def scores(keys):
            parts = []
            for h in heads:
                prods = q_ref[kvh * n.rep_heads + h, :, live][None] * keys
                acc = prods[:, :SUB]
                for d in range(SUB, n.head, SUB):
                    acc = acc + prods[:, d : d + SUB]
                parts.append(acc)
            return sums_to_rows(parts)

        def qk(i):
            at = pl.ds(i * FAR, FAR)
            s_ref[at, :, live] = scores(kv_v[A, at, rows, :].astype(F32))

        loop(n.page // FAR, qk)
        fresh = range(t + 1)
        news = [scores(kn_ref[i, A, rows, live][None])[A] for i in fresh]
        lim, has_new = lane_ref[pl.ds(A, 1), live], lane_ref[pl.ds(B, 1), live] > 0
        news = [jnp.where(has_new, s * scale, NEG) for s in news]
        valid = lax.broadcasted_iota(I32, (n.page, n.rep_heads, n.slots), A) < lim[None]
        old = jnp.where(valid, s_ref[:, :, live] * scale, NEG)
        m = jnp.max(old, axis=A)
        for s in news:
            m = jnp.maximum(m, s)
        probs = jnp.where(valid, jnp.exp(old - m[None]), 0.0)
        s_ref[:, :, live] = probs
        news = [jnp.where(has_new, jnp.exp(s - m), 0.0) for s in news]
        count = jnp.sum(probs, axis=A)
        for p in news:
            count = count + p
        out[pl.ds(n.own_rows, SUB), live] = m
        out[pl.ds(n.own_rows + SUB, SUB), live] = count
        vals = [kn_ref[i, B, rows, live] for i in fresh]
        for h in heads:
            acc = news[A][h : h + 1] * vals[A]
            for p, v in zip(news[1:], vals[1:], strict=True):
                acc = acc + p[h : h + 1] * v
            out[pl.ds(h * n.head, n.head), live] = acc

        def pv(i):
            vals = [kv_v[B, i * FAR + j, rows, :].astype(F32) for j in range(FAR)]
            ps = [s_ref[i * FAR + j, :, live] for j in range(FAR)]
            for h in heads:
                at = pl.ds(h * n.head, n.head)
                acc = out[at, live]
                for p, v in zip(ps, vals, strict=True):
                    acc = acc + p[h : h + 1] * v
                out[at, live] = acc

        loop(n.page // FAR, pv)

    def exchange(t):
        return remote(oa.at[t, 1 - c], ob.at[t], x_sem, (t,), peer)

    def attend_all(l, t, between):
        mine = n.kv_heads // PAIR
        need("KV", l)

        def body(i):
            attend(t, jnp.where(i < mine, (1 - c) * mine + i, c * mine + i - mine))
            pl.when(i == mine - 1)(lambda: exchange(t).start())
            for at, work in between.items():
                pl.when(i == at)(work)

        loop(n.kv_heads, body)
        release("KV", l)

    low_lanes = lax.broadcasted_iota(I32, (1, LANES), B) < n.pair

    def by_chip(parts, put):
        for zp in range(n.chips // PAIR):
            a, b = (p[:, zp * LANES : (zp + 1) * LANES] for p in parts)
            put(PAIR * zp, jnp.where(low_lanes, a, pltpu.roll(b, n.pair, B)))
            put(PAIR * zp + 1, jnp.where(low_lanes, pltpu.roll(a, n.pair, B), b))

    def scatter(l, t):
        exchange(t).wait()

        def both_cores(hh, at):
            return jnp.concatenate([oa[t, c, hh, at, :], ob[t, hh, at, :]], axis=B)

        top, count = (
            jnp.concatenate([both_cores(hh, pl.ds(n.own_rows + off, SUB)) for hh in BOTH], axis=A) for off in (A, SUB))
        m_page = [jnp.where(pres_ref[pl.ds(p, 1), :] > 0, exact_dot(top, e_ref[p]), NEG) for p in BOTH]
        m_seq = jnp.maximum(*m_page)
        a = jnp.exp(jnp.minimum(top - exact_dot(m_seq, es_ref[...], right=B), 0.0))
        a_ref[A], a_ref[B] = a[:SUB], a[SUB:]
        l_seq = exact_dot(count * a, es_ref[...])
        for dense, at in ((m_seq, tops), (l_seq, sums)):
            def put(zz, v, at=at):
                for half in BOTH:
                    pd[t, zz, half, at, :] = v

            by_chip([dense[:SUB], dense[SUB:]], put)

        def body(i):
            for half in BOTH:
                h = half * heads_half + i
                parts = [
                    exact_dot(both_cores(hh, at_block(h, n.head)) * a_ref[hh, pl.ds(h, 1), :], es_ref[...]) for hh in BOTH]

                def put(zz, v, half=half):
                    pd[t, zz, half, at_block(i, n.head), :] = v

                by_chip(parts, put)

        loop(heads_half, body)

    def f_copy(t, stage):
        return remote(pf.at[t, 1 - c], rf.at[t, stage], f_sem, (t, stage), peer)

    def m_copy(t):
        return remote(hm.at[t, c], hm.at[t, c], m_sem, (t,), peer)

    def product(t, lhs, w):
        def body(i):
            cols = at_block(i, n.d_cols)
            val = dot(lhs(), w(cols))
            pf[t, A, :, cols] = val[: n.seqs]
            pf[t, B, :, cols] = val[n.seqs :]

        loop(n.d_model // n.d_cols, body)

    own = pl.ds(pl.multiple_of(h_rows[A], n.seqs), n.seqs)

    def out_proj(l, t):
        all_sent(pd.at[t, pl.ds(A, ring_copies // PAIR)], rs_sent.at[t])
        for half in BOTH:
            mine = pd.at[t, z, half]
            inv = (1.0 / mine[sums, :])[half * heads_half : (half + 1) * heads_half][:, None]
            flat = (mine[pl.ds(A, n.sub), :].reshape(heads_half, n.head, LANES) * inv).reshape(n.sub, LANES).T.astype(BF16)
            for hh in BOTH:
                olhs[:, pl.ds(hh * n.own_rows + half * n.sub, n.sub)] = flat[hh * n.pair : (hh + 1) * n.pair]
        need("o", l)
        product(t, lambda: olhs[...], lambda cols: wo_v[:, cols])
        release("o", l)
        f_copy(t, A).start()

    def mid(l, t):
        f_copy(t, A).wait()
        hm[t, c] = (h_all[t, own, :].astype(F32) + (pf[t, c] + rf[t, A])).astype(BF16)
        m_copy(t).start()

    def up(l, t, halfway):
        m_copy(t).wait()
        need("u", l)

        def body(i):
            cols = at_block(i, n.u_cols)
            u = dot(hm[t].reshape(n.pair, n.d_model), wu_v[:, cols]).astype(BF16).astype(F32)
            act[t, :, cols] = jax.nn.gelu(u, approximate=True).astype(BF16)
            for at, work in halfway.items():
                pl.when(i == at)(work)

        loop(n.ff_half // n.u_cols, body)
        release("u", l)

    def down(l, t):
        need("d", l)
        product(t, lambda: act[t], lambda cols: wbig[pl.ds(A, n.ff_half), cols])
        release("d", l)
        f_copy(t, B).start()

    def new_h(l, t):
        f_copy(t, B).wait()
        new = (hm[t, c].astype(F32) + (pf[t, c] + rf[t, B])).astype(BF16)
        h_all[t, own, :] = new
        y_ref[t] = new

    def ids_of(dev, axis):
        at = lax.broadcasted_iota(I32, (LANES, 1) if axis == A else (1, LANES), axis)
        return jnp.where(at < n.slots, dev * n.slots + at, -1)

    def tables():
        oa[...] = jnp.zeros_like(oa)
        for g, dev in enumerate((me, z * PAIR + 1 - c)):
            ids = ids_of(dev, A)
            target = ids
            for e in range(n.entries):
                target = jnp.where(ids == src_ref[e], dst_ref[e], target)
            stale = mask_rows(ids, dst_ref)
            hit = [jnp.where(tab_ref[pl.ds(p, 1), :] == target, 1.0, 0.0) for p in BOTH]
            now = [jnp.where(stale == 0, h, 0.0) for h in hit]
            at = pl.ds(g * LANES, LANES)
            for p in BOTH:
                e_ref[p, at, :] = now[p].astype(BF16)
            es_ref[at, :] = (now[A] + now[B]).astype(BF16)
            if g == A:
                oh_ref[...] = (hit[A] + hit[B]).astype(BF16)
                held = [h.astype(BF16) for h in (*now, hit[B])]
        for p in BOTH:
            pres_ref[pl.ds(p, 1), :] = jnp.sum(e_ref[p].astype(F32), axis=A, keepdims=True)
        lens = len_ref[...].astype(F32)
        rows = jnp.concatenate([lens, jnp.ones((SUB - 1, lens.shape[B]), F32)], axis=A).astype(BF16)
        first, last, fresh = (dot_by(rows, h, B, B) for h in held)
        at0, at1 = slice(A, 1), slice(B, PAIR)
        limit = jnp.where(first[at1] > 0, jnp.minimum(first[at0], n.page), jnp.where(last[at1] > 0, last[at0] - n.page, 0.0))
        lane_ref[pl.ds(A, 1), :] = limit.astype(I32)
        lane_ref[pl.ds(B, 1), :] = last[at1].astype(I32)
        ids = ids_of(me, B)
        is_src, is_dst = mask_rows(ids, src_ref), mask_rows(ids, dst_ref)
        pick_ref[...] = placed(ids[:, : n.slots], src_ref, n.slots)
        on_last = jnp.where(is_src == 0, fresh[at1], 0.0) > 0
        start = fresh[at0] - n.page
        vec_ref[...] = jnp.where(is_src + is_dst == 0, 1.0, 0.0) * jnp.ones((SUB, LANES), F32)
        for t in BOTH:
            vec_ref[pl.ds(t, 1), :] = jnp.where(on_last, start + t, -1.0)

    m_cols = mf.shape[B] // n.chips // PAIR

    def mig_pair():
        return remote(mg.at[1 - c], mx, gp_sem, (), peer)

    def m_at(step, half):
        return at_block(chips[step] * PAIR + half, m_cols)

    ms_copies, mg_copies = [], []
    for l in range(n.layers):
        ms_copies.append(total(lambda step, half: mg.at[c, :, m_at(step, half)], lambda way, d, half: mr.at[way, d - 1, half], gs_sent, gs_got, l))
        mg_copies.append(gather(lambda step, half: mf.at[:, m_at(step, half)], gg_sent, gg_got, l))

    def mig_add(step, way, d, half):
        at = m_at(step, half)
        mg[c, :, at] = mg[c, :, at] + mr[way, d - 1, half]

    m_ring = pl.ds(A, ring_copies * m_cols)

    def mig_sent(l):
        all_sent(mg.at[c, :, m_ring], gs_sent.at[l])

    def mig_out_copies(l):
        return remote(mf, mig_out.at[l, c], go_sem, (l,), peer), pltpu.make_async_copy(mf, mig_out.at[l, c], go_sem.at[PAIR, l])

    def extract(l):
        need("KV", l)
        if l > 0:
            mig_sent(l - 1)

        def body(i):
            for w in BOTH:
                for j in range(FAR):
                    r = i * FAR + j
                    mg[w, :, at_block(r, n.kv_cols)] = dot_by(pick_ref[...], kv_v[w, r], B, B).astype(BF16)

        loop(n.page // FAR, body)
        release("KV", l)
        mig_pair().start()

    def mig_start(l):
        if l > 0:
            for copy in mig_out_copies(l - 1):
                copy.wait()
        mig_pair().wait()
        mg[c] = mg[c] + mx[...]
        total_start(ms_copies[l])

    def mig_gather(l):
        for half in BOTH:
            mf[:, m_at(A, half)] = mg[c, :, m_at(A, half)]
        gather_start(mg_copies[l])

    def mig_end(l):
        all_sent(mf.at[:, m_ring], gg_sent.at[l])
        for copy in mig_out_copies(l):
            copy.start()

    steps = {"TAB": tables}
    for l in range(n.layers):
        steps[f"EXT{l}"] = functools.partial(extract, l)
        steps[f"MS{l}s"] = functools.partial(mig_start, l)
        steps[f"MG{l}s"] = functools.partial(mig_gather, l)
        for hop in HOPS:
            for half in BOTH:
                steps[f"MG{l}h{hop}{half}"] = functools.partial(gather_hop, mg_copies[l], hop, half)
                for way in BOTH:
                    steps[f"MS{l}k{hop}{way}{half}"] = functools.partial(total_hop, ms_copies[l], mig_add, hop, way, half)
        for t in BOTH:
            for name, work in (
                ("SEL", select), ("PROJ", project), ("SCAT", scatter), ("FO", out_proj), ("MID", mid), ("DOWN", down), ("NEWH", new_h),
            ):
                steps[f"{name}{l}{t}"] = functools.partial(work, l, t)
            steps[f"AG{l}{t}s"] = functools.partial(ag_start, l, t)
            steps[f"RS{l}{t}s"] = functools.partial(total_start, rs_copies[t])
            for hop in HOPS:
                for half in BOTH:
                    steps[f"AG{l}{t}h{hop}{half}"] = functools.partial(ag_hop, t, hop, half)
                    for way in BOTH:
                        steps[f"RS{l}{t}k{hop}{way}{half}"] = functools.partial(total_hop, rs_copies[t], merge(t), hop, way, half)

    for name in ("q", "k", "v", "K", "V", "o", "u"):
        load(name, A).start()
    for t in BOTH:
        h_all[t, own, :] = x_ref[t]

    todo = list(ORDER)
    on_way = {l: len([name for name in todo if name.startswith(f"MG{l}h")]) for l in range(n.layers)}

    def run(names):
        for name in names:
            steps[name]()
            if name.startswith("MG") and "h" in name:
                l = int(name[PAIR])
                on_way[l] -= 1
                if on_way[l] == 0:
                    mig_end(l)

    loops = {"ATT": (attend_all, n.kv_heads), "UP": (up, n.ff_half // n.u_cols)}
    while todo:
        name = todo.pop(A)
        word = name.rstrip("0123456789")
        if word in loops:
            work, count = loops[word]
            l, t, _ = (int(ch) for ch in name[len(word) :])
            between = {}
            for i in range(count - 1):
                upto = todo.index(f"{word}{l}{t}{i + 1}")
                if upto:
                    between[i] = functools.partial(run, todo[:upto])
                todo = todo[upto + 1 :]
            work(l, t, between)
        else:
            run([name])
    for copy in mig_out_copies(n.layers - 1):
        copy.wait()
    mig_sent(n.layers - 1)


def pool_kernel(dst_ref, vec_ref, mig_ref, new_ref, y_ref, k_ref, v_ref, ko_ref, vo_ref, yo_ref, moved, move_ref):
    step, rows, slots = k_ref.shape[1:]
    live = slice(A, slots)
    group = moved.shape[1] // rows
    tab = vec_ref[...]
    at0, at1, keep = (tab[i : i + 1, live].astype(BF16) for i in range(PAIR + 1))
    keep = keep > 0
    base = pl.program_id(B) * step
    turns = [(which, g) for which in BOTH for g in range(step // group)]

    @pl.when((pl.program_id(A) == 0) & (pl.program_id(B) == 0))
    def _():
        yo_ref[...] = y_ref[...]
        ids = lax.axis_index("kv") * slots + lax.broadcasted_iota(I32, (1, slots), B)
        move_ref[...] = placed(ids, dst_ref, slots)

    def move(which, g, slot):
        moved[slot] = dot_by(mig_ref[A, which, :, g * group * rows : (g + 1) * group * rows], move_ref[...], A, A).astype(BF16)

    move(A, A, A)
    for i, (which, g) in enumerate(turns):
        if i + 1 < len(turns):
            move(*turns[i + 1], (i + 1) % PAIR)
        pool_ref, out_ref = ((k_ref, ko_ref), (v_ref, vo_ref))[which]
        for j in range(group):
            r = g * group + j
            pos = jnp.full((1, slots), (base + r).astype(F32), F32).astype(BF16)
            val = jnp.where(keep, pool_ref[A, r], moved[i % PAIR, j * rows : (j + 1) * rows, :])
            val = jnp.where(at0 == pos, new_ref[A, A, which, :, live], val)
            out_ref[A, r] = jnp.where(at1 == pos, new_ref[A, B, which, :, live], val)


def new_pools(pools, mig, knew, vec, dst, y):
    layers, page, rows, slots = pools[A].shape
    step, group = page // PAIR, FAR
    entries = mig.shape[PAIR]
    block = pl.BlockSpec((1, step, rows, slots), lambda l, i: (l, i, A, A))
    whole = pl.BlockSpec(y.shape, lambda l, i: (A, A, A))
    return pl.pallas_call(
        pool_kernel,
        out_shape=[jax.ShapeDtypeStruct(pools[A].shape, BF16)] * PAIR + [jax.ShapeDtypeStruct(y.shape, BF16)],
        grid=(layers, page // step),
        in_specs=[
            pl.BlockSpec(memory_space=pltpu.SMEM),
            pl.BlockSpec(vec.shape, lambda l, i: (A, A)),
            pl.BlockSpec((1, PAIR, entries, step * rows), lambda l, i: (l, A, A, i)),
            pl.BlockSpec((1, PAIR, PAIR, rows, LANES), lambda l, i: (l, A, A, A, A)),
            whole, block, block,
        ],
        out_specs=[block, block, whole],
        scratch_shapes=[pltpu.VMEM((PAIR, group * rows, slots), BF16), pltpu.VMEM((entries, slots), BF16)],
        compiler_params=pltpu.CompilerParams(dimension_semantics=("arbitrary",) * PAIR, vmem_limit_bytes=VMEM_BYTES),
        name="new_pools",
    )(dst, vec, mig, knew, y, *pools)


def solution(mesh):
    devs = mesh.shape["kv"]
    pool_spec = P(("rep", "kv"))
    tok_spec = P(None, ("rep", "kv"), None)

    def device_fn(embeds, w_query, w_key, w_value, w_out, w_up, w_down, k_pool, v_pool, new_table, seq_lens, mig_src, mig_dst):
        slots, layers, page, kv_heads, head = k_pool.shape
        seqs, d_model = embeds.shape[1:]
        rep_heads = w_query.shape[-1] // head // kv_heads
        own_rows = rep_heads * head
        n = SimpleNamespace(
            layers=layers, d_model=d_model, ff_half=w_up.shape[-1] // PAIR, chips=devs // PAIR, seqs=seqs, pair=PAIR * seqs,
            slots=slots, kv_heads=kv_heads, head=head, page=page, rep_heads=rep_heads, own_rows=own_rows, sub=own_rows // PAIR,
            wide=kv_heads // PAIR * own_rows, kv_cols=kv_heads * head, entries=mig_src.shape[A],
            s_cols=d_model // PAIR, d_cols=d_model // FAR, u_cols=w_up.shape[-1] // FAR)
        total = seqs * devs
        pages = page * n.kv_cols
        pools = [jnp.moveaxis(p, A, -1).reshape(layers, page, n.kv_cols, slots) for p in (k_pool, v_pool)]
        dma, two = pltpu.SemaphoreType.DMA, PAIR
        ring = (two, FAR, two)
        bf = lambda *shape: pltpu.VMEM(shape, BF16)
        f32 = lambda *shape: pltpu.VMEM(shape, F32)
        hbm, vmem, smem = (pl.BlockSpec(memory_space=m) for m in (pl.ANY, pltpu.VMEM, pltpu.SMEM))
        y, knew, vec, mig = pl.pallas_call(
            functools.partial(main_kernel, n),
            out_shape=[
                jax.ShapeDtypeStruct((two, seqs, d_model), BF16),
                jax.ShapeDtypeStruct((layers, two, two, n.kv_cols, LANES), BF16),
                jax.ShapeDtypeStruct((SUB, LANES), F32),
                jax.ShapeDtypeStruct((layers, two, n.entries, pages), BF16),
            ],
            in_specs=[smem] * two + [vmem] * (two + 1) + [hbm] * SUB,
            out_specs=[vmem] * (two + 1) + [hbm],
            scratch_shapes=[
                bf(LANES, total), bf(two, two * LANES, total), bf(two * LANES, total), f32(SUB, total), pltpu.VMEM((SUB, LANES), I32),
                bf(n.entries, slots), bf(two, n.entries, pages), bf(n.entries, pages),
                bf(two, FAR, two, n.entries, pages // devs), bf(n.entries, pages),
                bf(two, total, d_model), bf(slots, d_model), bf(max(d_model, n.ff_half), d_model), bf(d_model, n.kv_cols),
                bf(d_model, n.kv_cols), bf(n.wide, d_model), bf(d_model, n.ff_half), bf(two, page, n.kv_cols, slots),
                f32(kv_heads * rep_heads, head, LANES), f32(two, two, n.kv_cols, LANES), f32(page, rep_heads, LANES),
                f32(two, two, two, own_rows + two * SUB, LANES), f32(two, two, own_rows + two * SUB, LANES),
                f32(two, rep_heads, two * LANES), f32(two, n.chips, two, n.sub + two * SUB, LANES),
                f32(two, two, FAR, two, n.sub + two * SUB, LANES), bf(n.pair, n.wide), f32(two, two, seqs, d_model),
                f32(two, two, seqs, d_model), bf(two, two, seqs, d_model), bf(two, n.pair, n.ff_half),
                dma((two,)), dma((two, *ring)), dma((two, two)), dma((two,)), dma((two, *ring)), dma((two, two)),
                dma((two, two, two)), dma((two, two)), dma((layers,)), dma((layers, *ring)), dma((layers,)), dma((layers, *ring)),
                dma((two,)), dma((two + 1, layers)), dma((SUB,)),
            ],
            compiler_params=pltpu.CompilerParams(collective_id=A, has_side_effects=True, vmem_limit_bytes=VMEM_BYTES),
            name="decode",
        )(mig_src, mig_dst, new_table.T, seq_lens[None], embeds, w_query, w_key, w_value, w_out, w_up, w_down, *pools)
        *outs, y = new_pools(pools, mig, knew, vec, mig_dst, y)
        outs = [jnp.moveaxis(p.reshape(layers, page, kv_heads, head, slots), -1, A) for p in outs]
        return y, *outs

    return jax.shard_map(
        device_fn, mesh=mesh,
        in_specs=(tok_spec, *(P(),) * (SUB - PAIR), pool_spec, pool_spec, P("rep", None), *(P("rep"),) * (FAR - 1)),
        out_specs=(tok_spec, pool_spec, pool_spec), check_vma=False)
```

time: 2050 us -> 228 us (0.11)
  local copies, waits for them, and re-layouts: 959 us -> 0 us
  blocking collectives: 384 us -> 0 us
  other arithmetic: 240 us -> 0 us
  waiting for transfers between devices: 239 us -> 0 us
  Pallas kernels: 0 us -> 228 us
  matrix products: 168 us -> 0 us
  starting transfers between devices: 26.1 us -> 0 us
    scatter x17 -> x0, local copies, waits for them, and re-layouts: 513 us -> none  [the longest x5 234 us: decode_layer(): k_pool.at[local_ids, layer_idx, offsets].set(kv_rows[0], mode='drop')]
    all_gather x4 -> x0, blocking collectives: 384 us -> none  [decode_layer(): lax.all_gather(jnp.stack([new_keys, new_vals]), 'kv', axis=1, tiled=True)]
    pallas_call x0 -> x2, Pallas kernels: none -> 228 us  [the longest x1 211 us: device_fn(): pl.pallas_call(functools.partial(main_kernel, n), out_shape=[jax.ShapeDty...]
    dot_general x32 -> x0, matrix products: 168 us -> none  [the longest x4 39.7 us: decode_layer(): jnp.dot(hidden, w_up[layer_idx], preferred_element_type=jnp.float32)]
    slice x28 -> x0, local copies, waits for them, and re-layouts: 126 us -> none  [the longest x4 36.3 us: decode_layer(): v_pool[:, layer_idx]]
    all_to_all x4 -> x0, waiting for transfers between devices: 124 us -> none  [merge_partials(): received = lax.all_to_all(packed, 'kv', 0, 0, tiled=True)]
    broadcast_in_dim x15 -> x0, local copies, waits for them, and re-layouts: 109 us -> none  [the longest x8 54.5 us: local_partials(): seq_sum[..., None]]
    unnamed x94 -> x0, local copies, waits for them, and re-layouts: 96.2 us -> none
  transfers between devices with their start and end apart: 9 -> 0, of which waited for: 4 -> 0; matrix products, arithmetic and copies ran while one was open for 47% -> 0% of each run, Pallas kernels for 0% -> 0%
where the time goes in v5:
time: 228 us
  Pallas kernels  228 us (100%)
    pallas_call x1, Pallas kernels, device_fn(): pl.pallas_call(functools.partial(main_kernel, n), out_shape=[jax.ShapeDty...  211 us
    pallas_call x1, Pallas kernels, new_pools(): pl.pallas_call(pool_kernel, out_shape=[jax.ShapeDtypeStruct(pools[A].shap...  16.2 us

profile of v5, /device:TPU:21, one launch (start us, length us, event | category | flops | bytes accessed | tf_op | source)
XLA Modules:
  0.0 228.1 jit_solution(15283660615294770779)
XLA Ops:
  0.6 211.3 %decode.1 = (bf16[2,32,2048]{2,1,0:T(8,128)(2,1)}, bf16[2,2,2,256,128]{4,3,2,1,0:T(8,128)(2,1)}, f32[8,128]{1,0:T(8,128)}, bf16[2,2,16,16384]{3,2,1,0:T(8,128)(2,1)}) custom-call(s32[16]{0:T(128)} %src_ref.1, s32[16]{0:T(128)} %dst_ref.3, s32[2,512]{1,0:T(2,128)} %bitcast.18, s32[1,512]{1,0:T(1,128)} %bitcast.19, bf16[2,32,2048]{2,1,0:T(8,128)(2,1)} %x_ref.1, ...), custom_call_target="tpu_custom_call" | custom-call | tf_op jit(solution)/shard_map/decode/pallas_call | solution.py:718
  212.0 16.2 %new_pools.1 = (bf16[2,64,256,80]{3,2,1,0:T(8,128)(2,1)}, bf16[2,64,256,80]{3,2,1,0:T(8,128)(2,1)}, bf16[2,32,2048]{2,1,0:T(8,128)(2,1)}) custom-call(s32[16]{0:T(128)} %dst_ref.3, f32[8,128]{1,0:T(8,128)} %get-tuple-element.10.vec_ref, bf16[2,2,16,16384]{3,2,1,0:T(8,128)(2,1)} %get-tuple-element.11.mig_ref, ...), custom_call_target="tpu_custom_call" | custom-call | tf_op jit(solution)/shard_map/new_pools/pallas_call | solution.py:677

commit v6 on v5

--- a/solution.py
+++ b/solution.py
@@ -27,26 +27,25 @@
 
 W = Names()
 ORDER = (
-    W.AG00s, W.AG01s, W.TAB, W.EXT0, W.AG00h10, W.AG00h11, W.AG01h10, W.AG01h11, W.MS0s, W.AG00h20, W.AG00h21,
-    W.AG01h20, W.AG01h21, W.MS0k400, W.MS0k310, W.MS0k301, W.MS0k411, W.AG00h30, W.AG00h31, W.AG01h30, W.AG01h31,
-    W.MS0k300, W.MS0k210, W.MS0k201, W.MS0k311, W.AG00h40, W.AG00h41, W.AG01h40, W.SEL00, W.PROJ00, W.AG01h41,
-    W.MS0k200, W.MS0k211, W.MS0k110, W.MS0k101, W.ATT000, W.ATT001, W.MS0k100, W.MS0k111, W.MG0s, W.ATT002, W.ATT003,
-    W.MG0h10, W.MG0h11, W.SCAT00, W.RS00s, W.SEL01, W.PROJ01, W.MG0h20, W.MG0h21, W.ATT010, W.RS00k400, W.RS00k310,
-    W.ATT011, W.RS00k411, W.RS00k301, W.MG0h30, W.MG0h31, W.ATT012, W.RS00k300, W.RS00k210, W.ATT013, W.RS00k311,
-    W.RS00k201, W.MG0h41, W.SCAT01, W.RS01s, W.MG0h40, W.RS00k200, W.RS00k110, W.EXT1, W.RS00k211, W.RS00k101,
-    W.RS01k400, W.RS01k310, W.MS1s, W.RS01k301, W.RS01k411, W.RS00k100, W.RS00k111, W.FO00, W.RS01k300, W.MS1k400,
-    W.RS01k210, W.MS1k301, W.MS1k310, W.MS1k411, W.MID00, W.RS01k201, W.RS01k311, W.UP000, W.UP001, W.DOWN00,
-    W.RS01k200, W.RS01k110, W.MS1k300, W.MS1k210, W.MS1k311, W.MS1k201, W.NEWH00, W.AG10s, W.RS01k101, W.RS01k211,
-    W.MS1k110, W.MS1k211, W.RS01k100, W.MS1k200, W.MS1k101, W.AG10h10, W.AG10h11, W.RS01k111, W.FO01, W.MS1k111,
-    W.MS1k100, W.MG1s, W.MID01, W.AG10h20, W.AG10h21, W.UP010, W.UP011, W.DOWN01, W.MG1h10, W.MG1h11, W.AG10h30,
-    W.AG10h31, W.NEWH01, W.AG11s, W.MG1h20, W.MG1h21, W.AG10h40, W.AG10h41, W.AG11h10, W.SEL10, W.AG11h11, W.PROJ10,
-    W.MG1h30, W.MG1h31, W.ATT100, W.AG11h20, W.AG11h21, W.ATT101, W.MG1h40, W.MG1h41, W.ATT102, W.AG11h30, W.AG11h31,
-    W.ATT103, W.SCAT10, W.RS10s, W.AG11h40, W.AG11h41, W.SEL11, W.PROJ11, W.ATT110, W.RS10k400, W.RS10k310, W.ATT111,
-    W.RS10k411, W.RS10k301, W.ATT112, W.RS10k300, W.RS10k210, W.ATT113, W.RS10k311, W.RS10k201, W.SCAT11, W.RS11s,
-    W.RS10k200, W.RS10k110, W.RS10k211, W.RS10k101, W.RS11k400, W.RS11k310, W.RS11k301, W.RS11k411, W.RS10k100,
-    W.RS10k111, W.FO10, W.RS11k300, W.RS11k210, W.MID10, W.RS11k201, W.RS11k311, W.UP100, W.UP101, W.DOWN10,
-    W.RS11k200, W.RS11k110, W.NEWH10, W.RS11k101, W.RS11k211, W.RS11k100, W.RS11k111, W.FO11, W.MID11, W.UP110,
-    W.UP111, W.DOWN11, W.NEWH11,
+    W.AG00s, W.AG01s, W.TAB, W.EXT0, W.AG00h10, W.AG00h11, W.AG01h10, W.AG01h11, W.AG00h20, W.AG00h21, W.AG01h20,
+    W.AG01h21, W.AG00h30, W.AG00h31, W.AG01h30, W.AG01h31, W.AG00h40, W.AG00h41, W.SEL00, W.AG01h40, W.PROJ00,
+    W.AG01h41, W.ATT000, W.MS0s, W.ATT001, W.ATT002, W.MS0k400, W.MS0k411, W.MS0k310, W.MS0k301, W.SCAT00, W.RS00s,
+    W.SEL01, W.MS0k300, W.MS0k311, W.PROJ01, W.MS0k210, W.MS0k201, W.ATT010, W.RS00k400, W.RS00k310, W.ATT011,
+    W.RS00k411, W.RS00k301, W.MS0k200, W.MS0k211, W.ATT012, W.RS00k300, W.RS00k210, W.MS0k110, W.MS0k101, W.SCAT01,
+    W.RS00k311, W.RS00k201, W.RS01s, W.MS0k100, W.MS0k111, W.EXT1, W.RS00k200, W.RS00k110, W.RS00k211, W.RS00k101,
+    W.RS01k310, W.RS01k400, W.RS01k411, W.RS01k301, W.RS00k111, W.RS00k100, W.FO00, W.RS01k210, W.RS01k300, W.MID00,
+    W.UP000, W.UP001, W.RS01k311, W.RS01k201, W.DOWN00, W.RS01k200, W.RS01k110, W.NEWH00, W.AG10s, W.RS01k211,
+    W.RS01k101, W.RS01k100, W.AG10h10, W.AG10h11, W.RS01k111, W.FO01, W.AG10h20, W.MID01, W.AG10h21, W.UP010, W.UP011,
+    W.AG10h30, W.DOWN01, W.AG10h31, W.NEWH01, W.AG11s, W.AG10h40, W.AG10h41, W.MG0s, W.SEL10, W.AG11h10, W.PROJ10,
+    W.AG11h11, W.MG0h10, W.ATT100, W.AG11h20, W.MG0h11, W.ATT101, W.AG11h21, W.MG0h20, W.ATT102, W.AG11h30, W.MG0h21,
+    W.SCAT10, W.RS10s, W.AG11h31, W.MG0h30, W.AG11h40, W.MG0h31, W.RS10k400, W.RS10k310, W.RS10k301, W.RS10k411,
+    W.MG0h40, W.AG11h41, W.MG0h41, W.MS1s, W.SEL11, W.PROJ11, W.RS10k300, W.RS10k210, W.ATT110, W.RS10k311,
+    W.RS10k201, W.MS1k400, W.MS1k310, W.MS1k301, W.ATT111, W.RS10k200, W.RS10k110, W.MS1k411, W.ATT112, W.RS10k211,
+    W.RS10k101, W.MS1k300, W.MS1k210, W.SCAT11, W.RS11s, W.MS1k311, W.MS1k201, W.RS10k100, W.MS1k200, W.RS10k111,
+    W.FO10, W.MS1k110, W.MID10, W.RS11k400, W.RS11k310, W.UP100, W.UP101, W.RS11k411, W.RS11k301, W.MS1k101, W.DOWN10,
+    W.MS1k211, W.MS1k100, W.RS11k210, W.RS11k300, W.NEWH10, W.RS11k311, W.RS11k201, W.MS1k111, W.MG1s, W.RS11k200,
+    W.RS11k110, W.RS11k101, W.RS11k211, W.MG1h10, W.MG1h11, W.RS11k100, W.RS11k111, W.FO11, W.MG1h20, W.MG1h21,
+    W.MID11, W.UP110, W.MG1h30, W.UP111, W.MG1h31, W.DOWN11, W.MG1h40, W.MG1h41, W.NEWH11,
 )
 
 
@@ -121,9 +120,9 @@
     src_ref, dst_ref, tab_ref, len_ref, x_ref, wq, wk, wv, wo, wu, wd, kp, vp,
     y_ref, knew_ref, vec_ref, mig_out,
     oh_ref, e_ref, es_ref, pres_ref, lane_ref, pick_ref, mg, mx, mr, mf,
-    h_all, hsel, wbig, wk_v, wv_v, wo_v, wu_v, kv_v, q_ref, kn_ref, s_ref, oa, ob, a_ref, pd, rd,
+    h_all, hsel, wbig, wk_v, wv_v, wo_v, wu_v, raw, kv_p, q_ref, kn_ref, kn_p, s_ref, oa, ob, a_ref, pd, rd,
     olhs, pf, rf, hm, act, ag_sent, ag_got, dd_sem, rs_sent, rs_got, x_sem, f_sem, m_sem, gs_sent, gs_got, gg_sent, gg_got,
-    gp_sem, go_sem, w_sem,
+    gp_sem, go_sem, p_sem, w_sem,
 ):
     me = lax.axis_index("kv")
     z, c = me // PAIR, lax.rem(me, PAIR)
@@ -161,10 +160,9 @@
         "q": lambda l: (wq.at[l], wbig.at[pl.ds(A, n.d_model), :]), "k": lambda l: (wk.at[l], wk_v), "v": lambda l: (wv.at[l], wv_v),
         "o": lambda l: (wo.at[l, mine_o, :], wo_v), "u": lambda l: (wu.at[l, :, mine_f], wu_v),
         "d": lambda l: (wd.at[l, mine_f, :], wbig.at[pl.ds(A, n.ff_half), :]),
-        "K": lambda l: (kp.at[l], kv_v.at[A]), "V": lambda l: (vp.at[l], kv_v.at[B]),
     }
-    follows = {"q": ("d", A), "d": ("q", B)} | {name: (name, B) for name in "kvouKV"}
-    users = {name: PAIR for name in "qkvoud"} | {name: PAIR + 1 for name in "KV"}
+    follows = {"q": ("d", A), "d": ("q", B)} | {name: (name, B) for name in "kvou"}
+    users = {name: PAIR for name in "qkvoud"}
     ready, used = set(), {}
 
     def load(name, l):
@@ -256,7 +254,8 @@
         remote(from_peer, from_peer, dd_sem, (t,), peer).wait()
         all_sent(h_all.at[t, pl.ds(A, blocks * n.seqs), :], ag_sent.at[t])
 
-    tops, sums = pl.ds(n.sub, SUB), pl.ds(n.sub + SUB, SUB)
+    stats = pl.ds(n.sub, SUB)
+    top_rows = lax.broadcasted_iota(I32, (SUB, LANES), A) < heads_half
     rs_copies = [
         total(lambda step, half, t=t: pd.at[t, chips[step], half], lambda way, d, half, t=t: rd.at[t, way, d - 1, half], rs_sent, rs_got, t)
         for t in BOTH
@@ -265,14 +264,13 @@
     def merge(t):
         def add(step, way, d, half):
             got, mine = rd.at[t, way, d - 1, half], pd.at[t, chips[step], half]
-            m1, m2 = got[tops, :], mine[tops, :]
-            m = jnp.maximum(m1, m2)
-            a1, a2 = jnp.exp(m1 - m), jnp.exp(m2 - m)
-            mine[tops, :] = m
-            mine[sums, :] = a1 * got[sums, :] + a2 * mine[sums, :]
+            s1, s2 = got[stats, :], mine[stats, :]
+            m = jnp.maximum(s1, s2)
+            a1, a2 = jnp.exp(s1 - m), jnp.exp(s2 - m)
+            mine[stats, :] = jnp.where(top_rows, m, pltpu.roll(a1, heads_half, A) * s1 + pltpu.roll(a2, heads_half, A) * s2)
             at = pl.ds(A, n.sub)
             by_head = (heads_half, n.head, LANES)
-            a1, a2 = (a[half * heads_half : (half + 1) * heads_half][:, None] for a in (a1, a2))
+            a1, a2 = (a[:heads_half][:, None] for a in (a1, a2))
             mine[at, :] = (a1 * got[at, :].reshape(by_head) + a2 * mine[at, :].reshape(by_head)).reshape(n.sub, LANES)
 
         return add
@@ -290,29 +288,47 @@
         rows = dot(hsel[...], w).astype(BF16).astype(F32)
         return jnp.concatenate([rows, jnp.zeros((LANES - n.slots, rows.shape[B]), F32)], axis=A).T
 
+    units = (PAIR * (1 - c), PAIR * (1 - c) + 1, PAIR * c)
+    spread_head = PAIR * c + 1
+    first_part = LANES - n.slots
+
+    def packed(u, own, other):
+        rest = (other[..., :first_part], other[..., first_part:], own[..., n.slots :])[u]
+        if rest.shape[-1] < first_part:
+            pad = jnp.zeros((*own.shape[:-1], first_part - rest.shape[-1]), own.dtype)
+            rest = jnp.concatenate([rest, pad], axis=-1) if rest.shape[-1] else pad
+        return jnp.concatenate([own, rest], axis=-1)
+
     def project(l, t):
         need("qkv", l)
-        per = n.d_cols // n.head
-
-        def body(i):
-            q_ref[pl.ds(i * per, per)] = turned(wbig[pl.ds(A, n.d_model), at_block(i, n.d_cols)]).reshape(per, n.head, LANES)
-
-        loop(n.kv_heads * n.rep_heads // per, body)
+
+        def query(kvh):
+            return turned(wbig[pl.ds(A, n.d_model), at_block(kvh, n.own_rows)])
+
+        other = query(spread_head)[:, : n.slots]
+        for u, kvh in enumerate(units):
+            q_ref[u] = packed(u, query(kvh)[:, : n.slots], other)
         for i, w in enumerate((wk_v, wv_v)):
             kn_ref[t, i] = turned(w[...])
             knew_ref[l, t, i] = kn_ref[t, i].astype(BF16)
+            for u, kvh in enumerate(units):
+                own, other = (kn_ref[t, i, at_block(head, n.head), live] for head in (kvh, spread_head))
+                kn_p[t, i, at_block(u, n.head), :] = packed(u, own, other)
         release("qkv", l)
 
-    def attend(t, kvh):
-        rows = at_block(kvh, n.head)
+    def attend(t, u):
+        rows = at_block(u, n.head)
         scale = n.head ** -0.5
-        out = oa.at[t, kvh // PAIR, lax.rem(kvh, PAIR)]
+        out = oa.at[t, jnp.where(u < PAIR, 1 - c, c), jnp.where(u < PAIR, u, A)]
         heads = range(n.rep_heads)
+
+        def pages(w, at):
+            return kv_p[w, at, rows, :].astype(F32)
 
         def scores(keys):
             parts = []
             for h in heads:
-                prods = q_ref[kvh * n.rep_heads + h, :, live][None] * keys
+                prods = q_ref[u, pl.ds(h * n.head, n.head), :][None] * keys
                 acc = prods[:, :SUB]
                 for d in range(SUB, n.head, SUB):
                     acc = acc + prods[:, d : d + SUB]
@@ -321,42 +337,42 @@
 
         def qk(i):
             at = pl.ds(i * FAR, FAR)
-            s_ref[at, :, live] = scores(kv_v[A, at, rows, :].astype(F32))
+            s_ref[at, :, :] = scores(pages(A, at))
 
         loop(n.page // FAR, qk)
         fresh = range(t + 1)
-        news = [scores(kn_ref[i, A, rows, live][None])[A] for i in fresh]
-        lim, has_new = lane_ref[pl.ds(A, 1), live], lane_ref[pl.ds(B, 1), live] > 0
+        news = [scores(kn_p[i, A, rows, :][None])[A] for i in fresh]
+        lim, has_new = lane_ref[pl.ds(PAIR * u, 1), :], lane_ref[pl.ds(PAIR * u + 1, 1), :] > 0
         news = [jnp.where(has_new, s * scale, NEG) for s in news]
-        valid = lax.broadcasted_iota(I32, (n.page, n.rep_heads, n.slots), A) < lim[None]
-        old = jnp.where(valid, s_ref[:, :, live] * scale, NEG)
+        valid = lax.broadcasted_iota(I32, (n.page, n.rep_heads, lim.shape[B]), A) < lim[None]
+        old = jnp.where(valid, s_ref[:, :, :] * scale, NEG)
         m = jnp.max(old, axis=A)
         for s in news:
             m = jnp.maximum(m, s)
         probs = jnp.where(valid, jnp.exp(old - m[None]), 0.0)
-        s_ref[:, :, live] = probs
+        s_ref[:, :, :] = probs
         news = [jnp.where(has_new, jnp.exp(s - m), 0.0) for s in news]
         count = jnp.sum(probs, axis=A)
         for p in news:
             count = count + p
-        out[pl.ds(n.own_rows, SUB), live] = m
-        out[pl.ds(n.own_rows + SUB, SUB), live] = count
-        vals = [kn_ref[i, B, rows, live] for i in fresh]
+        out[pl.ds(n.own_rows, SUB), :] = m
+        out[pl.ds(n.own_rows + SUB, SUB), :] = count
+        vals = [kn_p[i, B, rows, :] for i in fresh]
         for h in heads:
             acc = news[A][h : h + 1] * vals[A]
             for p, v in zip(news[1:], vals[1:], strict=True):
                 acc = acc + p[h : h + 1] * v
-            out[pl.ds(h * n.head, n.head), live] = acc
+            out[pl.ds(h * n.head, n.head), :] = acc
 
         def pv(i):
-            vals = [kv_v[B, i * FAR + j, rows, :].astype(F32) for j in range(FAR)]
-            ps = [s_ref[i * FAR + j, :, live] for j in range(FAR)]
+            vals = [v for v in pages(B, pl.ds(i * FAR, FAR))]
+            ps = [s_ref[i * FAR + j, :, :] for j in range(FAR)]
             for h in heads:
                 at = pl.ds(h * n.head, n.head)
-                acc = out[at, live]
+                acc = out[at, :]
                 for p, v in zip(ps, vals, strict=True):
                     acc = acc + p[h : h + 1] * v
-                out[at, live] = acc
+                out[at, :] = acc
 
         loop(n.page // FAR, pv)
 
@@ -364,17 +380,16 @@
         return remote(oa.at[t, 1 - c], ob.at[t], x_sem, (t,), peer)
 
     def attend_all(l, t, between):
-        mine = n.kv_heads // PAIR
-        need("KV", l)
-
-        def body(i):
-            attend(t, jnp.where(i < mine, (1 - c) * mine + i, c * mine + i - mine))
-            pl.when(i == mine - 1)(lambda: exchange(t).start())
+        def body(u):
+            attend(t, u)
+            pl.when(u == B)(lambda: exchange(t).start())
             for at, work in between.items():
-                pl.when(i == at)(work)
-
-        loop(n.kv_heads, body)
-        release("KV", l)
+                pl.when(u == at)(work)
+
+        loop(len(units), body)
+        lane = lax.broadcasted_iota(I32, (1, LANES), B)
+        near, far = (pltpu.roll(oa[t, 1 - c, v], first_part * (v + 1), B) for v in BOTH)
+        oa[t, c, B] = jnp.where(lane < first_part, near, far)
 
     low_lanes = lax.broadcasted_iota(I32, (1, LANES), B) < n.pair
 
@@ -397,12 +412,13 @@
         a = jnp.exp(jnp.minimum(top - exact_dot(m_seq, es_ref[...], right=B), 0.0))
         a_ref[A], a_ref[B] = a[:SUB], a[SUB:]
         l_seq = exact_dot(count * a, es_ref[...])
-        for dense, at in ((m_seq, tops), (l_seq, sums)):
-            def put(zz, v, at=at):
-                for half in BOTH:
-                    pd[t, zz, half, at, :] = v
-
-            by_chip([dense[:SUB], dense[SUB:]], put)
+        dense = {}
+        for what, v in enumerate((m_seq, l_seq)):
+            by_chip([v[:SUB], v[SUB:]], lambda zz, v, what=what: dense.update({(zz, what): v}))
+        for zz in range(n.chips):
+            m, l = dense[zz, A], dense[zz, B]
+            pd[t, zz, A, stats, :] = jnp.where(top_rows, m, pltpu.roll(l, heads_half, A))
+            pd[t, zz, B, stats, :] = jnp.where(top_rows, pltpu.roll(m, heads_half, A), l)
 
         def body(i):
             for half in BOTH:
@@ -438,7 +454,7 @@
         all_sent(pd.at[t, pl.ds(A, ring_copies // PAIR)], rs_sent.at[t])
         for half in BOTH:
             mine = pd.at[t, z, half]
-            inv = (1.0 / mine[sums, :])[half * heads_half : (half + 1) * heads_half][:, None]
+            inv = (1.0 / mine[stats, :])[heads_half:][:, None]
             flat = (mine[pl.ds(A, n.sub), :].reshape(heads_half, n.head, LANES) * inv).reshape(n.sub, LANES).T.astype(BF16)
             for hh in BOTH:
                 olhs[:, pl.ds(hh * n.own_rows + half * n.sub, n.sub)] = flat[hh * n.pair : (hh + 1) * n.pair]
@@ -506,8 +522,10 @@
         first, last, fresh = (dot_by(rows, h, B, B) for h in held)
         at0, at1 = slice(A, 1), slice(B, PAIR)
         limit = jnp.where(first[at1] > 0, jnp.minimum(first[at0], n.page), jnp.where(last[at1] > 0, last[at0] - n.page, 0.0))
-        lane_ref[pl.ds(A, 1), :] = limit.astype(I32)
-        lane_ref[pl.ds(B, 1), :] = last[at1].astype(I32)
+        for i, row in enumerate((limit, last[at1])):
+            row = row[:, : n.slots]
+            for u in range(len(units)):
+                lane_ref[pl.ds(PAIR * u + i, 1), :] = packed(u, row, row).astype(I32)
         ids = ids_of(me, B)
         is_src, is_dst = mask_rows(ids, src_ref), mask_rows(ids, dst_ref)
         pick_ref[...] = placed(ids[:, : n.slots], src_ref, n.slots)
@@ -542,19 +560,40 @@
     def mig_out_copies(l):
         return remote(mf, mig_out.at[l, c], go_sem, (l,), peer), pltpu.make_async_copy(mf, mig_out.at[l, c], go_sem.at[PAIR, l])
 
+    def page_loads(l, i, slot):
+        at = pl.ds(pl.multiple_of(i * SUB, SUB), SUB)
+        return [pltpu.make_async_copy(pool.at[l, at], raw.at[slot, w], p_sem.at[slot, w]) for w, pool in enumerate((kp, vp))]
+
+    def first_pages(l):
+        for i in range(raw.shape[A]):
+            for copy in page_loads(l, i, i):
+                copy.start()
+
     def extract(l):
-        need("KV", l)
         if l > 0:
             mig_sent(l - 1)
+        chunks, held = n.page // SUB, raw.shape[A]
 
         def body(i):
+            slot = lax.rem(i, held)
+            for copy in page_loads(l, i, slot):
+                copy.wait()
+            at = pl.ds(pl.multiple_of(i * SUB, SUB), SUB)
             for w in BOTH:
-                for j in range(FAR):
-                    r = i * FAR + j
-                    mg[w, :, at_block(r, n.kv_cols)] = dot_by(pick_ref[...], kv_v[w, r], B, B).astype(BF16)
-
-        loop(n.page // FAR, body)
-        release("KV", l)
+                rows = raw[slot, w].reshape(SUB * n.kv_cols, n.slots)
+                mg[w, :, at_block(i, SUB * n.kv_cols)] = dot_by(pick_ref[...], rows, B, B).astype(BF16)
+                other = raw[slot, w, :, at_block(spread_head, n.head), :]
+                for u, kvh in enumerate(units):
+                    kv_p[w, at, at_block(u, n.head), :] = packed(u, raw[slot, w, :, at_block(kvh, n.head), :], other)
+
+            @pl.when(i + held < chunks)
+            def _():
+                for copy in page_loads(l, i + held, slot):
+                    copy.start()
+
+        loop(chunks, body)
+        if l + 1 < n.layers:
+            first_pages(l + 1)
         mig_pair().start()
 
     def mig_start(l):
@@ -566,9 +605,11 @@
         total_start(ms_copies[l])
 
     def mig_gather(l):
+        gather_start(mg_copies[l])
+
+    def mig_own():
         for half in BOTH:
             mf[:, m_at(A, half)] = mg[c, :, m_at(A, half)]
-        gather_start(mg_copies[l])
 
     def mig_end(l):
         all_sent(mf.at[:, m_ring], gg_sent.at[l])
@@ -598,24 +639,25 @@
                     for way in BOTH:
                         steps[f"RS{l}{t}k{hop}{way}{half}"] = functools.partial(total_hop, rs_copies[t], merge(t), hop, way, half)
 
-    for name in ("q", "k", "v", "K", "V", "o", "u"):
+    first_pages(A)
+    for name in ("q", "k", "v", "o", "u"):
         load(name, A).start()
     for t in BOTH:
         h_all[t, own, :] = x_ref[t]
 
     todo = list(ORDER)
-    on_way = {l: len([name for name in todo if name.startswith(f"MG{l}h")]) for l in range(n.layers)}
+    on_way = {kind: len([name for name in todo if name.startswith(kind)]) for l in range(n.layers) for kind in (f"MS{l}k", f"MG{l}h")}
 
     def run(names):
         for name in names:
             steps[name]()
-            if name.startswith("MG") and "h" in name:
-                l = int(name[PAIR])
-                on_way[l] -= 1
-                if on_way[l] == 0:
-                    mig_end(l)
-
-    loops = {"ATT": (attend_all, n.kv_heads), "UP": (up, n.ff_half // n.u_cols)}
+            kind = name[:FAR]
+            if kind in on_way:
+                on_way[kind] -= 1
+                if on_way[kind] == 0:
+                    mig_end(int(kind[PAIR])) if "h" in kind else mig_own()
+
+    loops = {"ATT": (attend_all, len(units)), "UP": (up, n.ff_half // n.u_cols)}
     while todo:
         name = todo.pop(A)
         word = name.rstrip("0123456789")
@@ -730,15 +772,15 @@
                 bf(n.entries, slots), bf(two, n.entries, pages), bf(n.entries, pages),
                 bf(two, FAR, two, n.entries, pages // devs), bf(n.entries, pages),
                 bf(two, total, d_model), bf(slots, d_model), bf(max(d_model, n.ff_half), d_model), bf(d_model, n.kv_cols),
-                bf(d_model, n.kv_cols), bf(n.wide, d_model), bf(d_model, n.ff_half), bf(two, page, n.kv_cols, slots),
-                f32(kv_heads * rep_heads, head, LANES), f32(two, two, n.kv_cols, LANES), f32(page, rep_heads, LANES),
+                bf(d_model, n.kv_cols), bf(n.wide, d_model), bf(d_model, n.ff_half), bf(two + 1, two, SUB, n.kv_cols, slots), bf(two, page, (kv_heads - 1) * head, LANES),
+                f32(kv_heads - 1, own_rows, LANES), f32(two, two, n.kv_cols, LANES), f32(two, two, (kv_heads - 1) * head, LANES), f32(page, rep_heads, LANES),
                 f32(two, two, two, own_rows + two * SUB, LANES), f32(two, two, own_rows + two * SUB, LANES),
-                f32(two, rep_heads, two * LANES), f32(two, n.chips, two, n.sub + two * SUB, LANES),
-                f32(two, two, FAR, two, n.sub + two * SUB, LANES), bf(n.pair, n.wide), f32(two, two, seqs, d_model),
+                f32(two, rep_heads, two * LANES), f32(two, n.chips, two, n.sub + SUB, LANES),
+                f32(two, two, FAR, two, n.sub + SUB, LANES), bf(n.pair, n.wide), f32(two, two, seqs, d_model),
                 f32(two, two, seqs, d_model), bf(two, two, seqs, d_model), bf(two, n.pair, n.ff_half),
                 dma((two,)), dma((two, *ring)), dma((two, two)), dma((two,)), dma((two, *ring)), dma((two, two)),
                 dma((two, two, two)), dma((two, two)), dma((layers,)), dma((layers, *ring)), dma((layers,)), dma((layers, *ring)),
-                dma((two,)), dma((two + 1, layers)), dma((SUB,)),
+                dma((two,)), dma((two + 1, layers)), dma((two + 1, two)), dma((SUB,)),
             ],
             compiler_params=pltpu.CompilerParams(collective_id=A, has_side_effects=True, vmem_limit_bytes=VMEM_BYTES),
             name="decode",

time: 228 us -> 220 us (0.965)
  Pallas kernels: 228 us -> 219 us
    pallas_call x1, Pallas kernels: 211 us -> 203 us  [device_fn(): pl.pallas_call(functools.partial(main_kernel, n), out_shape=[jax.ShapeDty...]
where the time goes in v6:
time: 220 us
  Pallas kernels  219 us (100%)
    pallas_call x1, Pallas kernels, device_fn(): pl.pallas_call(functools.partial(main_kernel, n), out_shape=[jax.ShapeDty...  203 us
    pallas_call x1, Pallas kernels, new_pools(): pl.pallas_call(pool_kernel, out_shape=[jax.ShapeDtypeStruct(pools[A].shap...  16.2 us

profile of v6, /device:TPU:21, one launch (start us, length us, event | category | flops | bytes accessed | tf_op | source)
XLA Modules:
  0.0 219.5 jit_solution(3598466818128821734)
XLA Ops:
  0.6 202.7 %decode.1 = (bf16[2,32,2048]{2,1,0:T(8,128)(2,1)}, bf16[2,2,2,256,128]{4,3,2,1,0:T(8,128)(2,1)}, f32[8,128]{1,0:T(8,128)}, bf16[2,2,16,16384]{3,2,1,0:T(8,128)(2,1)}) custom-call(s32[16]{0:T(128)} %src_ref.1, s32[16]{0:T(128)} %dst_ref.3, s32[2,512]{1,0:T(2,128)} %bitcast.18, s32[1,512]{1,0:T(1,128)} %bitcast.19, bf16[2,32,2048]{2,1,0:T(8,128)(2,1)} %x_ref.1, ...), custom_call_target="tpu_custom_call" | custom-call | tf_op jit(solution)/shard_map/decode/pallas_call | solution.py:760
  203.4 16.2 %new_pools.1 = (bf16[2,64,256,80]{3,2,1,0:T(8,128)(2,1)}, bf16[2,64,256,80]{3,2,1,0:T(8,128)(2,1)}, bf16[2,32,2048]{2,1,0:T(8,128)(2,1)}) custom-call(s32[16]{0:T(128)} %dst_ref.3, f32[8,128]{1,0:T(8,128)} %get-tuple-element.10.vec_ref, bf16[2,2,16,16384]{3,2,1,0:T(8,128)(2,1)} %get-tuple-element.11.mig_ref, ...), custom_call_target="tpu_custom_call" | custom-call | tf_op jit(solution)/shard_map/new_pools/pallas_call | solution.py:719

commit v7 on v6

--- a/solution.py
+++ b/solution.py
@@ -148,12 +148,6 @@
 
     def remote(src, dst, sems, at, target):
         return remote_by(src, dst, sems.at[(A, *at)], sems.at[(B, *at)], target)
-
-    barrier = pltpu.get_barrier_semaphore()
-    others = (peer, *rings.values())
-    for target in others:
-        pl.semaphore_signal(barrier, inc=1, device_id=target, device_id_type=MESH)
-    pl.semaphore_wait(barrier, len(others))
 
     mine_o, mine_f = at_block(c, n.wide), at_block(c, n.ff_half)
     sources = {
@@ -420,18 +414,20 @@
             pd[t, zz, A, stats, :] = jnp.where(top_rows, m, pltpu.roll(l, heads_half, A))
             pd[t, zz, B, stats, :] = jnp.where(top_rows, pltpu.roll(m, heads_half, A), l)
 
-        def body(i):
+        def body(k):
             for half in BOTH:
-                h = half * heads_half + i
-                parts = [
-                    exact_dot(both_cores(hh, at_block(h, n.head)) * a_ref[hh, pl.ds(h, 1), :], es_ref[...]) for hh in BOTH]
-
-                def put(zz, v, half=half):
-                    pd[t, zz, half, at_block(i, n.head), :] = v
-
-                by_chip(parts, put)
-
-        loop(heads_half, body)
+                for j in BOTH:
+                    i = k * PAIR + j
+                    h = half * heads_half + i
+                    parts = [
+                        exact_dot(both_cores(hh, at_block(h, n.head)) * a_ref[hh, pl.ds(h, 1), :], es_ref[...]) for hh in BOTH]
+
+                    def put(zz, v, half=half, i=i):
+                        pd[t, zz, half, at_block(i, n.head), :] = v
+
+                    by_chip(parts, put)
+
+        loop(heads_half // PAIR, body)
 
     def f_copy(t, stage):
         return remote(pf.at[t, 1 - c], rf.at[t, stage], f_sem, (t, stage), peer)
@@ -441,12 +437,12 @@
 
     def product(t, lhs, w):
         def body(i):
-            cols = at_block(i, n.d_cols)
+            cols = at_block(i, n.s_cols)
             val = dot(lhs(), w(cols))
             pf[t, A, :, cols] = val[: n.seqs]
             pf[t, B, :, cols] = val[n.seqs :]
 
-        loop(n.d_model // n.d_cols, body)
+        loop(n.d_model // n.s_cols, body)
 
     own = pl.ds(pl.multiple_of(h_rows[A], n.seqs), n.seqs)
 
@@ -639,13 +635,24 @@
                     for way in BOTH:
                         steps[f"RS{l}{t}k{hop}{way}{half}"] = functools.partial(total_hop, rs_copies[t], merge(t), hop, way, half)
 
-    first_pages(A)
-    for name in ("q", "k", "v", "o", "u"):
-        load(name, A).start()
     for t in BOTH:
         h_all[t, own, :] = x_ref[t]
-
+    first_pages(A)
+    load("q", A).start()
+    barrier = pltpu.get_barrier_semaphore()
+    others = (peer, *rings.values())
+    for target in others:
+        pl.semaphore_signal(barrier, inc=1, device_id=target, device_id_type=MESH)
+    pl.semaphore_wait(barrier, len(others))
+
+    def later_loads():
+        for name in ("k", "v", "o", "u"):
+            load(name, A).start()
+
+
+    steps["LOADS"] = later_loads
     todo = list(ORDER)
+    todo.insert(PAIR, "LOADS")
     on_way = {kind: len([name for name in todo if name.startswith(kind)]) for l in range(n.layers) for kind in (f"MS{l}k", f"MG{l}h")}
 
     def run(names):

time: 220 us -> 216 us (0.982)
  Pallas kernels: 219 us -> 215 us
    pallas_call x1, Pallas kernels: 203 us -> 199 us  [device_fn(): pl.pallas_call(functools.partial(main_kernel, n), out_shape=[jax.ShapeDty...]
where the time goes in v7:
time: 216 us
  Pallas kernels  215 us (100%)
    pallas_call x1, Pallas kernels, device_fn(): pl.pallas_call(functools.partial(main_kernel, n), out_shape=[jax.ShapeDty...  199 us
    pallas_call x1, Pallas kernels, new_pools(): pl.pallas_call(pool_kernel, out_shape=[jax.ShapeDtypeStruct(pools[A].shap...  16.2 us

profile of v7, /device:TPU:21, one launch (start us, length us, event | category | flops | bytes accessed | tf_op | source)
XLA Modules:
  0.0 216.0 jit_solution(4019448399843419300)
XLA Ops:
  0.6 199.2 %decode.1 = (bf16[2,32,2048]{2,1,0:T(8,128)(2,1)}, bf16[2,2,2,256,128]{4,3,2,1,0:T(8,128)(2,1)}, f32[8,128]{1,0:T(8,128)}, bf16[2,2,16,16384]{3,2,1,0:T(8,128)(2,1)}) custom-call(s32[16]{0:T(128)} %src_ref.1, s32[16]{0:T(128)} %dst_ref.3, s32[2,512]{1,0:T(2,128)} %bitcast.18, s32[1,512]{1,0:T(1,128)} %bitcast.19, bf16[2,32,2048]{2,1,0:T(8,128)(2,1)} %x_ref.1, ...), custom_call_target="tpu_custom_call" | custom-call | tf_op jit(solution)/shard_map/decode/pallas_call | solution.py:767
  199.8 16.2 %new_pools.1 = (bf16[2,64,256,80]{3,2,1,0:T(8,128)(2,1)}, bf16[2,64,256,80]{3,2,1,0:T(8,128)(2,1)}, bf16[2,32,2048]{2,1,0:T(8,128)(2,1)}) custom-call(s32[16]{0:T(128)} %dst_ref.3, f32[8,128]{1,0:T(8,128)} %get-tuple-element.10.vec_ref, bf16[2,2,16,16384]{3,2,1,0:T(8,128)(2,1)} %get-tuple-element.11.mig_ref, ...), custom_call_target="tpu_custom_call" | custom-call | tf_op jit(solution)/shard_map/new_pools/pallas_call | solution.py:726

commit v8 on v7

--- a/solution.py
+++ b/solution.py
@@ -27,25 +27,25 @@
 
 W = Names()
 ORDER = (
-    W.AG00s, W.AG01s, W.TAB, W.EXT0, W.AG00h10, W.AG00h11, W.AG01h10, W.AG01h11, W.AG00h20, W.AG00h21, W.AG01h20,
-    W.AG01h21, W.AG00h30, W.AG00h31, W.AG01h30, W.AG01h31, W.AG00h40, W.AG00h41, W.SEL00, W.AG01h40, W.PROJ00,
-    W.AG01h41, W.ATT000, W.MS0s, W.ATT001, W.ATT002, W.MS0k400, W.MS0k411, W.MS0k310, W.MS0k301, W.SCAT00, W.RS00s,
-    W.SEL01, W.MS0k300, W.MS0k311, W.PROJ01, W.MS0k210, W.MS0k201, W.ATT010, W.RS00k400, W.RS00k310, W.ATT011,
-    W.RS00k411, W.RS00k301, W.MS0k200, W.MS0k211, W.ATT012, W.RS00k300, W.RS00k210, W.MS0k110, W.MS0k101, W.SCAT01,
-    W.RS00k311, W.RS00k201, W.RS01s, W.MS0k100, W.MS0k111, W.EXT1, W.RS00k200, W.RS00k110, W.RS00k211, W.RS00k101,
-    W.RS01k310, W.RS01k400, W.RS01k411, W.RS01k301, W.RS00k111, W.RS00k100, W.FO00, W.RS01k210, W.RS01k300, W.MID00,
-    W.UP000, W.UP001, W.RS01k311, W.RS01k201, W.DOWN00, W.RS01k200, W.RS01k110, W.NEWH00, W.AG10s, W.RS01k211,
-    W.RS01k101, W.RS01k100, W.AG10h10, W.AG10h11, W.RS01k111, W.FO01, W.AG10h20, W.MID01, W.AG10h21, W.UP010, W.UP011,
-    W.AG10h30, W.DOWN01, W.AG10h31, W.NEWH01, W.AG11s, W.AG10h40, W.AG10h41, W.MG0s, W.SEL10, W.AG11h10, W.PROJ10,
-    W.AG11h11, W.MG0h10, W.ATT100, W.AG11h20, W.MG0h11, W.ATT101, W.AG11h21, W.MG0h20, W.ATT102, W.AG11h30, W.MG0h21,
-    W.SCAT10, W.RS10s, W.AG11h31, W.MG0h30, W.AG11h40, W.MG0h31, W.RS10k400, W.RS10k310, W.RS10k301, W.RS10k411,
-    W.MG0h40, W.AG11h41, W.MG0h41, W.MS1s, W.SEL11, W.PROJ11, W.RS10k300, W.RS10k210, W.ATT110, W.RS10k311,
-    W.RS10k201, W.MS1k400, W.MS1k310, W.MS1k301, W.ATT111, W.RS10k200, W.RS10k110, W.MS1k411, W.ATT112, W.RS10k211,
-    W.RS10k101, W.MS1k300, W.MS1k210, W.SCAT11, W.RS11s, W.MS1k311, W.MS1k201, W.RS10k100, W.MS1k200, W.RS10k111,
-    W.FO10, W.MS1k110, W.MID10, W.RS11k400, W.RS11k310, W.UP100, W.UP101, W.RS11k411, W.RS11k301, W.MS1k101, W.DOWN10,
-    W.MS1k211, W.MS1k100, W.RS11k210, W.RS11k300, W.NEWH10, W.RS11k311, W.RS11k201, W.MS1k111, W.MG1s, W.RS11k200,
-    W.RS11k110, W.RS11k101, W.RS11k211, W.MG1h10, W.MG1h11, W.RS11k100, W.RS11k111, W.FO11, W.MG1h20, W.MG1h21,
-    W.MID11, W.UP110, W.MG1h30, W.UP111, W.MG1h31, W.DOWN11, W.MG1h40, W.MG1h41, W.NEWH11,
+    W.AG00s, W.AG01s, W.AG00h10, W.AG00h11, W.AG01h10, W.AG01h11, W.TAB, W.AG00h20, W.AG00h21, W.EXT0, W.AG01h21,
+    W.AG00h30, W.AG00h31, W.AG00h40, W.AG01h20, W.AG00h41, W.SEL00, W.MS0s, W.PROJ00, W.ATT000, W.AG01h30, W.MS0k301,
+    W.MS0k400, W.MS0k310, W.AG01h31, W.ATT001, W.ATT002, W.MS0k411, W.MS0k300, W.AG01h40, W.AG01h41, W.MS0k210,
+    W.SCAT00, W.SCAU00, W.SEL01, W.PROJ01, W.MS0k200, W.MS0k311, W.ATT010, W.RS00k400, W.MS0k201, W.RS00k310,
+    W.ATT011, W.RS00k301, W.RS00k411, W.ATT012, W.RS00k300, W.RS00k210, W.MS0k110, W.MS0k101, W.MS0k100, W.SCAT01,
+    W.RS00k311, W.RS00k200, W.MS0k211, W.SCAU01, W.RS00k201, W.RS01k400, W.MS0k111, W.RS00k211, W.EXT1, W.RS01k310,
+    W.RS00k100, W.RS00k110, W.RS01k411, W.RS00k101, W.RS00k111, W.RS01k301, W.FO00, W.MID00, W.MG0s, W.RS01k300,
+    W.RS01k210, W.UP000, W.UP001, W.RS01k201, W.RS01k311, W.DOWN00, W.NEWH00, W.AG10s, W.RS01k200, W.RS01k110,
+    W.RS01k211, W.AG10h10, W.AG10h11, W.RS01k100, W.RS01k101, W.MG0h10, W.RS01k111, W.FO01, W.AG10h20, W.AG10h21,
+    W.MID01, W.UP010, W.MG0h11, W.UP011, W.AG10h30, W.AG10h31, W.MG0h20, W.DOWN01, W.NEWH01, W.AG11s, W.AG10h41,
+    W.AG10h40, W.MG0h21, W.SEL10, W.MG0h30, W.PROJ10, W.AG11h10, W.ATT100, W.AG11h11, W.ATT101, W.AG11h20, W.MG0h31,
+    W.ATT102, W.AG11h21, W.SCAT10, W.AG11h30, W.AG11h31, W.SCAU10, W.RS10k400, W.MG0h41, W.AG11h40, W.MG0h40, W.MS1s,
+    W.AG11h41, W.SEL11, W.RS10k411, W.PROJ11, W.RS10k310, W.RS10k301, W.MS1k411, W.ATT110, W.MS1k400, W.RS10k300,
+    W.RS10k311, W.ATT111, W.RS10k210, W.MS1k311, W.MS1k301, W.RS10k201, W.MS1k310, W.ATT112, W.MS1k300, W.RS10k211,
+    W.RS10k200, W.SCAT11, W.SCAU11, W.MS1k200, W.MS1k210, W.RS10k110, W.RS11k310, W.RS10k100, W.RS11k400, W.RS10k111,
+    W.RS10k101, W.FO10, W.MS1k211, W.MS1k201, W.RS11k301, W.RS11k411, W.RS11k210, W.MID10, W.RS11k300, W.RS11k311,
+    W.RS11k201, W.MS1k101, W.MS1k111, W.MS1k110, W.UP100, W.MS1k100, W.MG1s, W.UP101, W.DOWN10, W.RS11k211,
+    W.RS11k200, W.RS11k110, W.RS11k101, W.MG1h10, W.MG1h11, W.RS11k111, W.RS11k100, W.FO11, W.MG1h20, W.MID11,
+    W.MG1h21, W.UP110, W.MG1h30, W.UP111, W.MG1h31, W.DOWN11, W.MG1h40, W.NEWH11, W.NEWH10, W.MG1h41,
 )
 
 
@@ -393,14 +393,13 @@
             put(PAIR * zp, jnp.where(low_lanes, a, pltpu.roll(b, n.pair, B)))
             put(PAIR * zp + 1, jnp.where(low_lanes, pltpu.roll(a, n.pair, B), b))
 
+    def both_cores(t, hh, at):
+        return jnp.concatenate([oa[t, c, hh, at, :], ob[t, hh, at, :]], axis=B)
+
     def scatter(l, t):
         exchange(t).wait()
-
-        def both_cores(hh, at):
-            return jnp.concatenate([oa[t, c, hh, at, :], ob[t, hh, at, :]], axis=B)
-
         top, count = (
-            jnp.concatenate([both_cores(hh, pl.ds(n.own_rows + off, SUB)) for hh in BOTH], axis=A) for off in (A, SUB))
+            jnp.concatenate([both_cores(t, hh, pl.ds(n.own_rows + off, SUB)) for hh in BOTH], axis=A) for off in (A, SUB))
         m_page = [jnp.where(pres_ref[pl.ds(p, 1), :] > 0, exact_dot(top, e_ref[p]), NEG) for p in BOTH]
         m_seq = jnp.maximum(*m_page)
         a = jnp.exp(jnp.minimum(top - exact_dot(m_seq, es_ref[...], right=B), 0.0))
@@ -414,20 +413,24 @@
             pd[t, zz, A, stats, :] = jnp.where(top_rows, m, pltpu.roll(l, heads_half, A))
             pd[t, zz, B, stats, :] = jnp.where(top_rows, pltpu.roll(m, heads_half, A), l)
 
+        scatter_half(A, l, t)
+
+    def scatter_half(half, l, t):
         def body(k):
-            for half in BOTH:
-                for j in BOTH:
-                    i = k * PAIR + j
-                    h = half * heads_half + i
-                    parts = [
-                        exact_dot(both_cores(hh, at_block(h, n.head)) * a_ref[hh, pl.ds(h, 1), :], es_ref[...]) for hh in BOTH]
-
-                    def put(zz, v, half=half, i=i):
-                        pd[t, zz, half, at_block(i, n.head), :] = v
-
-                    by_chip(parts, put)
-
-        loop(heads_half // PAIR, body)
+            for j in range(heads_half // PAIR):
+                i = k * PAIR + j
+                h = half * heads_half + i
+                parts = [
+                    exact_dot(both_cores(t, hh, at_block(h, n.head)) * a_ref[hh, pl.ds(h, 1), :], es_ref[...]) for hh in BOTH]
+
+                def put(zz, v, i=i):
+                    pd[t, zz, half, at_block(i, n.head), :] = v
+
+                by_chip(parts, put)
+
+        loop(PAIR, body)
+        for way in BOTH:
+            rs_copies[t](way, FAR if way == half else FAR - 1, half).start()
 
     def f_copy(t, stage):
         return remote(pf.at[t, 1 - c], rf.at[t, stage], f_sem, (t, stage), peer)
@@ -624,11 +627,10 @@
                     steps[f"MS{l}k{hop}{way}{half}"] = functools.partial(total_hop, ms_copies[l], mig_add, hop, way, half)
         for t in BOTH:
             for name, work in (
-                ("SEL", select), ("PROJ", project), ("SCAT", scatter), ("FO", out_proj), ("MID", mid), ("DOWN", down), ("NEWH", new_h),
+                ("SEL", select), ("PROJ", project), ("SCAT", scatter), ("SCAU", functools.partial(scatter_half, B)), ("FO", out_proj), ("MID", mid), ("DOWN", down), ("NEWH", new_h),
             ):
                 steps[f"{name}{l}{t}"] = functools.partial(work, l, t)
             steps[f"AG{l}{t}s"] = functools.partial(ag_start, l, t)
-            steps[f"RS{l}{t}s"] = functools.partial(total_start, rs_copies[t])
             for hop in HOPS:
                 for half in BOTH:
                     steps[f"AG{l}{t}h{hop}{half}"] = functools.partial(ag_hop, t, hop, half)

time: 216 us -> 209 us (0.968)
  Pallas kernels: 215 us -> 208 us
    pallas_call x1, Pallas kernels: 199 us -> 191 us  [device_fn(): pl.pallas_call(functools.partial(main_kernel, n), out_shape=[jax.ShapeDty...]
where the time goes in v8:
time: 209 us; the launch traced here: 208 us
  Pallas kernels  208 us (100%)
    pallas_call x1, Pallas kernels, device_fn(): pl.pallas_call(functools.partial(main_kernel, n), out_shape=[jax.ShapeDty...  191 us
    pallas_call x1, Pallas kernels, new_pools(): pl.pallas_call(pool_kernel, out_shape=[jax.ShapeDtypeStruct(pools[A].shap...  16.2 us

profile of v8, /device:TPU:21, one launch (start us, length us, event | category | flops | bytes accessed | tf_op | source)
XLA Modules:
  0.0 208.3 jit_solution(16470698094250479371)
XLA Ops:
  0.6 191.5 %decode.1 = (bf16[2,32,2048]{2,1,0:T(8,128)(2,1)}, bf16[2,2,2,256,128]{4,3,2,1,0:T(8,128)(2,1)}, f32[8,128]{1,0:T(8,128)}, bf16[2,2,16,16384]{3,2,1,0:T(8,128)(2,1)}) custom-call(s32[16]{0:T(128)} %src_ref.1, s32[16]{0:T(128)} %dst_ref.3, s32[2,512]{1,0:T(2,128)} %bitcast.18, s32[1,512]{1,0:T(1,128)} %bitcast.19, bf16[2,32,2048]{2,1,0:T(8,128)(2,1)} %x_ref.1, ...), custom_call_target="tpu_custom_call" | custom-call | tf_op jit(solution)/shard_map/decode/pallas_call | solution.py:769
  192.1 16.2 %new_pools.1 = (bf16[2,64,256,80]{3,2,1,0:T(8,128)(2,1)}, bf16[2,64,256,80]{3,2,1,0:T(8,128)(2,1)}, bf16[2,32,2048]{2,1,0:T(8,128)(2,1)}) custom-call(s32[16]{0:T(128)} %dst_ref.3, f32[8,128]{1,0:T(8,128)} %get-tuple-element.10.vec_ref, bf16[2,2,16,16384]{3,2,1,0:T(8,128)(2,1)} %get-tuple-element.11.mig_ref, ...), custom_call_target="tpu_custom_call" | custom-call | tf_op jit(solution)/shard_map/new_pools/pallas_call | solution.py:728

commit v9 on v8

--- a/solution.py
+++ b/solution.py
@@ -27,25 +27,27 @@
 
 W = Names()
 ORDER = (
-    W.AG00s, W.AG01s, W.AG00h10, W.AG00h11, W.AG01h10, W.AG01h11, W.TAB, W.AG00h20, W.AG00h21, W.EXT0, W.AG01h21,
-    W.AG00h30, W.AG00h31, W.AG00h40, W.AG01h20, W.AG00h41, W.SEL00, W.MS0s, W.PROJ00, W.ATT000, W.AG01h30, W.MS0k301,
-    W.MS0k400, W.MS0k310, W.AG01h31, W.ATT001, W.ATT002, W.MS0k411, W.MS0k300, W.AG01h40, W.AG01h41, W.MS0k210,
-    W.SCAT00, W.SCAU00, W.SEL01, W.PROJ01, W.MS0k200, W.MS0k311, W.ATT010, W.RS00k400, W.MS0k201, W.RS00k310,
-    W.ATT011, W.RS00k301, W.RS00k411, W.ATT012, W.RS00k300, W.RS00k210, W.MS0k110, W.MS0k101, W.MS0k100, W.SCAT01,
-    W.RS00k311, W.RS00k200, W.MS0k211, W.SCAU01, W.RS00k201, W.RS01k400, W.MS0k111, W.RS00k211, W.EXT1, W.RS01k310,
-    W.RS00k100, W.RS00k110, W.RS01k411, W.RS00k101, W.RS00k111, W.RS01k301, W.FO00, W.MID00, W.MG0s, W.RS01k300,
-    W.RS01k210, W.UP000, W.UP001, W.RS01k201, W.RS01k311, W.DOWN00, W.NEWH00, W.AG10s, W.RS01k200, W.RS01k110,
-    W.RS01k211, W.AG10h10, W.AG10h11, W.RS01k100, W.RS01k101, W.MG0h10, W.RS01k111, W.FO01, W.AG10h20, W.AG10h21,
-    W.MID01, W.UP010, W.MG0h11, W.UP011, W.AG10h30, W.AG10h31, W.MG0h20, W.DOWN01, W.NEWH01, W.AG11s, W.AG10h41,
-    W.AG10h40, W.MG0h21, W.SEL10, W.MG0h30, W.PROJ10, W.AG11h10, W.ATT100, W.AG11h11, W.ATT101, W.AG11h20, W.MG0h31,
-    W.ATT102, W.AG11h21, W.SCAT10, W.AG11h30, W.AG11h31, W.SCAU10, W.RS10k400, W.MG0h41, W.AG11h40, W.MG0h40, W.MS1s,
-    W.AG11h41, W.SEL11, W.RS10k411, W.PROJ11, W.RS10k310, W.RS10k301, W.MS1k411, W.ATT110, W.MS1k400, W.RS10k300,
-    W.RS10k311, W.ATT111, W.RS10k210, W.MS1k311, W.MS1k301, W.RS10k201, W.MS1k310, W.ATT112, W.MS1k300, W.RS10k211,
-    W.RS10k200, W.SCAT11, W.SCAU11, W.MS1k200, W.MS1k210, W.RS10k110, W.RS11k310, W.RS10k100, W.RS11k400, W.RS10k111,
-    W.RS10k101, W.FO10, W.MS1k211, W.MS1k201, W.RS11k301, W.RS11k411, W.RS11k210, W.MID10, W.RS11k300, W.RS11k311,
-    W.RS11k201, W.MS1k101, W.MS1k111, W.MS1k110, W.UP100, W.MS1k100, W.MG1s, W.UP101, W.DOWN10, W.RS11k211,
-    W.RS11k200, W.RS11k110, W.RS11k101, W.MG1h10, W.MG1h11, W.RS11k111, W.RS11k100, W.FO11, W.MG1h20, W.MID11,
-    W.MG1h21, W.UP110, W.MG1h30, W.UP111, W.MG1h31, W.DOWN11, W.MG1h40, W.NEWH11, W.NEWH10, W.MG1h41,
+    W.AG00s, W.TAB, W.AG01s, W.AG00h10, W.AG00h11, W.AG01h11, W.AG00h20, W.AG00h21, W.AG01h10, W.EXT0, W.AG00h30,
+    W.AG01h21, W.AG00h31, W.MS0s, W.AG01h20, W.AG01h31, W.AG00h40, W.AG00h41, W.SEL00, W.PROA00, W.MS0k301, W.PROJ00,
+    W.ATT000, W.AG01h30, W.MS0k400, W.MS0k411, W.ATT001, W.ATT002, W.ATT003, W.MS0k311, W.ATT004, W.ATT005, W.MS0k300,
+    W.AG01h41, W.AG01h40, W.MS0k310, W.SCAT00, W.SCAU00, W.SEL01, W.PROA01, W.MS0k200, W.PROJ01, W.ATT010, W.RS00k400,
+    W.RS00k310, W.ATT011, W.RS00k301, W.RS00k411, W.MS0k211, W.ATT012, W.MS0k201, W.ATT013, W.RS00k210, W.MS0k100,
+    W.RS00k300, W.ATT014, W.ATT015, W.RS00k311, W.RS00k201, W.SCAT01, W.RS00k211, W.RS00k101, W.RS00k200, W.SCAU01,
+    W.MS0k210, W.MS0k111, W.RS01k310, W.RS00k100, W.RS00k110, W.RS01k400, W.RS00k111, W.MS0k101, W.FO00, W.RS01k411,
+    W.RS01k301, W.MID00, W.MS0k110, W.MG0s, W.RS01k300, W.RS01k210, W.UP000, W.UP001, W.RS01k311, W.RS01k201,
+    W.DOW000, W.DOW001, W.NEWH00, W.MG0h10, W.AG10s, W.EXT1, W.RS01k200, W.RS01k211, W.MG0h11, W.AG10h10, W.RS01k101,
+    W.RS01k110, W.AG10h11, W.RS01k111, W.RS01k100, W.FO01, W.MG0h21, W.AG10h20, W.MID01, W.AG10h21, W.UP010, W.MG0h20,
+    W.UP011, W.DOW010, W.DOW011, W.AG10h31, W.AG10h30, W.MG0h31, W.MG0h30, W.NEWH01, W.AG11s, W.AG10h41, W.AG10h40,
+    W.SEL10, W.AG11h10, W.PROA10, W.AG11h11, W.MG0h41, W.MG0h40, W.PROJ10, W.ATT100, W.MS1s, W.ATT101, W.AG11h20,
+    W.AG11h21, W.ATT102, W.ATT103, W.MS1k411, W.ATT104, W.AG11h30, W.MS1k400, W.AG11h31, W.ATT105, W.SCAT10,
+    W.MS1k300, W.AG11h40, W.AG11h41, W.SCAU10, W.MS1k301, W.RS10k310, W.MS1k311, W.SEL11, W.PROA11, W.RS10k400,
+    W.MS1k200, W.RS10k411, W.MS1k310, W.PROJ11, W.ATT110, W.RS10k301, W.ATT111, W.ATT112, W.RS10k300, W.RS10k311,
+    W.ATT113, W.RS10k210, W.MS1k211, W.MS1k210, W.RS10k201, W.ATT114, W.MS1k201, W.ATT115, W.RS10k200, W.RS10k211,
+    W.SCAT11, W.MS1k100, W.SCAU11, W.MS1k111, W.MS1k110, W.RS10k111, W.RS11k400, W.RS10k110, W.RS10k101, W.RS10k100,
+    W.MS1k101, W.RS11k411, W.RS11k310, W.MG1s, W.FO10, W.RS11k301, W.MID10, W.RS11k300, W.RS11k311, W.UP100,
+    W.RS11k210, W.UP101, W.RS11k201, W.DOW100, W.MG1h11, W.RS11k200, W.RS11k211, W.DOW101, W.RS11k101, W.NEWH10,
+    W.MG1h10, W.RS11k110, W.MG1h21, W.RS11k111, W.RS11k100, W.FO11, W.MID11, W.MG1h20, W.MG1h31, W.UP110, W.UP111,
+    W.MG1h30, W.MG1h41, W.DOW110, W.DOW111, W.NEWH11, W.MG1h40,
 )
 
 
@@ -293,15 +295,18 @@
             rest = jnp.concatenate([rest, pad], axis=-1) if rest.shape[-1] else pad
         return jnp.concatenate([own, rest], axis=-1)
 
+    def query(kvh):
+        return turned(wbig[pl.ds(A, n.d_model), at_block(kvh, n.own_rows)])[:, : n.slots]
+
+    def project_first(l, t):
+        need("qkv", l)
+        other = query(spread_head)
+        for u in BOTH:
+            q_ref[u] = packed(u, query(units[u]), other)
+
     def project(l, t):
-        need("qkv", l)
-
-        def query(kvh):
-            return turned(wbig[pl.ds(A, n.d_model), at_block(kvh, n.own_rows)])
-
-        other = query(spread_head)[:, : n.slots]
-        for u, kvh in enumerate(units):
-            q_ref[u] = packed(u, query(kvh)[:, : n.slots], other)
+        own = query(units[PAIR])
+        q_ref[PAIR] = packed(PAIR, own, own)
         for i, w in enumerate((wk_v, wv_v)):
             kn_ref[t, i] = turned(w[...])
             knew_ref[l, t, i] = kn_ref[t, i].astype(BF16)
@@ -310,14 +315,18 @@
                 kn_p[t, i, at_block(u, n.head), :] = packed(u, own, other)
         release("qkv", l)
 
+    heads = range(n.rep_heads)
+
+    def outputs(t, u):
+        return oa.at[t, jnp.where(u < PAIR, 1 - c, c), jnp.where(u < PAIR, u, A)]
+
+    def pages(w, at, u):
+        return kv_p[w, at, at_block(u, n.head), :].astype(F32)
+
     def attend(t, u):
         rows = at_block(u, n.head)
         scale = n.head ** -0.5
-        out = oa.at[t, jnp.where(u < PAIR, 1 - c, c), jnp.where(u < PAIR, u, A)]
-        heads = range(n.rep_heads)
-
-        def pages(w, at):
-            return kv_p[w, at, rows, :].astype(F32)
+        out = outputs(t, u)
 
         def scores(keys):
             parts = []
@@ -331,7 +340,7 @@
 
         def qk(i):
             at = pl.ds(i * FAR, FAR)
-            s_ref[at, :, :] = scores(pages(A, at))
+            s_ref[at, :, :] = scores(pages(A, at, u))
 
         loop(n.page // FAR, qk)
         fresh = range(t + 1)
@@ -358,8 +367,11 @@
                 acc = acc + p[h : h + 1] * v
             out[pl.ds(h * n.head, n.head), :] = acc
 
+    def attend_values(t, u):
+        out = outputs(t, u)
+
         def pv(i):
-            vals = [v for v in pages(B, pl.ds(i * FAR, FAR))]
+            vals = [v for v in pages(B, pl.ds(i * FAR, FAR), u)]
             ps = [s_ref[i * FAR + j, :, :] for j in range(FAR)]
             for h in heads:
                 at = pl.ds(h * n.head, n.head)
@@ -376,9 +388,14 @@
     def attend_all(l, t, between):
         def body(u):
             attend(t, u)
+            for at, work in between.items():
+                if at % PAIR == A:
+                    pl.when(u == at // PAIR)(work)
+            attend_values(t, u)
             pl.when(u == B)(lambda: exchange(t).start())
             for at, work in between.items():
-                pl.when(u == at)(work)
+                if at % PAIR == B:
+                    pl.when(u == at // PAIR)(work)
 
         loop(len(units), body)
         lane = lax.broadcasted_iota(I32, (1, LANES), B)
@@ -438,12 +455,14 @@
     def m_copy(t):
         return remote(hm.at[t, c], hm.at[t, c], m_sem, (t,), peer)
 
-    def product(t, lhs, w):
+    def product(t, lhs, w, between):
         def body(i):
             cols = at_block(i, n.s_cols)
             val = dot(lhs(), w(cols))
             pf[t, A, :, cols] = val[: n.seqs]
             pf[t, B, :, cols] = val[n.seqs :]
+            for at, work in between.items():
+                pl.when(i == at)(work)
 
         loop(n.d_model // n.s_cols, body)
 
@@ -458,7 +477,7 @@
             for hh in BOTH:
                 olhs[:, pl.ds(hh * n.own_rows + half * n.sub, n.sub)] = flat[hh * n.pair : (hh + 1) * n.pair]
         need("o", l)
-        product(t, lambda: olhs[...], lambda cols: wo_v[:, cols])
+        product(t, lambda: olhs[...], lambda cols: wo_v[:, cols], {})
         release("o", l)
         f_copy(t, A).start()
 
@@ -481,9 +500,9 @@
         loop(n.ff_half // n.u_cols, body)
         release("u", l)
 
-    def down(l, t):
+    def down(l, t, between):
         need("d", l)
-        product(t, lambda: act[t], lambda cols: wbig[pl.ds(A, n.ff_half), cols])
+        product(t, lambda: act[t], lambda cols: wbig[pl.ds(A, n.ff_half), cols], between)
         release("d", l)
         f_copy(t, B).start()
 
@@ -627,7 +646,7 @@
                     steps[f"MS{l}k{hop}{way}{half}"] = functools.partial(total_hop, ms_copies[l], mig_add, hop, way, half)
         for t in BOTH:
             for name, work in (
-                ("SEL", select), ("PROJ", project), ("SCAT", scatter), ("SCAU", functools.partial(scatter_half, B)), ("FO", out_proj), ("MID", mid), ("DOWN", down), ("NEWH", new_h),
+                ("SEL", select), ("PROA", project_first), ("PROJ", project), ("SCAT", scatter), ("SCAU", functools.partial(scatter_half, B)), ("FO", out_proj), ("MID", mid), ("NEWH", new_h),
             ):
                 steps[f"{name}{l}{t}"] = functools.partial(work, l, t)
             steps[f"AG{l}{t}s"] = functools.partial(ag_start, l, t)
@@ -666,7 +685,7 @@
                 if on_way[kind] == 0:
                     mig_end(int(kind[PAIR])) if "h" in kind else mig_own()
 
-    loops = {"ATT": (attend_all, len(units)), "UP": (up, n.ff_half // n.u_cols)}
+    loops = {"ATT": (attend_all, PAIR * len(units)), "UP": (up, n.ff_half // n.u_cols), "DOW": (down, n.d_model // n.s_cols)}
     while todo:
         name = todo.pop(A)
         word = name.rstrip("0123456789")

time: 209 us -> 204 us (0.976)
  Pallas kernels: 208 us -> 203 us
    pallas_call x1, Pallas kernels: 191 us -> 187 us  [device_fn(): pl.pallas_call(functools.partial(main_kernel, n), out_shape=[jax.ShapeDty...]
where the time goes in v9:
time: 204 us
  Pallas kernels  203 us (100%)
    pallas_call x1, Pallas kernels, device_fn(): pl.pallas_call(functools.partial(main_kernel, n), out_shape=[jax.ShapeDty...  187 us
    pallas_call x1, Pallas kernels, new_pools(): pl.pallas_call(pool_kernel, out_shape=[jax.ShapeDtypeStruct(pools[A].shap...  16.2 us

profile of v9, /device:TPU:21, one launch (start us, length us, event | category | flops | bytes accessed | tf_op | source)
XLA Modules:
  0.0 203.8 jit_solution(6264269864839719473)
XLA Ops:
  0.6 187.0 %decode.1 = (bf16[2,32,2048]{2,1,0:T(8,128)(2,1)}, bf16[2,2,2,256,128]{4,3,2,1,0:T(8,128)(2,1)}, f32[8,128]{1,0:T(8,128)}, bf16[2,2,16,16384]{3,2,1,0:T(8,128)(2,1)}) custom-call(s32[16]{0:T(128)} %src_ref.1, s32[16]{0:T(128)} %dst_ref.3, s32[2,512]{1,0:T(2,128)} %bitcast.18, s32[1,512]{1,0:T(1,128)} %bitcast.19, bf16[2,32,2048]{2,1,0:T(8,128)(2,1)} %x_ref.1, ...), custom_call_target="tpu_custom_call" | custom-call | tf_op jit(solution)/shard_map/decode/pallas_call | solution.py:788
  187.6 16.2 %new_pools.1 = (bf16[2,64,256,80]{3,2,1,0:T(8,128)(2,1)}, bf16[2,64,256,80]{3,2,1,0:T(8,128)(2,1)}, bf16[2,32,2048]{2,1,0:T(8,128)(2,1)}) custom-call(s32[16]{0:T(128)} %dst_ref.3, f32[8,128]{1,0:T(8,128)} %get-tuple-element.10.vec_ref, bf16[2,2,16,16384]{3,2,1,0:T(8,128)(2,1)} %get-tuple-element.11.mig_ref, ...), custom_call_target="tpu_custom_call" | custom-call | tf_op jit(solution)/shard_map/new_pools/pallas_call | solution.py:747

commit v10 on v9

--- a/solution.py
+++ b/solution.py
@@ -27,27 +27,27 @@
 
 W = Names()
 ORDER = (
-    W.AG00s, W.TAB, W.AG01s, W.AG00h10, W.AG00h11, W.AG01h11, W.AG00h20, W.AG00h21, W.AG01h10, W.EXT0, W.AG00h30,
-    W.AG01h21, W.AG00h31, W.MS0s, W.AG01h20, W.AG01h31, W.AG00h40, W.AG00h41, W.SEL00, W.PROA00, W.MS0k301, W.PROJ00,
-    W.ATT000, W.AG01h30, W.MS0k400, W.MS0k411, W.ATT001, W.ATT002, W.ATT003, W.MS0k311, W.ATT004, W.ATT005, W.MS0k300,
-    W.AG01h41, W.AG01h40, W.MS0k310, W.SCAT00, W.SCAU00, W.SEL01, W.PROA01, W.MS0k200, W.PROJ01, W.ATT010, W.RS00k400,
-    W.RS00k310, W.ATT011, W.RS00k301, W.RS00k411, W.MS0k211, W.ATT012, W.MS0k201, W.ATT013, W.RS00k210, W.MS0k100,
-    W.RS00k300, W.ATT014, W.ATT015, W.RS00k311, W.RS00k201, W.SCAT01, W.RS00k211, W.RS00k101, W.RS00k200, W.SCAU01,
-    W.MS0k210, W.MS0k111, W.RS01k310, W.RS00k100, W.RS00k110, W.RS01k400, W.RS00k111, W.MS0k101, W.FO00, W.RS01k411,
-    W.RS01k301, W.MID00, W.MS0k110, W.MG0s, W.RS01k300, W.RS01k210, W.UP000, W.UP001, W.RS01k311, W.RS01k201,
-    W.DOW000, W.DOW001, W.NEWH00, W.MG0h10, W.AG10s, W.EXT1, W.RS01k200, W.RS01k211, W.MG0h11, W.AG10h10, W.RS01k101,
-    W.RS01k110, W.AG10h11, W.RS01k111, W.RS01k100, W.FO01, W.MG0h21, W.AG10h20, W.MID01, W.AG10h21, W.UP010, W.MG0h20,
-    W.UP011, W.DOW010, W.DOW011, W.AG10h31, W.AG10h30, W.MG0h31, W.MG0h30, W.NEWH01, W.AG11s, W.AG10h41, W.AG10h40,
-    W.SEL10, W.AG11h10, W.PROA10, W.AG11h11, W.MG0h41, W.MG0h40, W.PROJ10, W.ATT100, W.MS1s, W.ATT101, W.AG11h20,
-    W.AG11h21, W.ATT102, W.ATT103, W.MS1k411, W.ATT104, W.AG11h30, W.MS1k400, W.AG11h31, W.ATT105, W.SCAT10,
-    W.MS1k300, W.AG11h40, W.AG11h41, W.SCAU10, W.MS1k301, W.RS10k310, W.MS1k311, W.SEL11, W.PROA11, W.RS10k400,
-    W.MS1k200, W.RS10k411, W.MS1k310, W.PROJ11, W.ATT110, W.RS10k301, W.ATT111, W.ATT112, W.RS10k300, W.RS10k311,
-    W.ATT113, W.RS10k210, W.MS1k211, W.MS1k210, W.RS10k201, W.ATT114, W.MS1k201, W.ATT115, W.RS10k200, W.RS10k211,
-    W.SCAT11, W.MS1k100, W.SCAU11, W.MS1k111, W.MS1k110, W.RS10k111, W.RS11k400, W.RS10k110, W.RS10k101, W.RS10k100,
-    W.MS1k101, W.RS11k411, W.RS11k310, W.MG1s, W.FO10, W.RS11k301, W.MID10, W.RS11k300, W.RS11k311, W.UP100,
-    W.RS11k210, W.UP101, W.RS11k201, W.DOW100, W.MG1h11, W.RS11k200, W.RS11k211, W.DOW101, W.RS11k101, W.NEWH10,
-    W.MG1h10, W.RS11k110, W.MG1h21, W.RS11k111, W.RS11k100, W.FO11, W.MID11, W.MG1h20, W.MG1h31, W.UP110, W.UP111,
-    W.MG1h30, W.MG1h41, W.DOW110, W.DOW111, W.NEWH11, W.MG1h40,
+    W.AG00s, W.AG01s, W.TAB, W.AG00h10, W.AG00h11, W.EXT0, W.AG00h20, W.AG00h21, W.AG01h10, W.MS0s, W.AG01h11,
+    W.AG00h30, W.AG00h31, W.AG01h21, W.MS0k301, W.MS0k400, W.MS0k411, W.MS0k310, W.AG01h20, W.AG00h41, W.AG00h40,
+    W.SEL00, W.PROA00, W.PROJ00, W.ATT000, W.MS0k311, W.ATT001, W.ATT002, W.AG01h31, W.AG01h30, W.ATT003, W.MS0k201,
+    W.ATT004, W.MS0k300, W.MS0k210, W.ATT005, W.SCAT00, W.AG01h40, W.AG01h41, W.SCAU00, W.SEL01, W.PROA01, W.PROJ01,
+    W.RS00k310, W.RS00k400, W.ATT010, W.ATT011, W.RS00k411, W.RS00k301, W.MS0k110, W.ATT012, W.MS0k211, W.RS00k210,
+    W.MS0k200, W.RS00k300, W.ATT013, W.ATT014, W.RS00k201, W.RS00k311, W.ATT015, W.SCAT01, W.SCAU01, W.MS0k111,
+    W.RS00k101, W.RS00k200, W.MS0k100, W.RS00k211, W.RS01k310, W.RS01k400, W.RS01k411, W.MS0k101, W.RS01k301, W.MG0s,
+    W.RS00k100, W.RS00k111, W.RS00k110, W.FO00, W.MID00, W.RS01k300, W.RS01k210, W.UP000, W.RS01k311, W.UP001,
+    W.RS01k201, W.DOW000, W.MG0h11, W.DOW001, W.NEWH00, W.AG10s, W.RS01k211, W.RS01k200, W.MG0h10, W.RS01k110, W.EXT1,
+    W.AG10h11, W.AG10h10, W.RS01k101, W.RS01k100, W.MG0h21, W.RS01k111, W.FO01, W.MG0h20, W.AG10h21, W.MID01,
+    W.AG10h20, W.UP010, W.MG0h31, W.UP011, W.AG10h31, W.MG0h30, W.DOW010, W.AG10h30, W.DOW011, W.NEWH01, W.AG11s,
+    W.AG10h41, W.AG10h40, W.SEL10, W.PROA10, W.AG11h10, W.MG0h40, W.PROJ10, W.AG11h11, W.MG0h41, W.MS1s, W.ATT100,
+    W.ATT101, W.AG11h20, W.ATT102, W.AG11h21, W.ATT103, W.ATT104, W.MS1k411, W.AG11h30, W.MS1k301, W.MS1k310,
+    W.MS1k400, W.ATT105, W.AG11h31, W.SCAT10, W.SCAU10, W.AG11h41, W.AG11h40, W.SEL11, W.MS1k311, W.MS1k300, W.PROA11,
+    W.RS10k310, W.RS10k400, W.MS1k210, W.PROJ11, W.MS1k201, W.ATT110, W.RS10k301, W.RS10k411, W.MS1k200, W.ATT111,
+    W.ATT112, W.RS10k300, W.RS10k210, W.ATT113, W.ATT114, W.MS1k211, W.RS10k311, W.RS10k201, W.ATT115, W.SCAT11,
+    W.RS10k200, W.MS1k101, W.SCAU11, W.RS10k110, W.MS1k111, W.RS10k101, W.RS10k211, W.RS11k411, W.RS11k400,
+    W.RS10k100, W.MS1k110, W.RS11k301, W.RS11k310, W.MS1k100, W.RS10k111, W.FO10, W.MG1s, W.RS11k311, W.RS11k300,
+    W.MID10, W.UP100, W.UP101, W.RS11k210, W.RS11k201, W.MG1h11, W.DOW100, W.RS11k200, W.RS11k211, W.MG1h10,
+    W.RS11k110, W.RS11k101, W.RS11k100, W.MG1h21, W.RS11k111, W.FO11, W.MG1h20, W.DOW101, W.MID11, W.UP110, W.MG1h30,
+    W.MG1h31, W.UP111, W.DOW110, W.DOW111, W.NEWH10, W.MG1h41, W.MG1h40, W.NEWH11,
 )
 
 

time: 204 us -> 203 us (level)
  no operation moved by 1% of the time
where the time goes in v10:
time: 203 us
  Pallas kernels  202 us (100%)
    pallas_call x1, Pallas kernels, device_fn(): pl.pallas_call(functools.partial(main_kernel, n), out_shape=[jax.ShapeDty...  186 us
    pallas_call x1, Pallas kernels, new_pools(): pl.pallas_call(pool_kernel, out_shape=[jax.ShapeDtypeStruct(pools[A].shap...  16.2 us

profile of v10, /device:TPU:21, one launch (start us, length us, event | category | flops | bytes accessed | tf_op | source)
XLA Modules:
  0.0 202.5 jit_solution(12303222729520607606)
XLA Ops:
  0.6 185.7 %decode.1 = (bf16[2,32,2048]{2,1,0:T(8,128)(2,1)}, bf16[2,2,2,256,128]{4,3,2,1,0:T(8,128)(2,1)}, f32[8,128]{1,0:T(8,128)}, bf16[2,2,16,16384]{3,2,1,0:T(8,128)(2,1)}) custom-call(s32[16]{0:T(128)} %src_ref.1, s32[16]{0:T(128)} %dst_ref.3, s32[2,512]{1,0:T(2,128)} %bitcast.18, s32[1,512]{1,0:T(1,128)} %bitcast.19, bf16[2,32,2048]{2,1,0:T(8,128)(2,1)} %x_ref.1, ...), custom_call_target="tpu_custom_call" | custom-call | tf_op jit(solution)/shard_map/decode/pallas_call | solution.py:788
  186.3 16.2 %new_pools.1 = (bf16[2,64,256,80]{3,2,1,0:T(8,128)(2,1)}, bf16[2,64,256,80]{3,2,1,0:T(8,128)(2,1)}, bf16[2,32,2048]{2,1,0:T(8,128)(2,1)}) custom-call(s32[16]{0:T(128)} %dst_ref.3, f32[8,128]{1,0:T(8,128)} %get-tuple-element.10.vec_ref, bf16[2,2,16,16384]{3,2,1,0:T(8,128)(2,1)} %get-tuple-element.11.mig_ref, ...), custom_call_target="tpu_custom_call" | custom-call | tf_op jit(solution)/shard_map/new_pools/pallas_call | solution.py:747
